TPU v7x, 128 devices: a whole 4x4x4 slice. The times are simulated.
128 devices in a mesh: row: 8 (over x, core), col: 16 (over y, z).
Axes of the slice: x: 4, y: 4, z: 4, core: 2. Of those that a mesh axis runs over, the one named last changes fastest.
Arguments:
- panel_rows: float32 [8192, 4096], P('row', 'col'), may hold values from -0.75 to 0.75
- owner_slot: int32 [16, 16], replicated, may hold values from -1 to 31, as said below
Outputs:
- packed: float32 [8, 32, 512, 512], P('row', 'col')
Inputs may be any that keep to these rules, and one draw needn't show every extreme that they name: For j <= i, owner_slot[i, j] is the position of tile (i, j) among the 32 positions of group i // 2; tiles of one group have distinct positions; entries above the diagonal are -1. Position p lies on the device of col index p // 2.
All inputs are finite; a program needn't handle non-finite values.
Results may differ from a plain program's by a relative error of at most 0.0003.
Values sent between devices are 32-bit elements; how exact they have to be, the bound alone decides.
No kernel may reach another device: no remote copies, remote signals or barrier semaphores. Data moves between devices by JAX's collectives and lax.ppermute only.
A program may use at most 128 MiB of HBM per device.

v0:
```python
import functools

import jax
import jax.numpy as jnp
from jax import lax
from jax.experimental import pallas as pl
from jax.experimental.pallas import tpu as pltpu
from jax.sharding import Mesh
from jax.sharding import PartitionSpec as P


N = 4
VMEM = pltpu.VMEM
SMEM = pltpu.SMEM
HBM = pltpu.HBM


def move(value, target):
    pairs = []
    for c in range(2):
        for y in range(N):
            for z in range(N):
                core, gather, scatter = target(c, *((y, z) if c else (z, y)))
                to = (gather, scatter) if c else (scatter, gather)
                pairs.append(((c * N + y) * N + z, (core * N + to[0] % N) * N + to[1] % N))
    return lax.ppermute(value, ("c", "y", "z"), pairs)


def along(value, step):
    return move(value, lambda c, g, r: (c, g + step, r))


def across(value, step):
    return move(value, lambda c, g, r: (c, g, r + step))


def along_other(value, step):
    return move(value, lambda c, g, r: (1 - c, g + step, r))


def over(value, axis, step):
    size = lax.axis_size(axis)
    pairs = [(k, (k + step) % size) for k in range(size) if axis == "c" or k + step < size]
    return lax.ppermute(value, axis, pairs)


def specs(space, count):
    return [pl.BlockSpec(memory_space=space)] * count


def cut_kernel(q, at_ref, mine_ref, other_ref, *outs):
    for step in range(N):
        part = lax.rem(at_ref[1] + step, N)
        for group, ref in enumerate((mine_ref, other_ref)):
            for block in range(2):
                start = pl.multiple_of((2 * block + at_ref[0]) * N * q + part * q, q)
                row = (2 * group + block) * q
                outs[step][row : row + q, :] = ref[pl.ds(start, q), :]


def cut(at, mine, other):
    rows, inner = mine.shape
    q = rows // 16
    return pl.pallas_call(
        functools.partial(cut_kernel, q),
        out_shape=[jax.ShapeDtypeStruct((4 * q, inner), mine.dtype)] * N,
        in_specs=specs(SMEM, 1) + specs(VMEM, 2),
        out_specs=specs(VMEM, N),
        cost_estimate=pl.CostEstimate(flops=10**6, bytes_accessed=3 * rows * inner * 4, transcendentals=0),
        name="cut",
    )(at, mine, other)


def product_kernel(q, slabs, first, last, tab_ref, *refs):
    a_refs, refs = refs[: 2 * slabs], refs[2 * slabs :]
    b_refs, refs = refs[:N], refs[N:]
    total_ref, refs = (None, refs) if first else (refs[0], refs[1:])
    outs, refs = refs[: 8 if last else 1], refs[8 if last else 1 :]
    a_in, b_in, a3, b3, acc, in_sems, total_sem, out_sems, *held = refs
    rows, inner = a_refs[0].shape
    half, side = rows // 2, rows // 4
    copies = []
    for s in range(slabs):
        now = [(a_refs[2 * s + group], a_in.at[s, group * rows : (group + 1) * rows, :]) for group in range(2)]
        for d in range(N):
            now.append((b_refs[d].at[s], b_in.at[s, 4 * q * d : 4 * q * (d + 1), :]))
        now = [pltpu.make_async_copy(source, place, in_sems.at[s, k]) for k, (source, place) in enumerate(now)]
        for copy in now:
            copy.start()
        copies.append(now)
        if s == 0 and not first:
            total = pltpu.make_async_copy(total_ref, acc, total_sem.at[0])
            total.start()

    def halves(value):
        high = value.astype(jnp.bfloat16)
        return high, (value - high.astype(jnp.float32)).astype(jnp.bfloat16)

    def write(place, source, index):
        copy = pltpu.make_async_copy(source, place, out_sems.at[index])
        copy.start()
        return copy

    back = []
    for s in range(slabs):
        for copy in copies[s]:
            copy.wait()

        def split(k, carry):
            at = pl.ds(pl.multiple_of(k * half, half), half)
            high, low = halves(a_in[s, at, :])
            a3[at, 0:inner] = high
            a3[at, inner : 2 * inner] = low
            a3[at, 2 * inner :] = high
            return carry

        lax.fori_loop(0, 4, split, 0)
        for m in range(2):
            at = slice(m * half, (m + 1) * half)
            high, low = halves(b_in[s, at, :])
            b3[at, 0:inner] = high
            b3[at, inner : 2 * inner] = high
            b3[at, 2 * inner :] = low
        if s == 0 and not first:
            total.wait()

        def multiply(pair, carry):
            for part in range(2):
                n = 2 * pair + part
                right = a3[pl.ds(pl.multiple_of(n * side, side), side), :]
                for m in range(2):
                    at = slice(m * half, (m + 1) * half)
                    found = lax.dot_general(
                        b3[at, :], right, (((1,), (1,)), ((), ())), preferred_element_type=jnp.float32
                    )
                    acc[n, at, :] = found if first and s == 0 else acc[n, at, :] + found
            return carry

        if s < slabs - 1:
            lax.fori_loop(0, 4, multiply, 0)

    for group in range(2):
        lax.fori_loop(2 * group, 2 * group + 2, multiply, 0)
        if not last:
            part = slice(4 * group, 4 * group + 4)
            back.append(write(outs[0].at[part], acc.at[part], group))
            continue
        for chunk in (2, 1, 3, 0):
            index = 2 * chunk + group

            def place(k, carry):
                code = tab_ref[index * 8 + k]
                safe = jnp.maximum(code, 0)
                start = pl.multiple_of((safe // 2) * q, q)
                for b in range(2):
                    tile = acc[group * 4 + (safe % 2) * 2 + b, pl.ds(start, q), :]
                    held[0][index, k, :, b * side : (b + 1) * side] = jnp.where(code >= 0, tile, 0.0)
                return carry

            lax.fori_loop(0, 8, place, 0)
            back.append(write(outs[index], held[0].at[index], index))
    for copy in back:
        copy.wait()


def product(tab, slabs, slices, total, last):
    rows, inner = slabs[0].shape
    q, half, count = rows // 16, rows // 2, len(slabs) // 2
    first = total is None
    if last:
        out_shape = [jax.ShapeDtypeStruct((8, q, half), jnp.float32)] * 8
    else:
        out_shape = [jax.ShapeDtypeStruct((8, rows, half // 2), jnp.float32)]
    totals = [] if first else [total]
    return pl.pallas_call(
        functools.partial(product_kernel, q, count, first, last),
        out_shape=out_shape,
        in_specs=specs(SMEM, 1) + specs(HBM, 2 * count + N + len(totals)),
        out_specs=specs(HBM, len(out_shape)),
        scratch_shapes=[
            VMEM((count, 2 * rows, inner), jnp.float32),
            VMEM((count, rows, inner), jnp.float32),
            VMEM((2 * rows, 3 * inner), jnp.bfloat16),
            VMEM((rows, 3 * inner), jnp.bfloat16),
            VMEM((8, rows, half // 2), jnp.float32),
            pltpu.SemaphoreType.DMA((count, 6)),
            pltpu.SemaphoreType.DMA((1,)),
            pltpu.SemaphoreType.DMA((8,)),
        ]
        + ([VMEM((8, 8, q, half), jnp.float32)] if last else []),
        compiler_params=pltpu.CompilerParams(vmem_limit_bytes=40 * 1024 * 1024),
        cost_estimate=pl.CostEstimate(
            flops=4 * rows * rows * 3 * inner * count, bytes_accessed=12 * rows * inner * 4, transcendentals=0
        ),
    )(tab, *slabs, *slices, *totals)


def join_kernel(q, at_ref, *refs):
    pieces, out_ref, held = refs[:8], refs[8], refs[9]
    for index in range(8):
        kind = at_ref[0] if index < N else 1 - at_ref[0]
        mine = at_ref[1] if index < N else at_ref[2]
        part = lax.rem(mine + N - index % N, N)
        start = pl.multiple_of((kind * N + part) * q, q)
        for slot in range(2):
            held[slot, pl.ds(start, q), :] = pieces[index][slot]
    for slot in range(2):
        out_ref[0, slot] = held[slot].T


def join(at, pieces):
    _, q, half = pieces[0].shape
    return pl.pallas_call(
        functools.partial(join_kernel, q),
        out_shape=jax.ShapeDtypeStruct((1, 2, half, half), jnp.float32),
        in_specs=specs(SMEM, 1) + specs(VMEM, 8),
        out_specs=pl.BlockSpec(memory_space=VMEM),
        scratch_shapes=[VMEM((2, half, half), jnp.float32)],
        compiler_params=pltpu.CompilerParams(vmem_limit_bytes=32 * 1024 * 1024),
        cost_estimate=pl.CostEstimate(flops=10**6, bytes_accessed=16 * half * half, transcendentals=0),
        name="join",
    )(at, *pieces)


def tile_codes(owner, x, c, gather, scatter):
    blocks = owner.shape[0]
    i = lax.broadcasted_iota(jnp.int32, (blocks, blocks), 0)
    j = lax.broadcasted_iota(jnp.int32, (blocks, blocks), 1)
    group = j // 2
    array = ((x - group // 2 + N) % N) * 2 + jnp.where(group % 2 == c, 0, 1)
    code = jnp.where(j <= i, (array * 2 + j % 2) * 2 + i % 2 + 1, 0)
    index = jnp.arange(64, dtype=jnp.int32)
    far = (scatter + index // 16) % N
    mine = (index // 8) % 2
    near = (gather + (index // 2) % 4) % N
    wanted = jnp.where(c == 0, far * N + near, near * N + far) * 2 + index % 2
    wanted_group = 2 * x + jnp.where(mine == 0, c, 1 - c)
    hit = (owner[None] == wanted[:, None, None]) & ((i // 2)[None] == wanted_group[:, None, None])
    return jnp.sum(jnp.where(hit, code[None], 0), axis=(1, 2)) - 1


def update(panel, owner):
    x, c, y, z = (lax.axis_index(name) for name in "xcyz")
    gather, scatter = jnp.where(c == 0, z, y), jnp.where(c == 0, y, z)
    at = jnp.stack([c, gather, scatter]).astype(jnp.int32)
    tab = tile_codes(owner, x, c, gather, scatter)

    other = over(panel, "c", 1)
    first, *sends = cut(at, panel, other)
    small = [along(sends[s - 1], s) for s in range(1, N)]
    slices = []
    for piece in (first[None], jnp.stack([small[0], small[2]]), small[1][None]):
        slices.append([piece] + [over(piece, "x", d) for d in range(1, N)])

    up = [along(panel, 1), along(other, 1)]
    down = [along(panel, -1), along(other, -1)]
    beyond = [along(up[0], 1), along(down[1], -1)]

    (total,) = product(tab, [panel, other], slices[0], None, False)
    (total,) = product(tab, up + down, slices[1], total, False)
    own0, own1, near0, near1, far0, far1, last0, last1 = product(tab, beyond, slices[2], total, True)

    up_far, down_far = across(far0, 1), across(far1, -1)
    up_near, down_near = across(near1, 1), across(last0, -1)
    up_sum = across(near0 + up_far, 1)
    down_sum = across(last1 + down_far, -1)
    found, passed = [], []
    for s in range(N):
        part = slice(2 * s, 2 * s + 2)
        mine = own0[part] + up_sum[part] + down_near[part]
        theirs = own1[part] + down_sum[part] + up_near[part]
        found.append(mine if s == 0 else along(mine, s))
        passed.append(along_other(theirs, s))
    return join(at, found + passed)


def solution(mesh):
    grid = Mesh(mesh.devices.reshape(N, 2, N, N), ("x", "c", "y", "z"))
    return jax.shard_map(
        update,
        mesh=grid,
        in_specs=(P(("x", "c"), ("y", "z")), P()),
        out_specs=P(("x", "c"), ("y", "z"), None, None),
        check_vma=False,
    )
```

profile of v0, /device:TPU:1, one launch (start us, length us, event | category | flops | bytes accessed | tf_op | source)
XLA Modules:
  0.0 162.6 jit_solution(13955124680372777032)
XLA Ops:
  0.0 1.4 collective-permute-start.2
  1.4 1.4 collective-permute-start
  2.8 1.4 collective-permute-start.10
  4.2 0.6 pad_add_fusion.at_ref
  4.8 0.0 collective-permute-done.2.other_ref.refs_1_
  4.8 1.0 copy-done.1
  5.8 2.6 %cut.1 = (f32[256,256]{1,0:T(8,128)}, f32[256,256]{1,0:T(8,128)}, f32[256,256]{1,0:T(8,128)}, f32[256,256]{1,0:T(8,128)}) custom-call(s32[3]{0:T(128)} %pad_add_fusion.at_ref, f32[1024,256]{1,0:T(8,128)} %refs_0_.1, f32[1024,256]{1,0:T(8,128)} %copy-done.1), custom_call_target="tpu_custom_call" | custom-call | flops 1000000 | bytes 3145728 | tf_op jit(solution)/shard_map/cut/pallas_call | solution.py:64
  8.4 0.5 collective-permute-start.11
  8.9 2.2 %collective-permute-start.12 = (f32[256,256]{1,0:T(8,128)}, f32[256,256]{1,0:T(8,128)S(1)}, u32[]{:S(2)}, u32[]{:S(2)}) collective-permute-start(f32[256,256]{1,0:T(8,128)} %get-tuple-element.19), channel_id=1, source_target_pairs={{0,3},{1,0},{2,1},{3,2},{4,7},{5,4},{6,5},{7,6},{8,11},{9,8},{10,9... | collective-permute-start | bytes 786440 | tf_op jit(solution)/shard_map/ppermute | solution.py:26
  11.1 0.7 collective-permute-start.3
  11.8 7.9 %collective-permute-done.11 = f32[256,256]{1,0:T(8,128)S(1)} collective-permute-done((f32[256,256]{1,0:T(8,128)}, f32[256,256]{1,0:T(8,128)S(1)}, u32[]{:S(2)}, u32[]{:S(2)}) %collective-permute-start.11) | collective-permute-done | bytes 262176 | tf_op jit(solution)/shard_map/ppermute | solution.py:26
  19.7 3.1 %collective-permute-start.16 = (f32[1,256,256]{2,1,0:T(8,128)}, f32[1,256,256]{2,1,0:T(8,128)S(1)}, u32[]{:S(2)}, u32[]{:S(2)}) collective-permute-start(f32[1,256,256]{2,1,0:T(8,128)} %bitcast.7), channel_id=1, source_target_pairs={{0,32},{32,64},{64,96},{1,33},{33,65},{65,97},{2,34},{34,66},{66,9... | collective-permute-start | bytes 786440 | tf_op jit(solution)/shard_map/ppermute | solution.py:44
  22.9 0.0 collective-permute-done.12
  22.9 5.1 %collective-permute-start.17 = (f32[1,256,256]{2,1,0:T(8,128)}, f32[1,256,256]{2,1,0:T(8,128)}, u32[]{:S(2)}, u32[]{:S(2)}) collective-permute-start(f32[1,256,256]{2,1,0:T(8,128)} %bitcast.8), channel_id=1, source_target_pairs={{0,64},{32,96},{1,65},{33,97},{2,66},{34,98},{3,67},{35,99},{4,68}... | collective-permute-start | bytes 786440 | tf_op jit(solution)/shard_map/ppermute | solution.py:44
  28.0 0.0 collective-permute-done.refs_0_
  28.0 0.1 collective-permute-start.9
  28.1 1.3 collective-permute-start.13
  29.5 0.7 copy-done.5
  30.2 3.8 %collective-permute-start.18 = (f32[1,256,256]{2,1,0:T(8,128)}, f32[1,256,256]{2,1,0:T(8,128)}, u32[]{:S(2)}, u32[]{:S(2)}) collective-permute-start(f32[1,256,256]{2,1,0:T(8,128)} %bitcast.9), channel_id=1, source_target_pairs={{0,96},{1,97},{2,98},{3,99},{4,100},{5,101},{6,102},{7,103},{8,104... | collective-permute-start | bytes 786440 | tf_op jit(solution)/shard_map/ppermute | solution.py:44
  34.0 0.0 collective-permute-done.17.refs_4_
  34.0 1.2 collective-permute-start.5
  35.2 0.1 broadcast_select_fusion
  35.4 0.9 select_reduce_fusion
  36.2 0.7 collective-permute-done.18.refs_5_
  36.9 9.1 %collective-permute-done.5 = f32[256,256]{1,0:T(8,128)S(1)} collective-permute-done((f32[256,256]{1,0:T(8,128)}, f32[256,256]{1,0:T(8,128)S(1)}, u32[]{:S(2)}, u32[]{:S(2)}) %collective-permute-start.5) | collective-permute-done | bytes 262176 | tf_op jit(solution)/shard_map/ppermute | solution.py:26
  46.0 1.3 collective-permute-start.14
  47.3 1.3 collective-permute-start.15
  48.7 0.4 collective-permute-start.4
  49.1 1.2 copy-done
  50.3 1.2 copy-done.2
  51.5 0.9 copy-done.4
  52.5 0.9 copy-done.6
  53.4 7.2 %shard_map.28.refs_8_ = f32[8,1024,256]{2,1,0:T(8,128)S(1)} custom-call(s32[64]{0:T(128)S(1)} %broadcast_add_fusion.2.tab_ref, f32[1024,256]{1,0:T(8,128)S(1)} %copy-done, f32[1024,256]{1,0:T(8,128)S(1)} %copy-done.2, f32[1,256,256]{2,1,0:T(8,128)S(1)} %bitcast.10, f32[1,256,256]{2,1,0:T(8,128)S(1)} %copy-done.6, ...), custom_call_target="tpu_custom_call" | custom-call | flops 3221225472 | bytes 12582912 | tf_op jit(solution)/shard_map/pallas_call | solution.py:175
  60.6 3.2 %copy-done.7 = f32[8,1024,256]{2,1,0:T(8,128)} copy-done((f32[8,1024,256]{2,1,0:T(8,128)}, f32[8,1024,256]{2,1,0:T(8,128)S(1)}, u32[]{:S(2)}) %copy-start.7) | copy-done | bytes 8388632
  63.8 2.0 %collective-permute-start.6 = (f32[1,256,256]{2,1,0:T(8,128)S(1)}, f32[1,256,256]{2,1,0:T(8,128)S(1)}, u32[]{:S(2)}, u32[]{:S(2)}) collective-permute-start(f32[1,256,256]{2,1,0:T(8,128)S(1)} %bitcast.11), channel_id=1, source_target_pairs={{0,32},{32,64},{64,96},{1,33},{33,65},{65,97},{2,34},{34,66},{66,9... | collective-permute-start | bytes 786440 | tf_op jit(solution)/shard_map/ppermute | solution.py:44
  65.9 3.0 %collective-permute-done.15.refs_7_ = f32[2,256,256]{2,1,0:T(8,128)S(1)} collective-permute-done((f32[2,256,256]{2,1,0:T(8,128)S(1)}, f32[2,256,256]{2,1,0:T(8,128)S(1)}, u32[]{:S(2)}, u32[]{:S(2)}) %collective-permute-start.15) | collective-permute-done | bytes 524320 | tf_op jit(solution)/shard_map/ppermute | solution.py:44
  68.9 1.3 collective-permute-start.7
  70.2 5.3 %collective-permute-start.8 = (f32[1,256,256]{2,1,0:T(8,128)S(1)}, f32[1,256,256]{2,1,0:T(8,128)S(1)}, u32[]{:S(2)}, u32[]{:S(2)}) collective-permute-start(f32[1,256,256]{2,1,0:T(8,128)S(1)} %bitcast.13), channel_id=1, source_target_pairs={{0,96},{1,97},{2,98},{3,99},{4,100},{5,101},{6,102},{7,103},{8,104... | collective-permute-start | bytes 786440 | tf_op jit(solution)/shard_map/ppermute | solution.py:44
  75.5 15.3 %shard_map.29.refs_6_ = f32[8,1024,256]{2,1,0:T(8,128)} custom-call(s32[64]{0:T(128)S(1)} %broadcast_add_fusion.2.tab_ref, f32[1024,256]{1,0:T(8,128)S(1)} %collective-permute-done.refs_0_, f32[1024,256]{1,0:T(8,128)} %collective-permute-done.9.refs_1_, f32[1024,256]{1,0:T(8,128)S(1)} %collective-permute-done.10.refs_2_, ...), custom_call_target="tpu_custom_call" | custom-call | flops 6442450944 | bytes 12582912 | tf_op jit(solution)/shard_map/pallas_call | solution.py:175
  90.9 10.9 %shard_map.30 = (f32[8,64,512]{2,1,0:T(8,128)S(1)}, f32[8,64,512]{2,1,0:T(8,128)S(1)}, f32[8,64,512]{2,1,0:T(8,128)S(1)}, f32[8,64,512]{2,1,0:T(8,128)S(1)}, f32...) custom-call(s32[64]{0:T(128)S(1)} %broadcast_add_fusion.2.tab_ref, ...), custom_call_target="tpu_custom_call" | custom-call | flops 3221225472 | bytes 12582912 | tf_op jit(solution)/shard_map/pallas_call | solution.py:175
  101.8 4.3 %collective-permute-start.25 = (f32[8,64,512]{2,1,0:T(8,128)S(1)}, f32[8,64,512]{2,1,0:T(8,128)S(1)}, u32[]{:S(2)}, u32[]{:S(2)}) collective-permute-start(f32[8,64,512]{2,1,0:T(8,128)S(1)} %get-tuple-element.27), channel_id=1, source_target_pairs={{0,12},{1,13},{2,14},{3,15},{4,0},{5,1},{6,2},{7,3},{8,4},{9,5},{1... | collective-permute-start | bytes 3145736 | tf_op jit(solution)/shard_map/ppermute | solution.py:26
  106.1 0.0 collective-permute-start.19
  106.1 11.7 %collective-permute-done.25 = f32[8,64,512]{2,1,0:T(8,128)S(1)} collective-permute-done((f32[8,64,512]{2,1,0:T(8,128)S(1)}, f32[8,64,512]{2,1,0:T(8,128)S(1)}, u32[]{:S(2)}, u32[]{:S(2)}) %collective-permute-start.25) | collective-permute-done | bytes 1048608 | tf_op jit(solution)/shard_map/ppermute | solution.py:26
  117.8 0.2 add.271
  118.0 3.5 %collective-permute-start.26 = (f32[8,64,512]{2,1,0:T(8,128)S(1)}, f32[8,64,512]{2,1,0:T(8,128)S(1)}, u32[]{:S(2)}, u32[]{:S(2)}) collective-permute-start(f32[8,64,512]{2,1,0:T(8,128)S(1)} %add.271), channel_id=1, source_target_pairs={{0,12},{1,13},{2,14},{3,15},{4,0},{5,1},{6,2},{7,3},{8,4},{9,5},{1... | collective-permute-start | bytes 3145736 | tf_op jit(solution)/shard_map/ppermute | solution.py:26
  121.5 0.1 collective-permute-start.21
  121.6 0.2 add.262
  121.8 1.5 collective-permute-start.20
  123.2 9.2 %collective-permute-done.27 = f32[8,64,512]{2,1,0:T(8,128)S(1)} collective-permute-done((f32[8,64,512]{2,1,0:T(8,128)S(1)}, f32[8,64,512]{2,1,0:T(8,128)S(1)}, u32[]{:S(2)}, u32[]{:S(2)}) %collective-permute-start.27) | collective-permute-done | bytes 1048608 | tf_op jit(solution)/shard_map/ppermute | solution.py:26
  132.4 0.8 collective-permute-done.26
  133.2 0.4 slice_add_fusion
  133.6 0.1 collective-permute-start.28
  133.7 0.1 collective-permute-start.29
  133.8 3.7 %collective-permute-start.30 = (f32[2,64,512]{2,1,0:T(8,128)S(1)}, f32[2,64,512]{2,1,0:T(8,128)S(1)}, u32[]{:S(2)}, u32[]{:S(2)}) collective-permute-start(f32[2,64,512]{2,1,0:T(8,128)S(1)} %get-tuple-element.30), channel_id=1, source_target_pairs={{0,18},{1,19},{2,16},{3,17},{4,22},{5,23},{6,20},{7,21},{8,26},{9,... | collective-permute-start | bytes 786440 | tf_op jit(solution)/shard_map/ppermute | solution.py:26
  137.5 9.8 %collective-permute-done.21 = f32[8,64,512]{2,1,0:T(8,128)S(1)} collective-permute-done((f32[8,64,512]{2,1,0:T(8,128)S(1)}, f32[8,64,512]{2,1,0:T(8,128)S(1)}, u32[]{:S(2)}, u32[]{:S(2)}) %collective-permute-start.21) | collective-permute-done | bytes 1048608 | tf_op jit(solution)/shard_map/ppermute | solution.py:26
  147.3 2.1 %collective-permute-start.31 = (f32[2,64,512]{2,1,0:T(8,128)S(1)}, f32[2,64,512]{2,1,0:T(8,128)S(1)}, u32[]{:S(2)}, u32[]{:S(2)}) collective-permute-start(f32[2,64,512]{2,1,0:T(8,128)S(1)} %get-tuple-element.29), channel_id=1, source_target_pairs={{0,19},{1,16},{2,17},{3,18},{4,23},{5,20},{6,21},{7,22},{8,27},{9,... | collective-permute-start | bytes 786440 | tf_op jit(solution)/shard_map/ppermute | solution.py:26
  149.4 0.4 slice_add_fusion.8
  149.7 0.1 collective-permute-start.22
  149.8 3.2 %collective-permute-start.23 = (f32[2,64,512]{2,1,0:T(8,128)S(1)}, f32[2,64,512]{2,1,0:T(8,128)S(1)}, u32[]{:S(2)}, u32[]{:S(2)}) collective-permute-start(f32[2,64,512]{2,1,0:T(8,128)S(1)} %get-tuple-element.34), channel_id=1, source_target_pairs={{0,2},{1,3},{2,0},{3,1},{4,6},{5,7},{6,4},{7,5},{8,10},{9,11},{10,... | collective-permute-start | bytes 786440 | tf_op jit(solution)/shard_map/ppermute | solution.py:26
  153.0 0.0 collective-permute-done.31.refs_7_
  153.1 3.5 %collective-permute-done.22.refs_1_ = f32[2,64,512]{2,1,0:T(8,128)S(1)} collective-permute-done((f32[2,64,512]{2,1,0:T(8,128)S(1)}, f32[2,64,512]{2,1,0:T(8,128)S(1)}, u32[]{:S(2)}, u32[]{:S(2)}) %collective-permute-start.22) | collective-permute-done | bytes 262176 | tf_op jit(solution)/shard_map/ppermute | solution.py:26
  156.5 3.1 %collective-permute-done.23.refs_2_ = f32[2,64,512]{2,1,0:T(8,128)S(1)} collective-permute-done((f32[2,64,512]{2,1,0:T(8,128)S(1)}, f32[2,64,512]{2,1,0:T(8,128)S(1)}, u32[]{:S(2)}, u32[]{:S(2)}) %collective-permute-start.23) | collective-permute-done | bytes 262176 | tf_op jit(solution)/shard_map/ppermute | solution.py:26
  159.6 0.4 collective-permute-done.24.refs_3_
  160.0 2.6 %join.1 = f32[1,2,512,512]{3,2,1,0:T(8,128)} custom-call(s32[3]{0:T(128)S(1)} %copy-done.3, f32[2,64,512]{2,1,0:T(8,128)S(1)} %get-tuple-element.36.refs_0_, f32[2,64,512]{2,1,0:T(8,128)S(1)} %collective-permute-done.22.refs_1_, f32[2,64,512]{2,1,0:T(8,128)S(1)} %collective-permute-done.23.refs_2_, f32[2,64,512]{2,1,0:T(8,128)S(1)} %collective-permute-done.24.refs_3_, ...), custom_call_target="tpu_custom_call" | custom-call | flops 1000000 | bytes 4194304 | tf_op jit(solution)/shard_map/join/pallas_call | solution.py:213
  (34 shorter events, 0.1 us)
Async XLA Ops:
  0.0 4.8 %collective-permute-start.2 = (f32[1024,256]{1,0:T(8,128)}, f32[1024,256]{1,0:T(8,128)S(1)}, u32[]{:S(2)}, u32[]{:S(2)}) collective-permute-start(f32[1024,256]{1,0:T(8,128)} %refs_0_.1), channel_id=1, source_target_pairs={{0,16},{16,0},{1,17},{17,1},{2,18},{18,2},{3,19},{19,3},{4,20},{20... | collective-permute-start | bytes 3145736 | tf_op jit(solution)/shard_map/ppermute | solution.py:44
  1.4 26.6 %collective-permute-start = (f32[1024,256]{1,0:T(8,128)}, f32[1024,256]{1,0:T(8,128)S(1)}, u32[]{:S(2)}, u32[]{:S(2)}) collective-permute-start(f32[1024,256]{1,0:T(8,128)} %refs_0_.1), channel_id=1, source_target_pairs={{0,1},{1,2},{2,3},{3,0},{4,5},{5,6},{6,7},{7,4},{8,9},{9,10},{10,1... | collective-permute-start | bytes 3145736 | tf_op jit(solution)/shard_map/ppermute | solution.py:26
  2.8 25.3 %collective-permute-start.10 = (f32[1024,256]{1,0:T(8,128)}, f32[1024,256]{1,0:T(8,128)S(1)}, u32[]{:S(2)}, u32[]{:S(2)}) collective-permute-start(f32[1024,256]{1,0:T(8,128)} %refs_0_.1), channel_id=1, source_target_pairs={{0,3},{1,0},{2,1},{3,2},{4,7},{5,4},{6,5},{7,6},{8,11},{9,8},{10,9... | collective-permute-start | bytes 3145736 | tf_op jit(solution)/shard_map/ppermute | solution.py:26
  4.8 1.0 copy-start.1
  8.4 11.3 %collective-permute-start.11 = (f32[256,256]{1,0:T(8,128)}, f32[256,256]{1,0:T(8,128)S(1)}, u32[]{:S(2)}, u32[]{:S(2)}) collective-permute-start(f32[256,256]{1,0:T(8,128)} %get-tuple-element.18), channel_id=1, source_target_pairs={{0,1},{1,2},{2,3},{3,0},{4,5},{5,6},{6,7},{7,4},{8,9},{9,10},{10,1... | collective-permute-start | bytes 786440 | tf_op jit(solution)/shard_map/ppermute | solution.py:26
  8.9 14.0 %collective-permute-start.12 = (f32[256,256]{1,0:T(8,128)}, f32[256,256]{1,0:T(8,128)S(1)}, u32[]{:S(2)}, u32[]{:S(2)}) collective-permute-start(f32[256,256]{1,0:T(8,128)} %get-tuple-element.19), channel_id=1, source_target_pairs={{0,3},{1,0},{2,1},{3,2},{4,7},{5,4},{6,5},{7,6},{8,11},{9,8},{10,9... | collective-permute-start | bytes 786440 | tf_op jit(solution)/shard_map/ppermute | solution.py:26
  11.1 37.6 %collective-permute-start.3 = (f32[1024,256]{1,0:T(8,128)}, f32[1024,256]{1,0:T(8,128)}, u32[]{:S(2)}, u32[]{:S(2)}) collective-permute-start(f32[1024,256]{1,0:T(8,128)} %copy-done.1), channel_id=1, source_target_pairs={{0,3},{1,0},{2,1},{3,2},{4,7},{5,4},{6,5},{7,6},{8,11},{9,8},{10,9... | collective-permute-start | bytes 3145736 | tf_op jit(solution)/shard_map/ppermute | solution.py:26
  19.7 9.7 %collective-permute-start.16 = (f32[1,256,256]{2,1,0:T(8,128)}, f32[1,256,256]{2,1,0:T(8,128)S(1)}, u32[]{:S(2)}, u32[]{:S(2)}) collective-permute-start(f32[1,256,256]{2,1,0:T(8,128)} %bitcast.7), channel_id=1, source_target_pairs={{0,32},{32,64},{64,96},{1,33},{33,65},{65,97},{2,34},{34,66},{66,9... | collective-permute-start | bytes 786440 | tf_op jit(solution)/shard_map/ppermute | solution.py:44
  22.9 11.1 %collective-permute-start.17 = (f32[1,256,256]{2,1,0:T(8,128)}, f32[1,256,256]{2,1,0:T(8,128)}, u32[]{:S(2)}, u32[]{:S(2)}) collective-permute-start(f32[1,256,256]{2,1,0:T(8,128)} %bitcast.8), channel_id=1, source_target_pairs={{0,64},{32,96},{1,65},{33,97},{2,66},{34,98},{3,67},{35,99},{4,68}... | collective-permute-start | bytes 786440 | tf_op jit(solution)/shard_map/ppermute | solution.py:44
  28.0 42.2 %collective-permute-start.9 = (f32[1024,256]{1,0:T(8,128)}, f32[1024,256]{1,0:T(8,128)}, u32[]{:S(2)}, u32[]{:S(2)}) collective-permute-start(f32[1024,256]{1,0:T(8,128)} %copy-done.1), channel_id=1, source_target_pairs={{0,1},{1,2},{2,3},{3,0},{4,5},{5,6},{6,7},{7,4},{8,9},{9,10},{10,1... | collective-permute-start | bytes 3145736 | tf_op jit(solution)/shard_map/ppermute | solution.py:26
  28.1 19.2 %collective-permute-start.13 = (f32[2,256,256]{2,1,0:T(8,128)S(1)}, f32[2,256,256]{2,1,0:T(8,128)S(1)}, u32[]{:S(2)}, u32[]{:S(2)}) collective-permute-start(f32[2,256,256]{2,1,0:T(8,128)S(1)} %pad_maximum_fusion.refs_4_), channel_id=1, source_target_pairs={{0,32},{32,64},{64,96},{1,33},{33,65},{65,97},{2,34},{34,66},{66,9... | collective-permute-start | bytes 1572872 | tf_op jit(solution)/shard_map/ppermute | solution.py:44
  29.4 0.7 copy-start.5
  30.2 6.7 %collective-permute-start.18 = (f32[1,256,256]{2,1,0:T(8,128)}, f32[1,256,256]{2,1,0:T(8,128)}, u32[]{:S(2)}, u32[]{:S(2)}) collective-permute-start(f32[1,256,256]{2,1,0:T(8,128)} %bitcast.9), channel_id=1, source_target_pairs={{0,96},{1,97},{2,98},{3,99},{4,100},{5,101},{6,102},{7,103},{8,104... | collective-permute-start | bytes 786440 | tf_op jit(solution)/shard_map/ppermute | solution.py:44
  34.0 12.0 %collective-permute-start.5 = (f32[256,256]{1,0:T(8,128)}, f32[256,256]{1,0:T(8,128)S(1)}, u32[]{:S(2)}, u32[]{:S(2)}) collective-permute-start(f32[256,256]{1,0:T(8,128)} %get-tuple-element.17), channel_id=1, source_target_pairs={{0,2},{1,3},{2,0},{3,1},{4,6},{5,7},{6,4},{7,5},{8,10},{9,11},{10,... | collective-permute-start | bytes 786440 | tf_op jit(solution)/shard_map/ppermute | solution.py:26
  36.9 54.0 %collective-permute-start.1 = (f32[1024,256]{1,0:T(8,128)S(1)}, f32[1024,256]{1,0:T(8,128)S(1)}, u32[]{:S(2)}, u32[]{:S(2)}) collective-permute-start(f32[1024,256]{1,0:T(8,128)S(1)} %collective-permute-done.refs_0_), channel_id=1, source_target_pairs={{0,1},{1,2},{2,3},{3,0},{4,5},{5,6},{6,7},{7,4},{8,9},{9,10},{10,1... | collective-permute-start | bytes 3145736 | tf_op jit(solution)/shard_map/ppermute | solution.py:26
  46.0 17.8 %collective-permute-start.14 = (f32[2,256,256]{2,1,0:T(8,128)S(1)}, f32[2,256,256]{2,1,0:T(8,128)S(1)}, u32[]{:S(2)}, u32[]{:S(2)}) collective-permute-start(f32[2,256,256]{2,1,0:T(8,128)S(1)} %pad_maximum_fusion.refs_4_), channel_id=1, source_target_pairs={{0,64},{32,96},{1,65},{33,97},{2,66},{34,98},{3,67},{35,99},{4,68}... | collective-permute-start | bytes 1572872 | tf_op jit(solution)/shard_map/ppermute | solution.py:44
  47.3 21.6 %collective-permute-start.15 = (f32[2,256,256]{2,1,0:T(8,128)S(1)}, f32[2,256,256]{2,1,0:T(8,128)S(1)}, u32[]{:S(2)}, u32[]{:S(2)}) collective-permute-start(f32[2,256,256]{2,1,0:T(8,128)S(1)} %pad_maximum_fusion.refs_4_), channel_id=1, source_target_pairs={{0,96},{1,97},{2,98},{3,99},{4,100},{5,101},{6,102},{7,103},{8,104... | collective-permute-start | bytes 1572872 | tf_op jit(solution)/shard_map/ppermute | solution.py:44
  48.7 42.2 %collective-permute-start.4 = (f32[1024,256]{1,0:T(8,128)}, f32[1024,256]{1,0:T(8,128)S(1)}, u32[]{:S(2)}, u32[]{:S(2)}) collective-permute-start(f32[1024,256]{1,0:T(8,128)} %collective-permute-done.3.refs_3_), channel_id=1, source_target_pairs={{0,3},{1,0},{2,1},{3,2},{4,7},{5,4},{6,5},{7,6},{8,11},{9,8},{10,9... | collective-permute-start | bytes 3145736 | tf_op jit(solution)/shard_map/ppermute | solution.py:26
  49.1 1.2 copy-start
  50.3 1.2 copy-start.2
  51.5 0.9 copy-start.4
  52.5 0.9 copy-start.6
  60.6 3.2 %copy-start.7 = (f32[8,1024,256]{2,1,0:T(8,128)}, f32[8,1024,256]{2,1,0:T(8,128)S(1)}, u32[]{:S(2)}) copy-start(f32[8,1024,256]{2,1,0:T(8,128)S(1)} %shard_map.28.refs_8_) | copy-start | bytes 25165828
  63.8 27.0 %collective-permute-start.6 = (f32[1,256,256]{2,1,0:T(8,128)S(1)}, f32[1,256,256]{2,1,0:T(8,128)S(1)}, u32[]{:S(2)}, u32[]{:S(2)}) collective-permute-start(f32[1,256,256]{2,1,0:T(8,128)S(1)} %bitcast.11), channel_id=1, source_target_pairs={{0,32},{32,64},{64,96},{1,33},{33,65},{65,97},{2,34},{34,66},{66,9... | collective-permute-start | bytes 786440 | tf_op jit(solution)/shard_map/ppermute | solution.py:44
  68.9 21.9 %collective-permute-start.7 = (f32[1,256,256]{2,1,0:T(8,128)S(1)}, f32[1,256,256]{2,1,0:T(8,128)S(1)}, u32[]{:S(2)}, u32[]{:S(2)}) collective-permute-start(f32[1,256,256]{2,1,0:T(8,128)S(1)} %bitcast.12), channel_id=1, source_target_pairs={{0,64},{32,96},{1,65},{33,97},{2,66},{34,98},{3,67},{35,99},{4,68}... | collective-permute-start | bytes 786440 | tf_op jit(solution)/shard_map/ppermute | solution.py:44
  70.2 20.6 %collective-permute-start.8 = (f32[1,256,256]{2,1,0:T(8,128)S(1)}, f32[1,256,256]{2,1,0:T(8,128)S(1)}, u32[]{:S(2)}, u32[]{:S(2)}) collective-permute-start(f32[1,256,256]{2,1,0:T(8,128)S(1)} %bitcast.13), channel_id=1, source_target_pairs={{0,96},{1,97},{2,98},{3,99},{4,100},{5,101},{6,102},{7,103},{8,104... | collective-permute-start | bytes 786440 | tf_op jit(solution)/shard_map/ppermute | solution.py:44
  101.8 58.2 %copy-start.3 = (s32[3]{0:T(128)S(1)}, s32[3]{0:T(128)}, u32[]{:S(2)}) copy-start(s32[3]{0:T(128)} %pad_add_fusion.at_ref) | copy-start | bytes 40
  101.8 16.0 %collective-permute-start.25 = (f32[8,64,512]{2,1,0:T(8,128)S(1)}, f32[8,64,512]{2,1,0:T(8,128)S(1)}, u32[]{:S(2)}, u32[]{:S(2)}) collective-permute-start(f32[8,64,512]{2,1,0:T(8,128)S(1)} %get-tuple-element.27), channel_id=1, source_target_pairs={{0,12},{1,13},{2,14},{3,15},{4,0},{5,1},{6,2},{7,3},{8,4},{9,5},{1... | collective-permute-start | bytes 3145736 | tf_op jit(solution)/shard_map/ppermute | solution.py:26
  106.1 15.5 %collective-permute-start.19 = (f32[8,64,512]{2,1,0:T(8,128)S(1)}, f32[8,64,512]{2,1,0:T(8,128)S(1)}, u32[]{:S(2)}, u32[]{:S(2)}) collective-permute-start(f32[8,64,512]{2,1,0:T(8,128)S(1)} %get-tuple-element.23), channel_id=1, source_target_pairs={{0,4},{1,5},{2,6},{3,7},{4,8},{5,9},{6,10},{7,11},{8,12},{9,13},{1... | collective-permute-start | bytes 3145736 | tf_op jit(solution)/shard_map/ppermute | solution.py:26
  106.1 26.4 %collective-permute-start.27 = (f32[8,64,512]{2,1,0:T(8,128)S(1)}, f32[8,64,512]{2,1,0:T(8,128)S(1)}, u32[]{:S(2)}, u32[]{:S(2)}) collective-permute-start(f32[8,64,512]{2,1,0:T(8,128)S(1)} %get-tuple-element.28), channel_id=1, source_target_pairs={{0,4},{1,5},{2,6},{3,7},{4,8},{5,9},{6,10},{7,11},{8,12},{9,13},{1... | collective-permute-start | bytes 3145736 | tf_op jit(solution)/shard_map/ppermute | solution.py:26
  118.0 15.2 %collective-permute-start.26 = (f32[8,64,512]{2,1,0:T(8,128)S(1)}, f32[8,64,512]{2,1,0:T(8,128)S(1)}, u32[]{:S(2)}, u32[]{:S(2)}) collective-permute-start(f32[8,64,512]{2,1,0:T(8,128)S(1)} %add.271), channel_id=1, source_target_pairs={{0,12},{1,13},{2,14},{3,15},{4,0},{5,1},{6,2},{7,3},{8,4},{9,5},{1... | collective-permute-start | bytes 3145736 | tf_op jit(solution)/shard_map/ppermute | solution.py:26
  121.5 25.8 %collective-permute-start.21 = (f32[8,64,512]{2,1,0:T(8,128)S(1)}, f32[8,64,512]{2,1,0:T(8,128)S(1)}, u32[]{:S(2)}, u32[]{:S(2)}) collective-permute-start(f32[8,64,512]{2,1,0:T(8,128)S(1)} %get-tuple-element.24), channel_id=1, source_target_pairs={{0,12},{1,13},{2,14},{3,15},{4,0},{5,1},{6,2},{7,3},{8,4},{9,5},{1... | collective-permute-start | bytes 3145736 | tf_op jit(solution)/shard_map/ppermute | solution.py:26
  121.8 27.6 %collective-permute-start.20 = (f32[8,64,512]{2,1,0:T(8,128)S(1)}, f32[8,64,512]{2,1,0:T(8,128)S(1)}, u32[]{:S(2)}, u32[]{:S(2)}) collective-permute-start(f32[8,64,512]{2,1,0:T(8,128)S(1)} %add.262), channel_id=1, source_target_pairs={{0,4},{1,5},{2,6},{3,7},{4,8},{5,9},{6,10},{7,11},{8,12},{9,13},{1... | collective-permute-start | bytes 3145736 | tf_op jit(solution)/shard_map/ppermute | solution.py:26
  133.6 16.2 %collective-permute-start.28 = (f32[2,64,512]{2,1,0:T(8,128)S(1)}, f32[2,64,512]{2,1,0:T(8,128)S(1)}, u32[]{:S(2)}, u32[]{:S(2)}) collective-permute-start(f32[2,64,512]{2,1,0:T(8,128)S(1)} %get-tuple-element.32), channel_id=1, source_target_pairs={{0,16},{1,17},{2,18},{3,19},{4,20},{5,21},{6,22},{7,23},{8,24},{9,... | collective-permute-start | bytes 786440 | tf_op jit(solution)/shard_map/ppermute | solution.py:26
  133.7 19.3 %collective-permute-start.29 = (f32[2,64,512]{2,1,0:T(8,128)S(1)}, f32[2,64,512]{2,1,0:T(8,128)S(1)}, u32[]{:S(2)}, u32[]{:S(2)}) collective-permute-start(f32[2,64,512]{2,1,0:T(8,128)S(1)} %get-tuple-element.31), channel_id=1, source_target_pairs={{0,17},{1,18},{2,19},{3,16},{4,21},{5,22},{6,23},{7,20},{8,25},{9,... | collective-permute-start | bytes 786440 | tf_op jit(solution)/shard_map/ppermute | solution.py:26
  133.8 19.3 %collective-permute-start.30 = (f32[2,64,512]{2,1,0:T(8,128)S(1)}, f32[2,64,512]{2,1,0:T(8,128)S(1)}, u32[]{:S(2)}, u32[]{:S(2)}) collective-permute-start(f32[2,64,512]{2,1,0:T(8,128)S(1)} %get-tuple-element.30), channel_id=1, source_target_pairs={{0,18},{1,19},{2,16},{3,17},{4,22},{5,23},{6,20},{7,21},{8,26},{9,... | collective-permute-start | bytes 786440 | tf_op jit(solution)/shard_map/ppermute | solution.py:26
  147.3 5.8 %collective-permute-start.31 = (f32[2,64,512]{2,1,0:T(8,128)S(1)}, f32[2,64,512]{2,1,0:T(8,128)S(1)}, u32[]{:S(2)}, u32[]{:S(2)}) collective-permute-start(f32[2,64,512]{2,1,0:T(8,128)S(1)} %get-tuple-element.29), channel_id=1, source_target_pairs={{0,19},{1,16},{2,17},{3,18},{4,23},{5,20},{6,21},{7,22},{8,27},{9,... | collective-permute-start | bytes 786440 | tf_op jit(solution)/shard_map/ppermute | solution.py:26
  149.7 6.8 %collective-permute-start.22 = (f32[2,64,512]{2,1,0:T(8,128)S(1)}, f32[2,64,512]{2,1,0:T(8,128)S(1)}, u32[]{:S(2)}, u32[]{:S(2)}) collective-permute-start(f32[2,64,512]{2,1,0:T(8,128)S(1)} %get-tuple-element.35), channel_id=1, source_target_pairs={{0,1},{1,2},{2,3},{3,0},{4,5},{5,6},{6,7},{7,4},{8,9},{9,10},{10,1... | collective-permute-start | bytes 786440 | tf_op jit(solution)/shard_map/ppermute | solution.py:26
  149.8 9.8 %collective-permute-start.23 = (f32[2,64,512]{2,1,0:T(8,128)S(1)}, f32[2,64,512]{2,1,0:T(8,128)S(1)}, u32[]{:S(2)}, u32[]{:S(2)}) collective-permute-start(f32[2,64,512]{2,1,0:T(8,128)S(1)} %get-tuple-element.34), channel_id=1, source_target_pairs={{0,2},{1,3},{2,0},{3,1},{4,6},{5,7},{6,4},{7,5},{8,10},{9,11},{10,... | collective-permute-start | bytes 786440 | tf_op jit(solution)/shard_map/ppermute | solution.py:26
  153.0 6.9 %collective-permute-start.24 = (f32[2,64,512]{2,1,0:T(8,128)S(1)}, f32[2,64,512]{2,1,0:T(8,128)S(1)}, u32[]{:S(2)}, u32[]{:S(2)}) collective-permute-start(f32[2,64,512]{2,1,0:T(8,128)S(1)} %get-tuple-element.33), channel_id=1, source_target_pairs={{0,3},{1,0},{2,1},{3,2},{4,7},{5,4},{6,5},{7,6},{8,11},{9,8},{10,9... | collective-permute-start | bytes 786440 | tf_op jit(solution)/shard_map/ppermute | solution.py:26
where the time goes:
time: 165 us; the launch traced here: 163 us
  waiting for transfers between devices  59.3 us (36%)
  starting transfers between devices  52.5 us (32%)
  Pallas kernels  38.5 us (23%)
  local copies, waits for them, and re-layouts  9.27 us (6%)
  other arithmetic  2.73 us (2%)
    ppermute x22, waiting for transfers between devices, move(): return lax.ppermute(value, ('c', 'y', 'z'), pairs)  55.6 us
    pallas_call x3, Pallas kernels, product(): pl.pallas_call(functools.partial(product_kernel, q, count, first, last),...  33.3 us
    ppermute x22, starting transfers between devices, move(): return lax.ppermute(value, ('c', 'y', 'z'), pairs)  26.5 us
    ppermute x10, starting transfers between devices, over(): return lax.ppermute(value, axis, pairs)  26 us
    unnamed x16, local copies, waits for them, and re-layouts  9.27 us
    ppermute x10, waiting for transfers between devices, over(): return lax.ppermute(value, axis, pairs)  3.72 us
  transfers between devices with their start and end apart: 32, of which 11 were waited for; matrix products, arithmetic and copies ran while one was open for 2% of the time, Pallas kernels for 15%

commit v1 on v0

--- a/solution.py
+++ b/solution.py
@@ -13,6 +13,7 @@
 VMEM = pltpu.VMEM
 SMEM = pltpu.SMEM
 HBM = pltpu.HBM
+GRANT = 60 * 1024 * 1024
 
 
 def move(value, target):
@@ -38,10 +39,12 @@
     return move(value, lambda c, g, r: (1 - c, g + step, r))
 
 
-def over(value, axis, step):
-    size = lax.axis_size(axis)
-    pairs = [(k, (k + step) % size) for k in range(size) if axis == "c" or k + step < size]
-    return lax.ppermute(value, axis, pairs)
+def swap(value):
+    return lax.ppermute(value, "c", [(0, 1), (1, 0)])
+
+
+def hop(value, pairs):
+    return lax.ppermute(value, "x", pairs)
 
 
 def specs(space, count):
@@ -71,79 +74,104 @@
     )(at, mine, other)
 
 
-def product_kernel(q, slabs, first, last, tab_ref, *refs):
-    a_refs, refs = refs[: 2 * slabs], refs[2 * slabs :]
-    b_refs, refs = refs[:N], refs[N:]
-    total_ref, refs = (None, refs) if first else (refs[0], refs[1:])
+def split_kernel(*refs):
+    for source, place in zip(refs[:2], refs[2:]):
+        value = source[...]
+        inner = value.shape[1]
+        high = value.astype(jnp.bfloat16)
+        place[:, :inner] = high
+        place[:, inner:] = (value - high.astype(jnp.float32)).astype(jnp.bfloat16)
+
+
+def split(pair):
+    rows, inner = pair[0].shape
+    block = rows // 4
+    return pl.pallas_call(
+        split_kernel,
+        grid=(4,),
+        out_shape=[jax.ShapeDtypeStruct((rows, 2 * inner), jnp.bfloat16)] * 2,
+        in_specs=[pl.BlockSpec((block, inner), lambda i: (i, 0))] * 2,
+        out_specs=[pl.BlockSpec((block, 2 * inner), lambda i: (i, 0))] * 2,
+        cost_estimate=pl.CostEstimate(flops=10**6, bytes_accessed=16 * rows * inner, transcendentals=0),
+        compiler_params=pltpu.CompilerParams(vmem_limit_bytes=GRANT),
+    )(*pair)
+
+
+def product_kernel(q, work, totals, last, tab_ref, *refs):
+    count = len(work)
+    a_refs, refs = refs[: 2 * count], refs[2 * count :]
+    b_refs = []
+    for places in work:
+        b_refs.append(refs[: len(places)])
+        refs = refs[len(places) :]
+    total_refs, refs = refs[: len(totals)], refs[len(totals) :]
     outs, refs = refs[: 8 if last else 1], refs[8 if last else 1 :]
-    a_in, b_in, a3, b3, acc, in_sems, total_sem, out_sems, *held = refs
-    rows, inner = a_refs[0].shape
-    half, side = rows // 2, rows // 4
-    copies = []
-    for s in range(slabs):
-        now = [(a_refs[2 * s + group], a_in.at[s, group * rows : (group + 1) * rows, :]) for group in range(2)]
-        for d in range(N):
-            now.append((b_refs[d].at[s], b_in.at[s, 4 * q * d : 4 * q * (d + 1), :]))
-        now = [pltpu.make_async_copy(source, place, in_sems.at[s, k]) for k, (source, place) in enumerate(now)]
-        for copy in now:
-            copy.start()
-        copies.append(now)
-        if s == 0 and not first:
-            total = pltpu.make_async_copy(total_ref, acc, total_sem.at[0])
-            total.start()
-
-    def halves(value):
-        high = value.astype(jnp.bfloat16)
-        return high, (value - high.astype(jnp.float32)).astype(jnp.bfloat16)
-
-    def write(place, source, index):
-        copy = pltpu.make_async_copy(source, place, out_sems.at[index])
+    a_in, b_in, b2, acc, a_sems, b_sems, total_sems, out_sems, *held = refs
+    rows, inner = a_refs[0].shape[0], a_refs[0].shape[1] // 2
+    side, wide = rows // 4, 4 * q
+
+    def begin(source, place, sem):
+        copy = pltpu.make_async_copy(source, place, sem)
         copy.start()
         return copy
 
+    loads, waits = [], []
+    for k, places in enumerate(work):
+        now = [
+            begin(
+                b_refs[k][m].at[row : row + wide, :], b_in.at[k, wide * place : wide * (place + 1), :], b_sems.at[k, m]
+            )
+            for m, (place, row) in enumerate(places)
+        ]
+        for group in range(2):
+            now.append(
+                begin(a_refs[2 * k + group], a_in.at[k, group * rows : (group + 1) * rows, :], a_sems.at[k, group])
+            )
+        loads.append(now)
+        if k == 0:
+            for m, (ref, (low, high)) in enumerate(zip(total_refs, totals)):
+                part = (slice(None), slice(wide * low, wide * high), slice(None))
+                waits.append(begin(ref.at[part], acc.at[part], total_sems.at[m]))
+
     back = []
-    for s in range(slabs):
-        for copy in copies[s]:
+    fresh = not totals
+    for k, places in enumerate(work):
+        for copy in loads[k]:
             copy.wait()
-
-        def split(k, carry):
-            at = pl.ds(pl.multiple_of(k * half, half), half)
-            high, low = halves(a_in[s, at, :])
-            a3[at, 0:inner] = high
-            a3[at, inner : 2 * inner] = low
-            a3[at, 2 * inner :] = high
-            return carry
-
-        lax.fori_loop(0, 4, split, 0)
-        for m in range(2):
-            at = slice(m * half, (m + 1) * half)
-            high, low = halves(b_in[s, at, :])
-            b3[at, 0:inner] = high
-            b3[at, inner : 2 * inner] = high
-            b3[at, 2 * inner :] = low
-        if s == 0 and not first:
-            total.wait()
+        first, stop = places[0][0], places[-1][0] + 1
+        pieces = [(m, min(m + 2, stop)) for m in range(first, stop, 2)]
+        for low, high in pieces:
+            at = slice(wide * low, wide * high)
+            value = b_in[k, at, :]
+            upper = value.astype(jnp.bfloat16)
+            b2[at, :inner] = upper
+            b2[at, inner:] = (value - upper.astype(jnp.float32)).astype(jnp.bfloat16)
+        if k == 0:
+            for copy in waits:
+                copy.wait()
 
         def multiply(pair, carry):
             for part in range(2):
                 n = 2 * pair + part
-                right = a3[pl.ds(pl.multiple_of(n * side, side), side), :]
-                for m in range(2):
-                    at = slice(m * half, (m + 1) * half)
+                right = a_in[k, pl.ds(pl.multiple_of(n * side, side), side), :]
+                right = jnp.concatenate([right, right[:, :inner]], axis=1)
+                for low, high in pieces:
+                    at = slice(wide * low, wide * high)
+                    left = jnp.concatenate([b2[at, :inner], b2[at, :]], axis=1)
                     found = lax.dot_general(
-                        b3[at, :], right, (((1,), (1,)), ((), ())), preferred_element_type=jnp.float32
+                        left, right, (((1,), (1,)), ((), ())), preferred_element_type=jnp.float32
                     )
-                    acc[n, at, :] = found if first and s == 0 else acc[n, at, :] + found
+                    acc[n, at, :] = found if fresh and k == 0 else acc[n, at, :] + found
             return carry
 
-        if s < slabs - 1:
+        if k < count - 1:
             lax.fori_loop(0, 4, multiply, 0)
 
     for group in range(2):
         lax.fori_loop(2 * group, 2 * group + 2, multiply, 0)
         if not last:
-            part = slice(4 * group, 4 * group + 4)
-            back.append(write(outs[0].at[part], acc.at[part], group))
+            part = (slice(4 * group, 4 * group + 4), slice(wide * work[0][0][0], wide * (work[0][-1][0] + 1)), slice(None))
+            back.append(begin(acc.at[part], outs[0].at[part], out_sems.at[group]))
             continue
         for chunk in (2, 1, 3, 0):
             index = 2 * chunk + group
@@ -158,41 +186,42 @@
                 return carry
 
             lax.fori_loop(0, 8, place, 0)
-            back.append(write(outs[index], held[0].at[index], index))
+            back.append(begin(held[0].at[index], outs[index], out_sems.at[index]))
     for copy in back:
         copy.wait()
 
 
-def product(tab, slabs, slices, total, last):
-    rows, inner = slabs[0].shape
-    q, half, count = rows // 16, rows // 2, len(slabs) // 2
-    first = total is None
+def product(tab, work, totals, last):
+    rows, inner = work[0][0][0].shape[0], work[0][0][0].shape[1] // 2
+    q, half, count = rows // 16, rows // 2, len(work)
     if last:
         out_shape = [jax.ShapeDtypeStruct((8, q, half), jnp.float32)] * 8
     else:
         out_shape = [jax.ShapeDtypeStruct((8, rows, half // 2), jnp.float32)]
-    totals = [] if first else [total]
+    a_args = [part for parts, _ in work for part in parts]
+    b_args = [piece for _, slices in work for piece, _ in slices.values()]
+    places = tuple(tuple((place, row) for place, (_, row) in slices.items()) for _, slices in work)
     return pl.pallas_call(
-        functools.partial(product_kernel, q, count, first, last),
+        functools.partial(product_kernel, q, places, tuple(span for _, span in totals), last),
         out_shape=out_shape,
-        in_specs=specs(SMEM, 1) + specs(HBM, 2 * count + N + len(totals)),
+        in_specs=specs(SMEM, 1) + specs(HBM, len(a_args) + len(b_args) + len(totals)),
         out_specs=specs(HBM, len(out_shape)),
         scratch_shapes=[
-            VMEM((count, 2 * rows, inner), jnp.float32),
+            VMEM((count, 2 * rows, 2 * inner), jnp.bfloat16),
             VMEM((count, rows, inner), jnp.float32),
-            VMEM((2 * rows, 3 * inner), jnp.bfloat16),
-            VMEM((rows, 3 * inner), jnp.bfloat16),
+            VMEM((rows, 2 * inner), jnp.bfloat16),
             VMEM((8, rows, half // 2), jnp.float32),
-            pltpu.SemaphoreType.DMA((count, 6)),
-            pltpu.SemaphoreType.DMA((1,)),
+            pltpu.SemaphoreType.DMA((count, 2)),
+            pltpu.SemaphoreType.DMA((count, N)),
+            pltpu.SemaphoreType.DMA((2,)),
             pltpu.SemaphoreType.DMA((8,)),
         ]
         + ([VMEM((8, 8, q, half), jnp.float32)] if last else []),
-        compiler_params=pltpu.CompilerParams(vmem_limit_bytes=40 * 1024 * 1024),
+        compiler_params=pltpu.CompilerParams(vmem_limit_bytes=GRANT),
         cost_estimate=pl.CostEstimate(
             flops=4 * rows * rows * 3 * inner * count, bytes_accessed=12 * rows * inner * 4, transcendentals=0
         ),
-    )(tab, *slabs, *slices, *totals)
+    )(tab, *a_args, *b_args, *(total for total, _ in totals))
 
 
 def join_kernel(q, at_ref, *refs):
@@ -227,7 +256,8 @@
     i = lax.broadcasted_iota(jnp.int32, (blocks, blocks), 0)
     j = lax.broadcasted_iota(jnp.int32, (blocks, blocks), 1)
     group = j // 2
-    array = ((x - group // 2 + N) % N) * 2 + jnp.where(group % 2 == c, 0, 1)
+    behind = (x - group // 2 + N) % N
+    array = jnp.where(behind < 2, behind, 5 - behind) * 2 + jnp.where(group % 2 == c, 0, 1)
     code = jnp.where(j <= i, (array * 2 + j % 2) * 2 + i % 2 + 1, 0)
     index = jnp.arange(64, dtype=jnp.int32)
     far = (scatter + index // 16) % N
@@ -245,20 +275,41 @@
     at = jnp.stack([c, gather, scatter]).astype(jnp.int32)
     tab = tile_codes(owner, x, c, gather, scatter)
 
-    other = over(panel, "c", 1)
+    other = swap(panel)
+    up, down = [along(panel, 1)], [along(panel, -1)]
     first, *sends = cut(at, panel, other)
     small = [along(sends[s - 1], s) for s in range(1, N)]
-    slices = []
-    for piece in (first[None], jnp.stack([small[0], small[2]]), small[1][None]):
-        slices.append([piece] + [over(piece, "x", d) for d in range(1, N)])
-
-    up = [along(panel, 1), along(other, 1)]
-    down = [along(panel, -1), along(other, -1)]
+    up.append(along(other, 1))
+    down.append(along(other, -1))
     beyond = [along(up[0], 1), along(down[1], -1)]
 
-    (total,) = product(tab, [panel, other], slices[0], None, False)
-    (total,) = product(tab, up + down, slices[1], total, False)
-    own0, own1, near0, near1, far0, far1, last0, last1 = product(tab, beyond, slices[2], total, True)
+    onward, wrap = [(0, 1), (1, 2), (2, 3)], [(0, 3)]
+    both = jnp.concatenate([small[0], small[2]])
+    a1, a3 = hop(first, onward), hop(first, wrap)
+    b1, b3 = hop(both, onward), hop(both, wrap + [(1, 0)])
+    c1, c3 = hop(small[1], onward), hop(small[1], wrap)
+    a2, c2 = hop(a1, onward[1:]), hop(c1, onward[1:])
+    b2 = hop(b3, wrap + [(3, 2)])
+
+    own_parts = split([panel, other])
+    up_parts, down_parts = split(up), split(down)
+    far_parts = split(beyond)
+    wide = first.shape[0]
+    low, high = [(v, 0) for v in (both, b1, b3, b2)], [(v, wide) for v in (both, b1, b3, b2)]
+    zero, far = [(v, 0) for v in (first, a1, a3, a2)], [(v, 0) for v in (small[1], c1, c3, c2)]
+    three, four = range(3), range(4)
+    (base,) = product(tab, [(own_parts, dict(zip(four, zero)))], [], False)
+    (total,) = product(
+        tab, [(up_parts, dict(zip(three, low))), (down_parts, dict(zip(three, high)))], [(base, (0, 3))], False
+    )
+    outs = product(
+        tab,
+        [(up_parts, {3: low[3]}), (down_parts, {3: high[3]}), (far_parts, dict(zip(four, far)))],
+        [(total, (0, 3)), (base, (3, 4))],
+        True,
+    )
+    own0, own1, near0, near1, far0, far1, last0, last1 = outs
+
 
     up_far, down_far = across(far0, 1), across(far1, -1)
     up_near, down_near = across(near1, 1), across(last0, -1)

time: 165 us -> 183 us (1.11)
  Pallas kernels: 38.5 us -> 59 us
  local copies, waits for them, and re-layouts: 9.27 us -> 1.02 us
  other arithmetic: 2.73 us -> 7.03 us
  waiting for transfers between devices: 59.3 us -> 62.1 us
    pallas_call x3 -> x7, Pallas kernels: 33.3 us -> 53.8 us  [the longest x3 38.7 us: product(): pl.pallas_call(functools.partial(product_kernel, q, places, tuple((span f...]
    unnamed x16 -> x33, local copies, waits for them, and re-layouts: 9.27 us -> 1 us
    ppermute x22, waiting for transfers between devices: 55.6 us -> 62.1 us  [move(): return lax.ppermute(value, ('c', 'y', 'z'), pairs)]
    ppermute x10, starting transfers between devices: 26 us -> 19.5 us  [the longest x9 18.1 us: hop(): return lax.ppermute(value, 'x', pairs)]
    ppermute x22, starting transfers between devices: 26.5 us -> 32.9 us  [move(): return lax.ppermute(value, ('c', 'y', 'z'), pairs)]
    ppermute x10, waiting for transfers between devices: 3.72 us -> 0.03 us  [the longest x9 0.02 us: hop(): return lax.ppermute(value, 'x', pairs)]
  transfers between devices with their start and end apart: 32 -> 32, of which waited for: 11 -> 10; matrix products, arithmetic and copies ran while one was open for 2% -> 4% of each run, Pallas kernels for 15% -> 22%
where the time goes in v1:
time: 183 us; the launch traced here: 182 us
  waiting for transfers between devices  62.1 us (34%)
  Pallas kernels  59 us (32%)
  starting transfers between devices  52.4 us (29%)
  other arithmetic  7.03 us (4%)
    ppermute x22, waiting for transfers between devices, move(): return lax.ppermute(value, ('c', 'y', 'z'), pairs)  62.1 us
    pallas_call x3, Pallas kernels, product(): pl.pallas_call(functools.partial(product_kernel, q, places, tuple((span f...  38.7 us
    ppermute x22, starting transfers between devices, move(): return lax.ppermute(value, ('c', 'y', 'z'), pairs)  32.9 us
    ppermute x9, starting transfers between devices, hop(): return lax.ppermute(value, 'x', pairs)  18.1 us
    pallas_call x4, Pallas kernels, split(): pl.pallas_call(split_kernel, grid=(4,), out_shape=[jax.ShapeDtypeStruct((...  15.1 us
  transfers between devices with their start and end apart: 32, of which 10 were waited for; matrix products, arithmetic and copies ran while one was open for 4% of the time, Pallas kernels for 22%

profile of v1, /device:TPU:1, one launch (start us, length us, event | category | flops | bytes accessed | tf_op | source)
XLA Modules:
  0.0 182.0 jit_solution(15275914103754960162)
XLA Ops:
  0.0 1.4 collective-permute-start.1
  1.4 2.8 %collective-permute-start.3 = (f32[1024,256]{1,0:T(8,128)}, f32[1024,256]{1,0:T(8,128)S(1)}, u32[]{:S(2)}, u32[]{:S(2)}) collective-permute-start(f32[1024,256]{1,0:T(8,128)} %refs_0_.1), channel_id=1, source_target_pairs={{0,3},{1,0},{2,1},{3,2},{4,7},{5,4},{6,5},{7,6},{8,11},{9,8},{10,9... | collective-permute-start | bytes 3145736 | tf_op jit(solution)/shard_map/ppermute | solution.py:27
  4.2 0.0 collective-permute-start
  4.2 2.7 %collective-permute-start.4 = (f32[1024,256]{1,0:T(8,128)S(1)}, f32[1024,256]{1,0:T(8,128)}, u32[]{:S(2)}, u32[]{:S(2)}) collective-permute-start(f32[1024,256]{1,0:T(8,128)S(1)} %collective-permute-done.1.other_ref.refs_1_), channel_id=1, source_target_pairs={{0,3},{1,0},{2,1},{3,2},{4,7},{5,4},{6,5},{7,6},{8,11},{9,8},{10,9... | collective-permute-start | bytes 3145736 | tf_op jit(solution)/shard_map/ppermute | solution.py:27
  6.9 0.0 collective-permute-start.2
  6.9 0.7 pad_add_fusion.at_ref
  7.6 2.6 %cut.1 = (f32[256,256]{1,0:T(8,128)}, f32[256,256]{1,0:T(8,128)}, f32[256,256]{1,0:T(8,128)}, f32[256,256]{1,0:T(8,128)}) custom-call(s32[3]{0:T(128)} %pad_add_fusion.at_ref, f32[1024,256]{1,0:T(8,128)} %refs_0_.1, f32[1024,256]{1,0:T(8,128)} %copy-done.1), custom_call_target="tpu_custom_call" | custom-call | flops 1000000 | bytes 3145728 | tf_op jit(solution)/shard_map/cut/pallas_call | solution.py:67
  10.3 6.0 %collective-permute-done.3.refs_0_ = f32[1024,256]{1,0:T(8,128)S(1)} collective-permute-done((f32[1024,256]{1,0:T(8,128)}, f32[1024,256]{1,0:T(8,128)S(1)}, u32[]{:S(2)}, u32[]{:S(2)}) %collective-permute-start.3) | collective-permute-done | bytes 1048608 | tf_op jit(solution)/shard_map/ppermute | solution.py:27
  16.3 3.3 %collective-permute-start.8 = (f32[256,256]{1,0:T(8,128)}, f32[256,256]{1,0:T(8,128)S(1)}, u32[]{:S(2)}, u32[]{:S(2)}) collective-permute-start(f32[256,256]{1,0:T(8,128)} %get-tuple-element.32), channel_id=1, source_target_pairs={{0,3},{1,0},{2,1},{3,2},{4,7},{5,4},{6,5},{7,6},{8,11},{9,8},{10,9... | collective-permute-start | bytes 786440 | tf_op jit(solution)/shard_map/ppermute | solution.py:27
  19.6 3.1 %collective-permute-start.16 = (f32[256,256]{1,0:T(8,128)}, f32[256,256]{1,0:T(8,128)S(1)}, u32[]{:S(2)}, u32[]{:S(2)}) collective-permute-start(f32[256,256]{1,0:T(8,128)} %get-tuple-element.36.refs_2_), channel_id=1, source_target_pairs={{0,32},{32,64},{64,96},{1,33},{33,65},{65,97},{2,34},{34,66},{66,9... | collective-permute-start | bytes 786440 | tf_op jit(solution)/shard_map/ppermute | solution.py:47
  22.8 0.1 broadcast_select_fusion
  22.8 10.8 %collective-permute-done.7 = f32[256,256]{1,0:T(8,128)S(1)} collective-permute-done((f32[256,256]{1,0:T(8,128)}, f32[256,256]{1,0:T(8,128)S(1)}, u32[]{:S(2)}, u32[]{:S(2)}) %collective-permute-start.7) | collective-permute-done | bytes 262176 | tf_op jit(solution)/shard_map/ppermute | solution.py:27
  33.6 4.4 %collective-permute-start.17 = (f32[256,256]{1,0:T(8,128)}, f32[256,256]{1,0:T(8,128)S(1)}, u32[]{:S(2)}, u32[]{:S(2)}) collective-permute-start(f32[256,256]{1,0:T(8,128)} %get-tuple-element.36.refs_2_), channel_id=1, source_target_pairs={{0,96},{1,97},{2,98},{3,99},{4,100},{5,101},{6,102},{7,103},{8,104... | collective-permute-start | bytes 786440 | tf_op jit(solution)/shard_map/ppermute | solution.py:47
  38.0 0.1 collective-permute-start.11
  38.2 0.7 collective-permute-start.18
  38.8 0.9 select_reduce_fusion
  39.8 5.3 %collective-permute-done.11.refs_8_ = f32[256,256]{1,0:T(8,128)S(1)} collective-permute-done((f32[256,256]{1,0:T(8,128)}, f32[256,256]{1,0:T(8,128)S(1)}, u32[]{:S(2)}, u32[]{:S(2)}) %collective-permute-start.11) | collective-permute-done | bytes 262176 | tf_op jit(solution)/shard_map/ppermute | solution.py:27
  45.1 1.3 collective-permute-start.15
  46.4 1.9 %collective-permute-start.9 = (f32[512,256]{1,0:T(8,128)S(1)}, f32[512,256]{1,0:T(8,128)S(1)}, u32[]{:S(2)}, u32[]{:S(2)}) collective-permute-start(f32[512,256]{1,0:T(8,128)S(1)} %constant_dynamic-update-slice_fusion.refs_4_.refs_7_), channel_id=1, source_target_pairs={{0,96},{32,0},{1,97},{33,1},{2,98},{34,2},{3,99},{35,3},{4,100},{3... | collective-permute-start | bytes 1572872 | tf_op jit(solution)/shard_map/ppermute | solution.py:47
  48.4 2.7 %collective-permute-start.6 = (f32[1024,256]{1,0:T(8,128)}, f32[1024,256]{1,0:T(8,128)}, u32[]{:S(2)}, u32[]{:S(2)}) collective-permute-start(f32[1024,256]{1,0:T(8,128)} %collective-permute-done.4.refs_1_), channel_id=1, source_target_pairs={{0,3},{1,0},{2,1},{3,2},{4,7},{5,4},{6,5},{7,6},{8,11},{9,8},{10,9... | collective-permute-start | bytes 3145736 | tf_op jit(solution)/shard_map/ppermute | solution.py:27
  51.1 0.6 broadcast_add_fusion.2.tab_ref
  51.7 3.8 %shard_map.31 = (bf16[1024,512]{1,0:T(8,128)(2,1)}, bf16[1024,512]{1,0:T(8,128)(2,1)}) custom-call(f32[1024,256]{1,0:T(8,128)} %refs_0_.1, f32[1024,256]{1,0:T(8,128)} %copy-done.1), custom_call_target="tpu_custom_call" | custom-call | flops 1000000 | bytes 4194304 | tf_op jit(solution)/shard_map/pallas_call | solution.py:89
  55.5 3.4 %collective-permute-start.12 = (f32[256,256]{1,0:T(8,128)S(1)}, f32[256,256]{1,0:T(8,128)S(1)}, u32[]{:S(2)}, u32[]{:S(2)}) collective-permute-start(f32[256,256]{1,0:T(8,128)S(1)} %collective-permute-done.11.refs_8_), channel_id=1, source_target_pairs={{0,32},{32,64},{64,96},{1,33},{33,65},{65,97},{2,34},{34,66},{66,9... | collective-permute-start | bytes 786440 | tf_op jit(solution)/shard_map/ppermute | solution.py:47
  58.9 8.9 %shard_map.32.refs_10_.refs_13_ = f32[8,1024,256]{2,1,0:T(8,128)} custom-call(s32[64]{0:T(128)} %broadcast_add_fusion.2.tab_ref, bf16[1024,512]{1,0:T(8,128)(2,1)} %get-tuple-element.34.refs_0_, bf16[1024,512]{1,0:T(8,128)(2,1)} %get-tuple-element.35.refs_1_, f32[256,256]{1,0:T(8,128)} %get-tuple-element.36.refs_2_, f32[256,256]{1,0:T(8,128)} %copy-done.10, ...), custom_call_target="tpu_custom_call" | custom-call | flops 3221225472 | bytes 12582912 | tf_op jit(solution)/shard_map/pallas_call | solution.py:204
  67.7 3.8 %shard_map.29 = (bf16[1024,512]{1,0:T(8,128)(2,1)}, bf16[1024,512]{1,0:T(8,128)(2,1)}) custom-call(f32[1024,256]{1,0:T(8,128)} %copy-done.6, f32[1024,256]{1,0:T(8,128)} %collective-permute-done.4.refs_1_), custom_call_target="tpu_custom_call" | custom-call | flops 1000000 | bytes 4194304 | tf_op jit(solution)/shard_map/pallas_call | solution.py:89
  71.5 3.8 %shard_map.28 = (bf16[1024,512]{1,0:T(8,128)(2,1)}, bf16[1024,512]{1,0:T(8,128)(2,1)}) custom-call(f32[1024,256]{1,0:T(8,128)} %copy-done.5, f32[1024,256]{1,0:T(8,128)} %collective-permute-done.2.refs_1_), custom_call_target="tpu_custom_call" | custom-call | flops 1000000 | bytes 4194304 | tf_op jit(solution)/shard_map/pallas_call | solution.py:89
  75.4 1.3 collective-permute-start.13
  76.7 0.0 collective-permute-done.15.refs_5_.refs_8_
  76.7 0.0 copy-start.4
  76.7 0.7 collective-permute-start.14
  77.4 0.0 collective-permute-done.9.refs_6_.refs_9_
  77.4 1.3 collective-permute-start.10
  78.7 13.3 %shard_map.33.refs_12_ = f32[8,1024,256]{2,1,0:T(8,128)} custom-call(s32[64]{0:T(128)} %broadcast_add_fusion.2.tab_ref, bf16[1024,512]{1,0:T(8,128)(2,1)} %get-tuple-element.25.refs_0_, bf16[1024,512]{1,0:T(8,128)(2,1)} %get-tuple-element.26.refs_1_, bf16[1024,512]{1,0:T(8,128)(2,1)} %get-tuple-element.27.refs_2_, ...), custom_call_target="tpu_custom_call" | custom-call | flops 6442450944 | bytes 12582912 | tf_op jit(solution)/shard_map/pallas_call | solution.py:204
  92.0 0.0 collective-permute-done.6.refs_1_
  92.0 3.8 %shard_map.30 = (bf16[1024,512]{1,0:T(8,128)(2,1)}, bf16[1024,512]{1,0:T(8,128)(2,1)}) custom-call(f32[1024,256]{1,0:T(8,128)} %collective-permute-done.5.refs_0_, f32[1024,256]{1,0:T(8,128)} %collective-permute-done.6.refs_1_), custom_call_target="tpu_custom_call" | custom-call | flops 1000000 | bytes 4194304 | tf_op jit(solution)/shard_map/pallas_call | solution.py:89
  95.8 0.0 collective-permute-done.10.refs_6_.refs_7_
  95.9 0.7 copy-done.13
  96.5 0.1 copy-done.15
  96.6 0.2 copy-done.8
  96.8 16.5 %shard_map.34 = (f32[8,64,512]{2,1,0:T(8,128)}, f32[8,64,512]{2,1,0:T(8,128)}, f32[8,64,512]{2,1,0:T(8,128)}, f32[8,64,512]{2,1,0:T(8,128)}, f32[8,64,512]{2,1,0...) custom-call(s32[64]{0:T(128)} %broadcast_add_fusion.2.tab_ref, ...), custom_call_target="tpu_custom_call" | custom-call | flops 9663676416 | bytes 12582912 | tf_op jit(solution)/shard_map/pallas_call | solution.py:204
  113.3 1.4 collective-permute-start.19
  114.7 2.2 %collective-permute-start.25 = (f32[8,64,512]{2,1,0:T(8,128)}, f32[8,64,512]{2,1,0:T(8,128)S(1)}, u32[]{:S(2)}, u32[]{:S(2)}) collective-permute-start(f32[8,64,512]{2,1,0:T(8,128)} %get-tuple-element.43), channel_id=1, source_target_pairs={{0,12},{1,13},{2,14},{3,15},{4,0},{5,1},{6,2},{7,3},{8,4},{9,5},{1... | collective-permute-start | bytes 3145736 | tf_op jit(solution)/shard_map/ppermute | solution.py:27
  117.0 1.4 collective-permute-start.21
  118.4 11.2 %collective-permute-done.19 = f32[8,64,512]{2,1,0:T(8,128)S(1)} collective-permute-done((f32[8,64,512]{2,1,0:T(8,128)}, f32[8,64,512]{2,1,0:T(8,128)S(1)}, u32[]{:S(2)}, u32[]{:S(2)}) %collective-permute-start.19) | collective-permute-done | bytes 1048608 | tf_op jit(solution)/shard_map/ppermute | solution.py:27
  129.6 1.4 add.262
  131.0 0.1 collective-permute-start.20
  131.1 0.9 collective-permute-start.27
  132.0 0.0 collective-permute-done.25
  132.0 1.4 add.271
  133.5 1.9 %collective-permute-start.26 = (f32[8,64,512]{2,1,0:T(8,128)S(1)}, f32[8,64,512]{2,1,0:T(8,128)S(1)}, u32[]{:S(2)}, u32[]{:S(2)}) collective-permute-start(f32[8,64,512]{2,1,0:T(8,128)S(1)} %add.271), channel_id=1, source_target_pairs={{0,12},{1,13},{2,14},{3,15},{4,0},{5,1},{6,2},{7,3},{8,4},{9,5},{1... | collective-permute-start | bytes 3145736 | tf_op jit(solution)/shard_map/ppermute | solution.py:27
  135.4 5.0 %collective-permute-done.21 = f32[8,64,512]{2,1,0:T(8,128)S(1)} collective-permute-done((f32[8,64,512]{2,1,0:T(8,128)}, f32[8,64,512]{2,1,0:T(8,128)S(1)}, u32[]{:S(2)}, u32[]{:S(2)}) %collective-permute-start.21) | collective-permute-done | bytes 1048608 | tf_op jit(solution)/shard_map/ppermute | solution.py:27
  140.3 5.9 %collective-permute-done.20 = f32[8,64,512]{2,1,0:T(8,128)S(1)} collective-permute-done((f32[8,64,512]{2,1,0:T(8,128)S(1)}, f32[8,64,512]{2,1,0:T(8,128)S(1)}, u32[]{:S(2)}, u32[]{:S(2)}) %collective-permute-start.20) | collective-permute-done | bytes 1048608 | tf_op jit(solution)/shard_map/ppermute | solution.py:27
  146.2 1.6 slice_add_fusion.8
  147.8 0.2 collective-permute-start.24
  148.0 1.4 collective-permute-start.22
  149.3 8.1 %collective-permute-done.27 = f32[8,64,512]{2,1,0:T(8,128)S(1)} collective-permute-done((f32[8,64,512]{2,1,0:T(8,128)}, f32[8,64,512]{2,1,0:T(8,128)S(1)}, u32[]{:S(2)}, u32[]{:S(2)}) %collective-permute-start.27) | collective-permute-done | bytes 1048608 | tf_op jit(solution)/shard_map/ppermute | solution.py:27
  157.5 0.3 slice_add_fusion
  157.8 11.5 %collective-permute-start.31 = (f32[2,64,512]{2,1,0:T(8,128)S(1)}, f32[2,64,512]{2,1,0:T(8,128)S(1)}, u32[]{:S(2)}, u32[]{:S(2)}) collective-permute-start(f32[2,64,512]{2,1,0:T(8,128)S(1)} %get-tuple-element.45), channel_id=1, source_target_pairs={{0,19},{1,16},{2,17},{3,18},{4,23},{5,20},{6,21},{7,22},{8,27},{9,... | collective-permute-start | bytes 786440 | tf_op jit(solution)/shard_map/ppermute | solution.py:27
  169.3 0.3 collective-permute-start.30
  169.6 0.1 collective-permute-start.28
  169.7 2.9 %collective-permute-done.31.refs_7_ = f32[2,64,512]{2,1,0:T(8,128)S(1)} collective-permute-done((f32[2,64,512]{2,1,0:T(8,128)S(1)}, f32[2,64,512]{2,1,0:T(8,128)S(1)}, u32[]{:S(2)}, u32[]{:S(2)}) %collective-permute-start.31) | collective-permute-done | bytes 262176 | tf_op jit(solution)/shard_map/ppermute | solution.py:27
  172.7 4.1 %collective-permute-done.30.refs_6_ = f32[2,64,512]{2,1,0:T(8,128)S(1)} collective-permute-done((f32[2,64,512]{2,1,0:T(8,128)S(1)}, f32[2,64,512]{2,1,0:T(8,128)S(1)}, u32[]{:S(2)}, u32[]{:S(2)}) %collective-permute-start.30) | collective-permute-done | bytes 262176 | tf_op jit(solution)/shard_map/ppermute | solution.py:27
  176.7 2.7 %collective-permute-done.29.refs_5_ = f32[2,64,512]{2,1,0:T(8,128)S(1)} collective-permute-done((f32[2,64,512]{2,1,0:T(8,128)S(1)}, f32[2,64,512]{2,1,0:T(8,128)S(1)}, u32[]{:S(2)}, u32[]{:S(2)}) %collective-permute-start.29) | collective-permute-done | bytes 262176 | tf_op jit(solution)/shard_map/ppermute | solution.py:27
  179.4 2.6 %join.1 = f32[1,2,512,512]{3,2,1,0:T(8,128)} custom-call(s32[3]{0:T(128)S(1)} %copy-done, f32[2,64,512]{2,1,0:T(8,128)S(1)} %get-tuple-element.52.refs_0_, f32[2,64,512]{2,1,0:T(8,128)S(1)} %collective-permute-done.22.refs_1_, f32[2,64,512]{2,1,0:T(8,128)S(1)} %collective-permute-done.23.refs_2_, f32[2,64,512]{2,1,0:T(8,128)S(1)} %collective-permute-done.24.refs_3_, ...), custom_call_target="tpu_custom_call" | custom-call | flops 1000000 | bytes 4194304 | tf_op jit(solution)/shard_map/join/pallas_call | solution.py:242
  (55 shorter events, 0.2 us)
Async XLA Ops:
  0.0 4.2 %collective-permute-start.1 = (f32[1024,256]{1,0:T(8,128)}, f32[1024,256]{1,0:T(8,128)S(1)}, u32[]{:S(2)}, u32[]{:S(2)}) collective-permute-start(f32[1024,256]{1,0:T(8,128)} %refs_0_.1), channel_id=1, source_target_pairs={{0,16},{16,0},{1,17},{17,1},{2,18},{18,2},{3,19},{19,3},{4,20},{20... | collective-permute-start | bytes 3145736 | tf_op jit(solution)/shard_map/ppermute | solution.py:43
  1.4 14.9 %collective-permute-start.3 = (f32[1024,256]{1,0:T(8,128)}, f32[1024,256]{1,0:T(8,128)S(1)}, u32[]{:S(2)}, u32[]{:S(2)}) collective-permute-start(f32[1024,256]{1,0:T(8,128)} %refs_0_.1), channel_id=1, source_target_pairs={{0,3},{1,0},{2,1},{3,2},{4,7},{5,4},{6,5},{7,6},{8,11},{9,8},{10,9... | collective-permute-start | bytes 3145736 | tf_op jit(solution)/shard_map/ppermute | solution.py:27
  4.2 15.4 %collective-permute-start = (f32[1024,256]{1,0:T(8,128)}, f32[1024,256]{1,0:T(8,128)S(1)}, u32[]{:S(2)}, u32[]{:S(2)}) collective-permute-start(f32[1024,256]{1,0:T(8,128)} %refs_0_.1), channel_id=1, source_target_pairs={{0,1},{1,2},{2,3},{3,0},{4,5},{5,6},{6,7},{7,4},{8,9},{9,10},{10,1... | collective-permute-start | bytes 3145736 | tf_op jit(solution)/shard_map/ppermute | solution.py:27
  4.2 3.4 %copy-start.1 = (f32[1024,256]{1,0:T(8,128)}, f32[1024,256]{1,0:T(8,128)S(1)}, u32[]{:S(2)}) copy-start(f32[1024,256]{1,0:T(8,128)S(1)} %collective-permute-done.1.other_ref.refs_1_) | copy-start | bytes 3145732
  4.2 44.1 %collective-permute-start.4 = (f32[1024,256]{1,0:T(8,128)S(1)}, f32[1024,256]{1,0:T(8,128)}, u32[]{:S(2)}, u32[]{:S(2)}) collective-permute-start(f32[1024,256]{1,0:T(8,128)S(1)} %collective-permute-done.1.other_ref.refs_1_), channel_id=1, source_target_pairs={{0,3},{1,0},{2,1},{3,2},{4,7},{5,4},{6,5},{7,6},{8,11},{9,8},{10,9... | collective-permute-start | bytes 3145736 | tf_op jit(solution)/shard_map/ppermute | solution.py:27
  6.9 48.6 %collective-permute-start.2 = (f32[1024,256]{1,0:T(8,128)S(1)}, f32[1024,256]{1,0:T(8,128)}, u32[]{:S(2)}, u32[]{:S(2)}) collective-permute-start(f32[1024,256]{1,0:T(8,128)S(1)} %collective-permute-done.1.other_ref.refs_1_), channel_id=1, source_target_pairs={{0,1},{1,2},{2,3},{3,0},{4,5},{5,6},{6,7},{7,4},{8,9},{9,10},{10,1... | collective-permute-start | bytes 3145736 | tf_op jit(solution)/shard_map/ppermute | solution.py:27
  10.3 23.4 %collective-permute-start.7 = (f32[256,256]{1,0:T(8,128)}, f32[256,256]{1,0:T(8,128)S(1)}, u32[]{:S(2)}, u32[]{:S(2)}) collective-permute-start(f32[256,256]{1,0:T(8,128)} %get-tuple-element.31), channel_id=1, source_target_pairs={{0,1},{1,2},{2,3},{3,0},{4,5},{5,6},{6,7},{7,4},{8,9},{9,10},{10,1... | collective-permute-start | bytes 786440 | tf_op jit(solution)/shard_map/ppermute | solution.py:27
  16.3 28.8 %copy-start.6 = (f32[1024,256]{1,0:T(8,128)}, f32[1024,256]{1,0:T(8,128)S(1)}, u32[]{:S(2)}) copy-start(f32[1024,256]{1,0:T(8,128)S(1)} %collective-permute-done.3.refs_0_) | copy-start | bytes 3145732
  16.3 21.7 %collective-permute-start.8 = (f32[256,256]{1,0:T(8,128)}, f32[256,256]{1,0:T(8,128)S(1)}, u32[]{:S(2)}, u32[]{:S(2)}) collective-permute-start(f32[256,256]{1,0:T(8,128)} %get-tuple-element.32), channel_id=1, source_target_pairs={{0,3},{1,0},{2,1},{3,2},{4,7},{5,4},{6,5},{7,6},{8,11},{9,8},{10,9... | collective-permute-start | bytes 786440 | tf_op jit(solution)/shard_map/ppermute | solution.py:27
  19.6 51.9 %copy-start.5 = (f32[1024,256]{1,0:T(8,128)}, f32[1024,256]{1,0:T(8,128)S(1)}, u32[]{:S(2)}) copy-start(f32[1024,256]{1,0:T(8,128)S(1)} %collective-permute-done.refs_0_) | copy-start | bytes 3145732
  19.6 18.5 %collective-permute-start.16 = (f32[256,256]{1,0:T(8,128)}, f32[256,256]{1,0:T(8,128)S(1)}, u32[]{:S(2)}, u32[]{:S(2)}) collective-permute-start(f32[256,256]{1,0:T(8,128)} %get-tuple-element.36.refs_2_), channel_id=1, source_target_pairs={{0,32},{32,64},{64,96},{1,33},{33,65},{65,97},{2,34},{34,66},{66,9... | collective-permute-start | bytes 786440 | tf_op jit(solution)/shard_map/ppermute | solution.py:47
  33.6 11.4 %collective-permute-start.17 = (f32[256,256]{1,0:T(8,128)}, f32[256,256]{1,0:T(8,128)S(1)}, u32[]{:S(2)}, u32[]{:S(2)}) collective-permute-start(f32[256,256]{1,0:T(8,128)} %get-tuple-element.36.refs_2_), channel_id=1, source_target_pairs={{0,96},{1,97},{2,98},{3,99},{4,100},{5,101},{6,102},{7,103},{8,104... | collective-permute-start | bytes 786440 | tf_op jit(solution)/shard_map/ppermute | solution.py:47
  38.0 7.0 %collective-permute-start.11 = (f32[256,256]{1,0:T(8,128)}, f32[256,256]{1,0:T(8,128)S(1)}, u32[]{:S(2)}, u32[]{:S(2)}) collective-permute-start(f32[256,256]{1,0:T(8,128)} %get-tuple-element.33), channel_id=1, source_target_pairs={{0,2},{1,3},{2,0},{3,1},{4,6},{5,7},{6,4},{7,5},{8,10},{9,11},{10,... | collective-permute-start | bytes 786440 | tf_op jit(solution)/shard_map/ppermute | solution.py:27
  38.1 10.2 %copy-start.10 = (f32[256,256]{1,0:T(8,128)}, f32[256,256]{1,0:T(8,128)S(1)}, u32[]{:S(2)}) copy-start(f32[256,256]{1,0:T(8,128)S(1)} %collective-permute-done.16.refs_3_) | copy-start | bytes 786436
  38.2 8.3 %collective-permute-start.18 = (f32[256,256]{1,0:T(8,128)S(1)}, f32[256,256]{1,0:T(8,128)S(1)}, u32[]{:S(2)}, u32[]{:S(2)}) collective-permute-start(f32[256,256]{1,0:T(8,128)S(1)} %collective-permute-done.16.refs_3_), channel_id=1, source_target_pairs={{32,64},{64,96},{33,65},{65,97},{34,66},{66,98},{35,67},{67,99},{3... | collective-permute-start | bytes 786440 | tf_op jit(solution)/shard_map/ppermute | solution.py:47
  39.8 35.6 %copy-start.2 = (f32[512,256]{1,0:T(8,128)}, f32[512,256]{1,0:T(8,128)S(1)}, u32[]{:S(2)}) copy-start(f32[512,256]{1,0:T(8,128)S(1)} %constant_dynamic-update-slice_fusion.refs_4_.refs_7_) | copy-start | bytes 1572868
  45.1 30.3 %copy-start.9 = (f32[256,256]{1,0:T(8,128)}, f32[256,256]{1,0:T(8,128)S(1)}, u32[]{:S(2)}) copy-start(f32[256,256]{1,0:T(8,128)S(1)} %collective-permute-done.11.refs_8_) | copy-start | bytes 786436
  45.1 47.0 %collective-permute-start.5 = (f32[1024,256]{1,0:T(8,128)S(1)}, f32[1024,256]{1,0:T(8,128)}, u32[]{:S(2)}, u32[]{:S(2)}) collective-permute-start(f32[1024,256]{1,0:T(8,128)S(1)} %collective-permute-done.refs_0_), channel_id=1, source_target_pairs={{0,1},{1,2},{2,3},{3,0},{4,5},{5,6},{6,7},{7,4},{8,9},{9,10},{10,1... | collective-permute-start | bytes 3145736 | tf_op jit(solution)/shard_map/ppermute | solution.py:27
  45.1 6.0 %copy-start.12 = (f32[256,256]{1,0:T(8,128)}, f32[256,256]{1,0:T(8,128)S(1)}, u32[]{:S(2)}) copy-start(f32[256,256]{1,0:T(8,128)S(1)} %collective-permute-done.17.refs_4_) | copy-start | bytes 786436
  45.1 31.6 %collective-permute-start.15 = (f32[512,256]{1,0:T(8,128)S(1)}, f32[512,256]{1,0:T(8,128)S(1)}, u32[]{:S(2)}, u32[]{:S(2)}) collective-permute-start(f32[512,256]{1,0:T(8,128)S(1)} %constant_dynamic-update-slice_fusion.refs_4_.refs_7_), channel_id=1, source_target_pairs={{0,32},{32,64},{64,96},{1,33},{33,65},{65,97},{2,34},{34,66},{66,9... | collective-permute-start | bytes 1572872 | tf_op jit(solution)/shard_map/ppermute | solution.py:47
  46.4 4.7 %copy-start.14 = (f32[256,256]{1,0:T(8,128)}, f32[256,256]{1,0:T(8,128)S(1)}, u32[]{:S(2)}) copy-start(f32[256,256]{1,0:T(8,128)S(1)} %collective-permute-done.18.refs_5_) | copy-start | bytes 786436
  46.4 30.9 %collective-permute-start.9 = (f32[512,256]{1,0:T(8,128)S(1)}, f32[512,256]{1,0:T(8,128)S(1)}, u32[]{:S(2)}, u32[]{:S(2)}) collective-permute-start(f32[512,256]{1,0:T(8,128)S(1)} %constant_dynamic-update-slice_fusion.refs_4_.refs_7_), channel_id=1, source_target_pairs={{0,96},{32,0},{1,97},{33,1},{2,98},{34,2},{3,99},{35,3},{4,100},{3... | collective-permute-start | bytes 1572872 | tf_op jit(solution)/shard_map/ppermute | solution.py:47
  48.4 43.6 %collective-permute-start.6 = (f32[1024,256]{1,0:T(8,128)}, f32[1024,256]{1,0:T(8,128)}, u32[]{:S(2)}, u32[]{:S(2)}) collective-permute-start(f32[1024,256]{1,0:T(8,128)} %collective-permute-done.4.refs_1_), channel_id=1, source_target_pairs={{0,3},{1,0},{2,1},{3,2},{4,7},{5,4},{6,5},{7,6},{8,11},{9,8},{10,9... | collective-permute-start | bytes 3145736 | tf_op jit(solution)/shard_map/ppermute | solution.py:27
  55.5 19.9 %collective-permute-start.12 = (f32[256,256]{1,0:T(8,128)S(1)}, f32[256,256]{1,0:T(8,128)S(1)}, u32[]{:S(2)}, u32[]{:S(2)}) collective-permute-start(f32[256,256]{1,0:T(8,128)S(1)} %collective-permute-done.11.refs_8_), channel_id=1, source_target_pairs={{0,32},{32,64},{64,96},{1,33},{33,65},{65,97},{2,34},{34,66},{66,9... | collective-permute-start | bytes 786440 | tf_op jit(solution)/shard_map/ppermute | solution.py:47
  75.3 20.5 %copy-start.11 = (f32[256,256]{1,0:T(8,128)}, f32[256,256]{1,0:T(8,128)S(1)}, u32[]{:S(2)}) copy-start(f32[256,256]{1,0:T(8,128)S(1)} %collective-permute-done.12.refs_9_) | copy-start | bytes 786436
  75.4 20.5 %collective-permute-start.13 = (f32[256,256]{1,0:T(8,128)S(1)}, f32[256,256]{1,0:T(8,128)S(1)}, u32[]{:S(2)}, u32[]{:S(2)}) collective-permute-start(f32[256,256]{1,0:T(8,128)S(1)} %collective-permute-done.11.refs_8_), channel_id=1, source_target_pairs={{0,96},{1,97},{2,98},{3,99},{4,100},{5,101},{6,102},{7,103},{8,104... | collective-permute-start | bytes 786440 | tf_op jit(solution)/shard_map/ppermute | solution.py:47
  76.7 2.1 %copy-start.4 = (f32[512,256]{1,0:T(8,128)}, f32[512,256]{1,0:T(8,128)S(1)}, u32[]{:S(2)}) copy-start(f32[512,256]{1,0:T(8,128)S(1)} %collective-permute-done.15.refs_5_.refs_8_) | copy-start | bytes 1572868
  76.7 19.1 %collective-permute-start.14 = (f32[256,256]{1,0:T(8,128)S(1)}, f32[256,256]{1,0:T(8,128)S(1)}, u32[]{:S(2)}, u32[]{:S(2)}) collective-permute-start(f32[256,256]{1,0:T(8,128)S(1)} %collective-permute-done.12.refs_9_), channel_id=1, source_target_pairs={{32,64},{64,96},{33,65},{65,97},{34,66},{66,98},{35,67},{67,99},{3... | collective-permute-start | bytes 786440 | tf_op jit(solution)/shard_map/ppermute | solution.py:47
  77.4 1.4 copy-start.3
  77.4 18.4 %collective-permute-start.10 = (f32[512,256]{1,0:T(8,128)S(1)}, f32[512,256]{1,0:T(8,128)S(1)}, u32[]{:S(2)}, u32[]{:S(2)}) collective-permute-start(f32[512,256]{1,0:T(8,128)S(1)} %collective-permute-done.9.refs_6_.refs_9_), channel_id=1, source_target_pairs={{0,96},{96,64},{1,97},{97,65},{2,98},{98,66},{3,99},{99,67},{4,100... | collective-permute-start | bytes 1572872 | tf_op jit(solution)/shard_map/ppermute | solution.py:47
  95.8 0.7 copy-start.13
  95.8 0.8 copy-start.15
  95.9 0.9 copy-start.8
  113.3 44.2 %copy-start.7 = (f32[8,64,512]{2,1,0:T(8,128)S(1)}, f32[8,64,512]{2,1,0:T(8,128)}, u32[]{:S(2)}) copy-start(f32[8,64,512]{2,1,0:T(8,128)} %get-tuple-element.41) | copy-start | bytes 3145732
  113.3 66.1 %copy-start = (s32[3]{0:T(128)S(1)}, s32[3]{0:T(128)}, u32[]{:S(2)}) copy-start(s32[3]{0:T(128)} %pad_add_fusion.at_ref) | copy-start | bytes 40
  113.3 16.2 %collective-permute-start.19 = (f32[8,64,512]{2,1,0:T(8,128)}, f32[8,64,512]{2,1,0:T(8,128)S(1)}, u32[]{:S(2)}, u32[]{:S(2)}) collective-permute-start(f32[8,64,512]{2,1,0:T(8,128)} %get-tuple-element.39), channel_id=1, source_target_pairs={{0,4},{1,5},{2,6},{3,7},{4,8},{5,9},{6,10},{7,11},{8,12},{9,13},{1... | collective-permute-start | bytes 3145736 | tf_op jit(solution)/shard_map/ppermute | solution.py:27
  114.7 17.3 %collective-permute-start.25 = (f32[8,64,512]{2,1,0:T(8,128)}, f32[8,64,512]{2,1,0:T(8,128)S(1)}, u32[]{:S(2)}, u32[]{:S(2)}) collective-permute-start(f32[8,64,512]{2,1,0:T(8,128)} %get-tuple-element.43), channel_id=1, source_target_pairs={{0,12},{1,13},{2,14},{3,15},{4,0},{5,1},{6,2},{7,3},{8,4},{9,5},{1... | collective-permute-start | bytes 3145736 | tf_op jit(solution)/shard_map/ppermute | solution.py:27
  117.0 23.3 %collective-permute-start.21 = (f32[8,64,512]{2,1,0:T(8,128)}, f32[8,64,512]{2,1,0:T(8,128)S(1)}, u32[]{:S(2)}, u32[]{:S(2)}) collective-permute-start(f32[8,64,512]{2,1,0:T(8,128)} %get-tuple-element.40), channel_id=1, source_target_pairs={{0,12},{1,13},{2,14},{3,15},{4,0},{5,1},{6,2},{7,3},{8,4},{9,5},{1... | collective-permute-start | bytes 3145736 | tf_op jit(solution)/shard_map/ppermute | solution.py:27
  131.0 15.2 %collective-permute-start.20 = (f32[8,64,512]{2,1,0:T(8,128)S(1)}, f32[8,64,512]{2,1,0:T(8,128)S(1)}, u32[]{:S(2)}, u32[]{:S(2)}) collective-permute-start(f32[8,64,512]{2,1,0:T(8,128)S(1)} %add.262), channel_id=1, source_target_pairs={{0,4},{1,5},{2,6},{3,7},{4,8},{5,9},{6,10},{7,11},{8,12},{9,13},{1... | collective-permute-start | bytes 3145736 | tf_op jit(solution)/shard_map/ppermute | solution.py:27
  131.1 26.4 %collective-permute-start.27 = (f32[8,64,512]{2,1,0:T(8,128)}, f32[8,64,512]{2,1,0:T(8,128)S(1)}, u32[]{:S(2)}, u32[]{:S(2)}) collective-permute-start(f32[8,64,512]{2,1,0:T(8,128)} %get-tuple-element.44), channel_id=1, source_target_pairs={{0,4},{1,5},{2,6},{3,7},{4,8},{5,9},{6,10},{7,11},{8,12},{9,13},{1... | collective-permute-start | bytes 3145736 | tf_op jit(solution)/shard_map/ppermute | solution.py:27
  133.5 24.0 %collective-permute-start.26 = (f32[8,64,512]{2,1,0:T(8,128)S(1)}, f32[8,64,512]{2,1,0:T(8,128)S(1)}, u32[]{:S(2)}, u32[]{:S(2)}) collective-permute-start(f32[8,64,512]{2,1,0:T(8,128)S(1)} %add.271), channel_id=1, source_target_pairs={{0,12},{1,13},{2,14},{3,15},{4,0},{5,1},{6,2},{7,3},{8,4},{9,5},{1... | collective-permute-start | bytes 3145736 | tf_op jit(solution)/shard_map/ppermute | solution.py:27
  147.8 21.8 %collective-permute-start.24 = (f32[2,64,512]{2,1,0:T(8,128)S(1)}, f32[2,64,512]{2,1,0:T(8,128)S(1)}, u32[]{:S(2)}, u32[]{:S(2)}) collective-permute-start(f32[2,64,512]{2,1,0:T(8,128)S(1)} %get-tuple-element.49), channel_id=1, source_target_pairs={{0,3},{1,0},{2,1},{3,2},{4,7},{5,4},{6,5},{7,6},{8,11},{9,8},{10,9... | collective-permute-start | bytes 786440 | tf_op jit(solution)/shard_map/ppermute | solution.py:27
  148.0 21.6 %collective-permute-start.23 = (f32[2,64,512]{2,1,0:T(8,128)S(1)}, f32[2,64,512]{2,1,0:T(8,128)S(1)}, u32[]{:S(2)}, u32[]{:S(2)}) collective-permute-start(f32[2,64,512]{2,1,0:T(8,128)S(1)} %get-tuple-element.50), channel_id=1, source_target_pairs={{0,2},{1,3},{2,0},{3,1},{4,6},{5,7},{6,4},{7,5},{8,10},{9,11},{10,... | collective-permute-start | bytes 786440 | tf_op jit(solution)/shard_map/ppermute | solution.py:27
  148.0 21.7 %collective-permute-start.22 = (f32[2,64,512]{2,1,0:T(8,128)S(1)}, f32[2,64,512]{2,1,0:T(8,128)S(1)}, u32[]{:S(2)}, u32[]{:S(2)}) collective-permute-start(f32[2,64,512]{2,1,0:T(8,128)S(1)} %get-tuple-element.51), channel_id=1, source_target_pairs={{0,1},{1,2},{2,3},{3,0},{4,5},{5,6},{6,7},{7,4},{8,9},{9,10},{10,1... | collective-permute-start | bytes 786440 | tf_op jit(solution)/shard_map/ppermute | solution.py:27
  157.8 14.8 %collective-permute-start.31 = (f32[2,64,512]{2,1,0:T(8,128)S(1)}, f32[2,64,512]{2,1,0:T(8,128)S(1)}, u32[]{:S(2)}, u32[]{:S(2)}) collective-permute-start(f32[2,64,512]{2,1,0:T(8,128)S(1)} %get-tuple-element.45), channel_id=1, source_target_pairs={{0,19},{1,16},{2,17},{3,18},{4,23},{5,20},{6,21},{7,22},{8,27},{9,... | collective-permute-start | bytes 786440 | tf_op jit(solution)/shard_map/ppermute | solution.py:27
  169.3 7.4 %collective-permute-start.30 = (f32[2,64,512]{2,1,0:T(8,128)S(1)}, f32[2,64,512]{2,1,0:T(8,128)S(1)}, u32[]{:S(2)}, u32[]{:S(2)}) collective-permute-start(f32[2,64,512]{2,1,0:T(8,128)S(1)} %get-tuple-element.46), channel_id=1, source_target_pairs={{0,18},{1,19},{2,16},{3,17},{4,22},{5,23},{6,20},{7,21},{8,26},{9,... | collective-permute-start | bytes 786440 | tf_op jit(solution)/shard_map/ppermute | solution.py:27
  169.6 9.8 %collective-permute-start.29 = (f32[2,64,512]{2,1,0:T(8,128)S(1)}, f32[2,64,512]{2,1,0:T(8,128)S(1)}, u32[]{:S(2)}, u32[]{:S(2)}) collective-permute-start(f32[2,64,512]{2,1,0:T(8,128)S(1)} %get-tuple-element.47), channel_id=1, source_target_pairs={{0,17},{1,18},{2,19},{3,16},{4,21},{5,22},{6,23},{7,20},{8,25},{9,... | collective-permute-start | bytes 786440 | tf_op jit(solution)/shard_map/ppermute | solution.py:27
  169.6 9.8 %collective-permute-start.28 = (f32[2,64,512]{2,1,0:T(8,128)S(1)}, f32[2,64,512]{2,1,0:T(8,128)S(1)}, u32[]{:S(2)}, u32[]{:S(2)}) collective-permute-start(f32[2,64,512]{2,1,0:T(8,128)S(1)} %get-tuple-element.48), channel_id=1, source_target_pairs={{0,16},{1,17},{2,18},{3,19},{4,20},{5,21},{6,22},{7,23},{8,24},{9,... | collective-permute-start | bytes 786440 | tf_op jit(solution)/shard_map/ppermute | solution.py:27

commit v2 on v1

v2 whole, which is shorter than its diff:
```python
import functools

import jax
import jax.numpy as jnp
from jax import lax
from jax.experimental import pallas as pl
from jax.experimental.pallas import tpu as pltpu
from jax.sharding import Mesh
from jax.sharding import PartitionSpec as P


N = 4
VMEM = pltpu.VMEM
SMEM = pltpu.SMEM
GRANT = 16 * 1024 * 1024


def move(value, target):
    pairs = []
    for c in range(2):
        for y in range(N):
            for z in range(N):
                core, gather, scatter = target(c, *((y, z) if c else (z, y)))
                to = (gather, scatter) if c else (scatter, gather)
                pairs.append(((c * N + y) * N + z, (core * N + to[0] % N) * N + to[1] % N))
    return lax.ppermute(value, ("c", "y", "z"), pairs)


def along(value, step):
    return move(value, lambda c, g, r: (c, g + step, r))


def across(value, step):
    return move(value, lambda c, g, r: (c, g, r + step))


def along_other(value, step):
    return move(value, lambda c, g, r: (1 - c, g + step, r))


def swap(value):
    return lax.ppermute(value, "c", [(0, 1), (1, 0)])


def hop(value, pairs):
    return lax.ppermute(value, "x", pairs)


def specs(space, count):
    return [pl.BlockSpec(memory_space=space)] * count


def cut_kernel(q, at_ref, mine_ref, other_ref, *outs):
    for step in range(N):
        part = lax.rem(at_ref[1] + step, N)
        for group, ref in enumerate((mine_ref, other_ref)):
            for block in range(2):
                start = pl.multiple_of((2 * block + at_ref[0]) * N * q + part * q, q)
                row = (2 * group + block) * q
                outs[step][row : row + q, :] = ref[pl.ds(start, q), :]


def cut(at, mine, other):
    rows, inner = mine.shape
    q = rows // 16
    return pl.pallas_call(
        functools.partial(cut_kernel, q),
        out_shape=[jax.ShapeDtypeStruct((4 * q, inner), mine.dtype)] * N,
        in_specs=specs(SMEM, 1) + specs(VMEM, 2),
        out_specs=specs(VMEM, N),
        compiler_params=pltpu.CompilerParams(vmem_limit_bytes=GRANT),
        cost_estimate=pl.CostEstimate(flops=10**6, bytes_accessed=3 * rows * inner * 4, transcendentals=0),
        name="cut",
    )(at, mine, other)


def product_kernel(q, work, carried, last, tab_ref, *refs):
    slabs = []
    for raw, places in work:
        a_refs, refs = refs[: 2 if raw else 1], refs[2 if raw else 1 :]
        slabs.append((raw, a_refs, list(zip(places, refs))))
        refs = refs[len(places) :]
    total_ref, refs = (refs[0], refs[1:]) if carried else (None, refs)
    raws = sum(raw for raw, _ in work)
    if last:
        outs, (acc, b_parts, *a_parts) = refs[:8], refs[8:]
    else:
        acc, a_parts, b_parts = refs[0], list(refs[1 : 1 + raws]), refs[-1]
    wide, side = 4 * q, 4 * q

    def halves(value, place, at):
        inner = value.shape[1]
        high = value.astype(jnp.bfloat16)
        place[at, :inner] = high
        place[at, inner:] = (value - high.astype(jnp.float32)).astype(jnp.bfloat16)

    terms = {}
    used = 0
    for raw, a_refs, pieces in slabs:
        if raw:
            parts = a_parts.pop(0)
            rows = a_refs[0].shape[0]
            for group in range(2):
                halves(a_refs[group][...], parts, slice(group * rows, (group + 1) * rows))
        else:
            parts = a_refs[0]
        for (place, row), ref in pieces:
            at = slice(wide * used, wide * (used + 1))
            halves(ref[row : row + wide, :], b_parts, at)
            terms.setdefault(place, []).append((parts, at))
            used += 1

    for n in range(8):
        columns = slice(n * side, (n + 1) * side)
        for place, pairs in terms.items():
            found = None
            for parts, at in pairs:
                inner = parts.shape[1] // 2
                for left, right in ((0, 0), (0, 1), (1, 0)):
                    one = lax.dot_general(
                        b_parts[at, left * inner : (left + 1) * inner],
                        parts[columns, right * inner : (right + 1) * inner],
                        (((1,), (1,)), ((), ())),
                        preferred_element_type=jnp.float32,
                    )
                    found = one if found is None else found + one
            rows = slice(wide * place, wide * (place + 1))
            if carried and place < 3:
                found = total_ref[n, rows, :] + found
            acc[n, rows, :] = found

    if last:
        for index in range(8):

            def place(k, carry, index=index):
                code = tab_ref[index * 8 + k]
                safe = jnp.maximum(code, 0)
                start = pl.multiple_of((safe // 2) * q, q)
                for b in range(2):
                    tile = acc[(index % 2) * 4 + (safe % 2) * 2 + b, pl.ds(start, q), :]
                    outs[index][k, :, b * side : (b + 1) * side] = jnp.where(code >= 0, tile, 0.0)
                return carry

            lax.fori_loop(0, 8, place, 0, unroll=4)


def product(tab, work, total, last):
    args, form, raws, used = [tab], [], 0, 0
    for rows, slices in work:
        args += list(rows) + [piece for piece, _ in slices.values()]
        raw = len(rows) == 2
        raws, used = raws + raw, used + len(slices)
        form.append((raw, tuple((place, row) for place, (_, row) in slices.items())))
    inner = work[0][1][0][0].shape[1] if 0 in work[0][1] else work[0][1][3][0].shape[1]
    wide = inner
    q, rows = wide // 4, 4 * wide
    if total is not None:
        args.append(total)
    parts = jax.ShapeDtypeStruct((2 * rows, 2 * inner), jnp.bfloat16)
    b_scratch = VMEM((wide * used, 2 * inner), jnp.bfloat16)
    if last:
        out_shape = [jax.ShapeDtypeStruct((8, q, rows // 2), jnp.float32)] * 8
        scratch = [VMEM((8, rows, wide), jnp.float32), b_scratch] + [VMEM(parts.shape, parts.dtype)] * raws
    else:
        out_shape = [jax.ShapeDtypeStruct((8, 3 * wide, wide), jnp.float32)] + [parts] * raws
        scratch = [b_scratch]
    return pl.pallas_call(
        functools.partial(product_kernel, q, form, total is not None, last),
        out_shape=out_shape,
        in_specs=specs(SMEM, 1) + specs(VMEM, len(args) - 1),
        out_specs=specs(VMEM, len(out_shape)),
        scratch_shapes=scratch,
        input_output_aliases={} if last or total is None else {len(args) - 1: 0},
        compiler_params=pltpu.CompilerParams(vmem_limit_bytes=GRANT),
        cost_estimate=pl.CostEstimate(
            flops=24 * rows * rows * inner, bytes_accessed=12 * rows * inner * 4, transcendentals=0
        ),
    )(*args)


def join_kernel(q, at_ref, *refs):
    pieces, out_ref, held = refs[:8], refs[8], refs[9]
    for index in range(8):
        kind = at_ref[0] if index < N else 1 - at_ref[0]
        mine = at_ref[1] if index < N else at_ref[2]
        part = lax.rem(mine + N - index % N, N)
        start = pl.multiple_of((kind * N + part) * q, q)
        for slot in range(2):
            held[slot, pl.ds(start, q), :] = pieces[index][slot]
    for slot in range(2):
        out_ref[0, slot] = held[slot].T


def join(at, pieces):
    _, q, half = pieces[0].shape
    return pl.pallas_call(
        functools.partial(join_kernel, q),
        out_shape=jax.ShapeDtypeStruct((1, 2, half, half), jnp.float32),
        in_specs=specs(SMEM, 1) + specs(VMEM, 8),
        out_specs=pl.BlockSpec(memory_space=VMEM),
        scratch_shapes=[VMEM((2, half, half), jnp.float32)],
        compiler_params=pltpu.CompilerParams(vmem_limit_bytes=GRANT),
        cost_estimate=pl.CostEstimate(flops=10**6, bytes_accessed=16 * half * half, transcendentals=0),
        name="join",
    )(at, *pieces)


def tile_codes(owner, x, c, gather, scatter):
    blocks = owner.shape[0]
    i = lax.broadcasted_iota(jnp.int32, (blocks, blocks), 0)
    j = lax.broadcasted_iota(jnp.int32, (blocks, blocks), 1)
    group = j // 2
    behind = (x - group // 2 + N) % N
    array = jnp.where(behind < 2, behind, 5 - behind) * 2 + jnp.where(group % 2 == c, 0, 1)
    code = jnp.where(j <= i, (array * 2 + j % 2) * 2 + i % 2 + 1, 0)
    index = jnp.arange(64, dtype=jnp.int32)
    far = (scatter + index // 16) % N
    mine = (index // 8) % 2
    near = (gather + (index // 2) % 4) % N
    wanted = jnp.where(c == 0, far * N + near, near * N + far) * 2 + index % 2
    wanted_group = 2 * x + jnp.where(mine == 0, c, 1 - c)
    hit = (owner[None] == wanted[:, None, None]) & ((i // 2)[None] == wanted_group[:, None, None])
    return jnp.sum(jnp.where(hit, code[None], 0), axis=(1, 2)) - 1


def update(panel, owner):
    x, c, y, z = (lax.axis_index(name) for name in "xcyz")
    gather, scatter = jnp.where(c == 0, z, y), jnp.where(c == 0, y, z)
    at = jnp.stack([c, gather, scatter]).astype(jnp.int32)
    tab = tile_codes(owner, x, c, gather, scatter)

    other = swap(panel)
    up, down = [along(panel, 1)], [along(panel, -1)]
    first, *sends = cut(at, panel, other)
    small = [along(sends[s - 1], s) for s in range(1, N)]
    up.append(along(other, 1))
    down.append(along(other, -1))
    beyond = [along(up[0], 1), along(down[1], -1)]

    onward, wrap = [(0, 1), (1, 2), (2, 3)], [(0, 3)]
    both = jnp.concatenate([small[0], small[2]])
    a1, a3 = hop(first, onward), hop(first, wrap)
    b1, b3 = hop(both, onward), hop(both, wrap + [(1, 0)])
    c1, c3 = hop(small[1], onward), hop(small[1], wrap)
    a2, c2 = hop(a1, onward[1:]), hop(c1, onward[1:])
    b2 = hop(b3, wrap + [(3, 2)])

    wide = first.shape[0]
    low, high = [(v, 0) for v in (both, b1, b3, b2)], [(v, wide) for v in (both, b1, b3, b2)]
    zero, far = [(v, 0) for v in (first, a1, a3, a2)], [(v, 0) for v in (small[1], c1, c3, c2)]
    three, four = range(3), range(4)
    total, own_parts = product(tab, [((panel, other), dict(zip(three, zero)))], None, False)
    total, up_parts, down_parts = product(
        tab, [(up, dict(zip(three, low))), (down, dict(zip(three, high)))], total, False
    )
    outs = product(
        tab,
        [
            (beyond, dict(zip(four, far))),
            ((own_parts,), {3: zero[3]}),
            ((up_parts,), {3: low[3]}),
            ((down_parts,), {3: high[3]}),
        ],
        total,
        True,
    )
    own0, own1, near0, near1, far0, far1, last0, last1 = outs


    up_far, down_far = across(far0, 1), across(far1, -1)
    up_near, down_near = across(near1, 1), across(last0, -1)
    up_sum = across(near0 + up_far, 1)
    down_sum = across(last1 + down_far, -1)
    found, passed = [], []
    for s in range(N):
        part = slice(2 * s, 2 * s + 2)
        mine = own0[part] + up_sum[part] + down_near[part]
        theirs = own1[part] + down_sum[part] + up_near[part]
        found.append(mine if s == 0 else along(mine, s))
        passed.append(along_other(theirs, s))
    return join(at, found + passed)


def solution(mesh):
    grid = Mesh(mesh.devices.reshape(N, 2, N, N), ("x", "c", "y", "z"))
    return jax.shard_map(
        update,
        mesh=grid,
        in_specs=(P(("x", "c"), ("y", "z")), P()),
        out_specs=P(("x", "c"), ("y", "z"), None, None),
        check_vma=False,
    )
```

time: 183 us -> 151 us (0.83)
  Pallas kernels: 59 us -> 23 us
  starting transfers between devices: 52.4 us -> 79.4 us
  waiting for transfers between devices: 62.1 us -> 42 us
  other arithmetic: 7.03 us -> 1.48 us
  local copies, waits for them, and re-layouts: 1.02 us -> 3.17 us
    pallas_call x7 -> x3, Pallas kernels: 53.8 us -> 18.8 us  [product(): pl.pallas_call(functools.partial(product_kernel, q, form, total is not No...]
    ppermute x22, waiting for transfers between devices: 62.1 us -> 38.2 us  [move(): return lax.ppermute(value, ('c', 'y', 'z'), pairs)]
    ppermute x22, starting transfers between devices: 32.9 us -> 53.2 us  [move(): return lax.ppermute(value, ('c', 'y', 'z'), pairs)]
    ppermute x9, starting transfers between devices: 18.1 us -> 24.8 us  [hop(): return lax.ppermute(value, 'x', pairs)]
    ppermute x9, waiting for transfers between devices: 0.02 us -> 3.87 us  [hop(): return lax.ppermute(value, 'x', pairs)]
  transfers between devices with their start and end apart: 32 -> 32, of which waited for: 10 -> 11; matrix products, arithmetic and copies ran while one was open for 4% -> 2% of each run, Pallas kernels for 22% -> 8%
where the time goes in v2:
time: 151 us; the launch traced here: 149 us
  starting transfers between devices  79.4 us (53%)
  waiting for transfers between devices  42 us (28%)
  Pallas kernels  23 us (15%)
  local copies, waits for them, and re-layouts  3.17 us (2%)
    ppermute x22, starting transfers between devices, move(): return lax.ppermute(value, ('c', 'y', 'z'), pairs)  53.2 us
    ppermute x22, waiting for transfers between devices, move(): return lax.ppermute(value, ('c', 'y', 'z'), pairs)  38.2 us
    ppermute x9, starting transfers between devices, hop(): return lax.ppermute(value, 'x', pairs)  24.8 us
    pallas_call x3, Pallas kernels, product(): pl.pallas_call(functools.partial(product_kernel, q, form, total is not No...  18.8 us
    ppermute x9, waiting for transfers between devices, hop(): return lax.ppermute(value, 'x', pairs)  3.87 us
  transfers between devices with their start and end apart: 32, of which 11 were waited for; matrix products, arithmetic and copies ran while one was open for 2% of the time, Pallas kernels for 8%

profile of v2, /device:TPU:1, one launch (start us, length us, event | category | flops | bytes accessed | tf_op | source)
XLA Modules:
  0.0 149.3 jit_solution(2871310194110293696)
XLA Ops:
  0.0 1.4 collective-permute-start.2
  1.4 1.4 collective-permute-start
  2.8 1.4 collective-permute-start.17
  4.2 0.0 collective-permute-done.2.other_ref.refs_1_
  4.3 2.5 %collective-permute-start.3 = (f32[1024,256]{1,0:T(8,128)S(1)}, f32[1024,256]{1,0:T(8,128)}, u32[]{:S(2)}, u32[]{:S(2)}) collective-permute-start(f32[1024,256]{1,0:T(8,128)S(1)} %collective-permute-done.2.other_ref.refs_1_), channel_id=1, source_target_pairs={{0,3},{1,0},{2,1},{3,2},{4,7},{5,4},{6,5},{7,6},{8,11},{9,8},{10,9... | collective-permute-start | bytes 3145736 | tf_op jit(solution)/shard_map/ppermute | solution.py:26
  6.7 0.1 pad_add_fusion.at_ref
  6.8 1.2 copy-done
  8.0 1.6 %cut.1 = (f32[256,256]{1,0:T(8,128)}, f32[256,256]{1,0:T(8,128)}, f32[256,256]{1,0:T(8,128)}, f32[256,256]{1,0:T(8,128)}) custom-call(s32[3]{0:T(128)S(1)} %pad_add_fusion.at_ref, f32[1024,256]{1,0:T(8,128)S(1)} %copy-done, f32[1024,256]{1,0:T(8,128)S(1)} %collective-permute-done.2.other_ref.refs_1_), custom_call_target="tpu_custom_call" | custom-call | flops 1000000 | bytes 3145728 | tf_op jit(solution)/shard_map/cut/pallas_call | solution.py:66
  9.6 3.8 %collective-permute-start.9 = (f32[256,256]{1,0:T(8,128)}, f32[256,256]{1,0:T(8,128)}, u32[]{:S(2)}, u32[]{:S(2)}) collective-permute-start(f32[256,256]{1,0:T(8,128)} %get-tuple-element.23.refs_2_), channel_id=1, source_target_pairs={{0,32},{32,64},{64,96},{1,33},{33,65},{65,97},{2,34},{34,66},{66,9... | collective-permute-start | bytes 786440 | tf_op jit(solution)/shard_map/ppermute | solution.py:46
  13.5 0.0 collective-permute-start.13
  13.5 3.5 %collective-permute-done.refs_0_ = f32[1024,256]{1,0:T(8,128)S(1)} collective-permute-done((f32[1024,256]{1,0:T(8,128)}, f32[1024,256]{1,0:T(8,128)S(1)}, u32[]{:S(2)}, u32[]{:S(2)}) %collective-permute-start) | collective-permute-done | bytes 1048608 | tf_op jit(solution)/shard_map/ppermute | solution.py:26
  16.9 1.6 %collective-permute-start.14 = (f32[256,256]{1,0:T(8,128)}, f32[256,256]{1,0:T(8,128)}, u32[]{:S(2)}, u32[]{:S(2)}) collective-permute-start(f32[256,256]{1,0:T(8,128)} %get-tuple-element.26), channel_id=1, source_target_pairs={{0,3},{1,0},{2,1},{3,2},{4,7},{5,4},{6,5},{7,6},{8,11},{9,8},{10,9... | collective-permute-start | bytes 786440 | tf_op jit(solution)/shard_map/ppermute | solution.py:26
  18.5 1.2 collective-permute-start.5
  19.7 0.1 broadcast_select_fusion
  19.8 0.2 select_reduce_fusion
  20.0 0.0 collective-permute-done.9.refs_3_
  20.0 4.4 %collective-permute-start.10 = (f32[256,256]{1,0:T(8,128)}, f32[256,256]{1,0:T(8,128)S(1)}, u32[]{:S(2)}, u32[]{:S(2)}) collective-permute-start(f32[256,256]{1,0:T(8,128)} %get-tuple-element.23.refs_2_), channel_id=1, source_target_pairs={{0,96},{1,97},{2,98},{3,99},{4,100},{5,101},{6,102},{7,103},{8,104... | collective-permute-start | bytes 786440 | tf_op jit(solution)/shard_map/ppermute | solution.py:46
  24.4 0.0 collective-permute-done.13
  24.4 0.6 collective-permute-start.12
  25.0 0.7 collective-permute-done.5.refs_2_
  25.7 3.1 %collective-permute-start.6 = (f32[256,256]{1,0:T(8,128)S(1)}, f32[256,256]{1,0:T(8,128)S(1)}, u32[]{:S(2)}, u32[]{:S(2)}) collective-permute-start(f32[256,256]{1,0:T(8,128)S(1)} %collective-permute-done.5.refs_2_), channel_id=1, source_target_pairs={{0,32},{32,64},{64,96},{1,33},{33,65},{65,97},{2,34},{34,66},{66,9... | collective-permute-start | bytes 786440 | tf_op jit(solution)/shard_map/ppermute | solution.py:46
  28.9 2.2 %collective-permute-done.14 = f32[256,256]{1,0:T(8,128)} collective-permute-done((f32[256,256]{1,0:T(8,128)}, f32[256,256]{1,0:T(8,128)}, u32[]{:S(2)}, u32[]{:S(2)}) %collective-permute-start.14) | collective-permute-done | bytes 262176 | tf_op jit(solution)/shard_map/ppermute | solution.py:26
  31.1 0.7 collective-permute-start.11
  31.8 1.0 constant_dynamic-update-slice_fusion.1
  32.8 1.0 constant_dynamic-update-slice_fusion.refs_2_.refs_7_
  33.7 7.9 %collective-permute-start.1 = (f32[1024,256]{1,0:T(8,128)S(1)}, f32[1024,256]{1,0:T(8,128)S(1)}, u32[]{:S(2)}, u32[]{:S(2)}) collective-permute-start(f32[1024,256]{1,0:T(8,128)S(1)} %collective-permute-done.refs_0_), channel_id=1, source_target_pairs={{0,1},{1,2},{2,3},{3,0},{4,5},{5,6},{6,7},{7,4},{8,9},{9,10},{10,1... | collective-permute-start | bytes 3145736 | tf_op jit(solution)/shard_map/ppermute | solution.py:26
  41.7 0.0 collective-permute-done.6.refs_3_
  41.7 3.2 %collective-permute-start.16 = (f32[512,256]{1,0:T(8,128)S(1)}, f32[512,256]{1,0:T(8,128)S(1)}, u32[]{:S(2)}, u32[]{:S(2)}) collective-permute-start(f32[512,256]{1,0:T(8,128)S(1)} %constant_dynamic-update-slice_fusion.refs_2_.refs_7_), channel_id=1, source_target_pairs={{0,96},{32,0},{1,97},{33,1},{2,98},{34,2},{3,99},{35,3},{4,100},{3... | collective-permute-start | bytes 1572872 | tf_op jit(solution)/shard_map/ppermute | solution.py:46
  44.8 3.5 %collective-permute-start.15 = (f32[512,256]{1,0:T(8,128)S(1)}, f32[512,256]{1,0:T(8,128)S(1)}, u32[]{:S(2)}, u32[]{:S(2)}) collective-permute-start(f32[512,256]{1,0:T(8,128)S(1)} %constant_dynamic-update-slice_fusion.refs_2_.refs_7_), channel_id=1, source_target_pairs={{0,32},{32,64},{64,96},{1,33},{33,65},{65,97},{2,34},{34,66},{66,9... | collective-permute-start | bytes 1572872 | tf_op jit(solution)/shard_map/ppermute | solution.py:46
  48.3 0.0 collective-permute-done.3.refs_6_
  48.3 3.0 %collective-permute-start.4 = (f32[1024,256]{1,0:T(8,128)}, f32[1024,256]{1,0:T(8,128)S(1)}, u32[]{:S(2)}, u32[]{:S(2)}) collective-permute-start(f32[1024,256]{1,0:T(8,128)} %collective-permute-done.3.refs_6_), channel_id=1, source_target_pairs={{0,3},{1,0},{2,1},{3,2},{4,7},{5,4},{6,5},{7,6},{8,11},{9,8},{10,9... | collective-permute-start | bytes 3145736 | tf_op jit(solution)/shard_map/ppermute | solution.py:26
  51.4 3.7 %shard_map.28 = (f32[8,768,256]{2,1,0:T(8,128)S(1)}, bf16[2048,512]{1,0:T(8,128)(2,1)S(1)}) custom-call(s32[64]{0:T(128)S(1)} %broadcast_add_fusion.2.tab_ref, f32[1024,256]{1,0:T(8,128)S(1)} %copy-done.1, f32[1024,256]{1,0:T(8,128)S(1)} %collective-permute-done.2.other_ref.refs_1_, f32[256,256]{1,0:T(8,128)} %get-tuple-element.23.refs_2_, ...), custom_call_target="tpu_custom_call" | custom-call | flops 6442450944 | bytes 12582912 | tf_op jit(solution)/shard_map/pallas_call | solution.py:167
  55.1 0.5 collective-permute-done.16.refs_4_.refs_9_
  55.5 3.4 %collective-permute-start.7 = (f32[256,256]{1,0:T(8,128)S(1)}, f32[256,256]{1,0:T(8,128)S(1)}, u32[]{:S(2)}, u32[]{:S(2)}) collective-permute-start(f32[256,256]{1,0:T(8,128)S(1)} %collective-permute-done.5.refs_2_), channel_id=1, source_target_pairs={{0,96},{1,97},{2,98},{3,99},{4,100},{5,101},{6,102},{7,103},{8,104... | collective-permute-start | bytes 786440 | tf_op jit(solution)/shard_map/ppermute | solution.py:46
  58.9 0.0 collective-permute-done.15.refs_3_.refs_8_
  58.9 0.7 collective-permute-start.8
  59.6 2.1 %collective-permute-start.18 = (f32[512,256]{1,0:T(8,128)S(1)}, f32[512,256]{1,0:T(8,128)S(1)}, u32[]{:S(2)}, u32[]{:S(2)}) collective-permute-start(f32[512,256]{1,0:T(8,128)S(1)} %collective-permute-done.16.refs_4_.refs_9_), channel_id=1, source_target_pairs={{0,96},{96,64},{1,97},{97,65},{2,98},{98,66},{3,99},{99,67},{4,100... | collective-permute-start | bytes 1572872 | tf_op jit(solution)/shard_map/ppermute | solution.py:46
  61.7 7.3 %shard_map.29 = (f32[8,768,256]{2,1,0:T(8,128)S(1)}, bf16[2048,512]{1,0:T(8,128)(2,1)S(1)}, bf16[2048,512]{1,0:T(8,128)(2,1)S(1)}) custom-call(s32[64]{0:T(128)S(1)} %broadcast_add_fusion.2.tab_ref, f32[1024,256]{1,0:T(8,128)S(1)} %collective-permute-done.refs_0_, f32[1024,256]{1,0:T(8,128)S(1)} %collective-permute-done.12.refs_1_, ...), custom_call_target="tpu_custom_call", output_to_operand_aliasing={{0}: (11, {})} | custom-call | flops 6442450944 | bytes 12582912 | tf_op jit(solution)/shard_map/pallas_call | solution.py:167
  69.0 0.0 collective-permute-done.7.refs_4_
  69.0 0.0 collective-permute-done.8.refs_5_
  69.0 3.4 %collective-permute-done.18.refs_9_.refs_11_ = f32[512,256]{1,0:T(8,128)S(1)} collective-permute-done((f32[512,256]{1,0:T(8,128)S(1)}, f32[512,256]{1,0:T(8,128)S(1)}, u32[]{:S(2)}, u32[]{:S(2)}) %collective-permute-start.18) | collective-permute-done | bytes 524320 | tf_op jit(solution)/shard_map/ppermute | solution.py:46
  72.4 7.8 %shard_map.30 = (f32[8,64,512]{2,1,0:T(8,128)S(1)}, f32[8,64,512]{2,1,0:T(8,128)S(1)}, f32[8,64,512]{2,1,0:T(8,128)S(1)}, f32[8,64,512]{2,1,0:T(8,128)S(1)}, f32...) custom-call(s32[64]{0:T(128)S(1)} %broadcast_add_fusion.2.tab_ref, ...), custom_call_target="tpu_custom_call" | custom-call | flops 6442450944 | bytes 12582912 | tf_op jit(solution)/shard_map/pallas_call | solution.py:167
  80.2 7.2 %collective-permute-start.25 = (f32[8,64,512]{2,1,0:T(8,128)S(1)}, f32[8,64,512]{2,1,0:T(8,128)S(1)}, u32[]{:S(2)}, u32[]{:S(2)}) collective-permute-start(f32[8,64,512]{2,1,0:T(8,128)S(1)} %get-tuple-element.37), channel_id=1, source_target_pairs={{0,12},{1,13},{2,14},{3,15},{4,0},{5,1},{6,2},{7,3},{8,4},{9,5},{1... | collective-permute-start | bytes 3145736 | tf_op jit(solution)/shard_map/ppermute | solution.py:26
  87.4 0.6 collective-permute-start.27
  88.0 11.1 %collective-permute-done.25 = f32[8,64,512]{2,1,0:T(8,128)S(1)} collective-permute-done((f32[8,64,512]{2,1,0:T(8,128)S(1)}, f32[8,64,512]{2,1,0:T(8,128)S(1)}, u32[]{:S(2)}, u32[]{:S(2)}) %collective-permute-start.25) | collective-permute-done | bytes 1048608 | tf_op jit(solution)/shard_map/ppermute | solution.py:26
  99.1 0.2 add.271
  99.4 3.5 %collective-permute-start.26 = (f32[8,64,512]{2,1,0:T(8,128)S(1)}, f32[8,64,512]{2,1,0:T(8,128)S(1)}, u32[]{:S(2)}, u32[]{:S(2)}) collective-permute-start(f32[8,64,512]{2,1,0:T(8,128)S(1)} %add.271), channel_id=1, source_target_pairs={{0,12},{1,13},{2,14},{3,15},{4,0},{5,1},{6,2},{7,3},{8,4},{9,5},{1... | collective-permute-start | bytes 3145736 | tf_op jit(solution)/shard_map/ppermute | solution.py:26
  102.8 0.1 collective-permute-start.21
  102.9 0.2 add.262
  103.1 1.7 %collective-permute-start.20 = (f32[8,64,512]{2,1,0:T(8,128)S(1)}, f32[8,64,512]{2,1,0:T(8,128)S(1)}, u32[]{:S(2)}, u32[]{:S(2)}) collective-permute-start(f32[8,64,512]{2,1,0:T(8,128)S(1)} %add.262), channel_id=1, source_target_pairs={{0,4},{1,5},{2,6},{3,7},{4,8},{5,9},{6,10},{7,11},{8,12},{9,13},{1... | collective-permute-start | bytes 3145736 | tf_op jit(solution)/shard_map/ppermute | solution.py:26
  104.8 9.0 %collective-permute-done.27 = f32[8,64,512]{2,1,0:T(8,128)S(1)} collective-permute-done((f32[8,64,512]{2,1,0:T(8,128)S(1)}, f32[8,64,512]{2,1,0:T(8,128)S(1)}, u32[]{:S(2)}, u32[]{:S(2)}) %collective-permute-start.27) | collective-permute-done | bytes 1048608 | tf_op jit(solution)/shard_map/ppermute | solution.py:26
  113.8 0.8 collective-permute-done.26
  114.6 0.3 slice_add_fusion
  114.9 5.3 %collective-permute-start.28 = (f32[2,64,512]{2,1,0:T(8,128)S(1)}, f32[2,64,512]{2,1,0:T(8,128)S(1)}, u32[]{:S(2)}, u32[]{:S(2)}) collective-permute-start(f32[2,64,512]{2,1,0:T(8,128)S(1)} %get-tuple-element.42), channel_id=1, source_target_pairs={{0,16},{1,17},{2,18},{3,19},{4,20},{5,21},{6,22},{7,23},{8,24},{9,... | collective-permute-start | bytes 786440 | tf_op jit(solution)/shard_map/ppermute | solution.py:26
  120.2 1.7 %collective-permute-start.29 = (f32[2,64,512]{2,1,0:T(8,128)S(1)}, f32[2,64,512]{2,1,0:T(8,128)S(1)}, u32[]{:S(2)}, u32[]{:S(2)}) collective-permute-start(f32[2,64,512]{2,1,0:T(8,128)S(1)} %get-tuple-element.41), channel_id=1, source_target_pairs={{0,17},{1,18},{2,19},{3,16},{4,21},{5,22},{6,23},{7,20},{8,25},{9,... | collective-permute-start | bytes 786440 | tf_op jit(solution)/shard_map/ppermute | solution.py:26
  121.9 3.9 %collective-permute-done.21 = f32[8,64,512]{2,1,0:T(8,128)S(1)} collective-permute-done((f32[8,64,512]{2,1,0:T(8,128)S(1)}, f32[8,64,512]{2,1,0:T(8,128)S(1)}, u32[]{:S(2)}, u32[]{:S(2)}) %collective-permute-start.21) | collective-permute-done | bytes 1048608 | tf_op jit(solution)/shard_map/ppermute | solution.py:26
  125.8 10.3 %collective-permute-start.31 = (f32[2,64,512]{2,1,0:T(8,128)S(1)}, f32[2,64,512]{2,1,0:T(8,128)S(1)}, u32[]{:S(2)}, u32[]{:S(2)}) collective-permute-start(f32[2,64,512]{2,1,0:T(8,128)S(1)} %get-tuple-element.39), channel_id=1, source_target_pairs={{0,19},{1,16},{2,17},{3,18},{4,23},{5,20},{6,21},{7,22},{8,27},{9,... | collective-permute-start | bytes 786440 | tf_op jit(solution)/shard_map/ppermute | solution.py:26
  136.1 0.3 slice_add_fusion.8
  136.5 0.4 collective-permute-start.22
  136.9 0.9 collective-permute-start.23
  137.8 2.0 %collective-permute-start.24 = (f32[2,64,512]{2,1,0:T(8,128)S(1)}, f32[2,64,512]{2,1,0:T(8,128)S(1)}, u32[]{:S(2)}, u32[]{:S(2)}) collective-permute-start(f32[2,64,512]{2,1,0:T(8,128)S(1)} %get-tuple-element.43), channel_id=1, source_target_pairs={{0,3},{1,0},{2,1},{3,2},{4,7},{5,4},{6,5},{7,6},{8,11},{9,8},{10,9... | collective-permute-start | bytes 786440 | tf_op jit(solution)/shard_map/ppermute | solution.py:26
  139.8 6.3 %collective-permute-done.22.refs_1_ = f32[2,64,512]{2,1,0:T(8,128)S(1)} collective-permute-done((f32[2,64,512]{2,1,0:T(8,128)S(1)}, f32[2,64,512]{2,1,0:T(8,128)S(1)}, u32[]{:S(2)}, u32[]{:S(2)}) %collective-permute-start.22) | collective-permute-done | bytes 262176 | tf_op jit(solution)/shard_map/ppermute | solution.py:26
  146.1 0.6 collective-permute-done.24.refs_3_
  146.7 2.6 %join.1 = f32[1,2,512,512]{3,2,1,0:T(8,128)} custom-call(s32[3]{0:T(128)S(1)} %pad_add_fusion.at_ref, f32[2,64,512]{2,1,0:T(8,128)S(1)} %get-tuple-element.46.refs_0_, f32[2,64,512]{2,1,0:T(8,128)S(1)} %collective-permute-done.22.refs_1_, f32[2,64,512]{2,1,0:T(8,128)S(1)} %collective-permute-done.23.refs_2_, ...), custom_call_target="tpu_custom_call" | custom-call | flops 1000000 | bytes 4194304 | tf_op jit(solution)/shard_map/join/pallas_call | solution.py:196
  (25 shorter events, 0.1 us)
Async XLA Ops:
  0.0 19.8 %copy-start.2 = (s32[16,16]{1,0:T(8,128)S(1)}, s32[16,16]{1,0:T(8,128)}, u32[]{:S(2)}) copy-start(s32[16,16]{1,0:T(8,128)} %param.3) | copy-start | bytes 3076
  0.0 4.2 %collective-permute-start.2 = (f32[1024,256]{1,0:T(8,128)}, f32[1024,256]{1,0:T(8,128)S(1)}, u32[]{:S(2)}, u32[]{:S(2)}) collective-permute-start(f32[1024,256]{1,0:T(8,128)} %refs_0_.1), channel_id=1, source_target_pairs={{0,16},{16,0},{1,17},{17,1},{2,18},{18,2},{3,19},{19,3},{4,20},{20... | collective-permute-start | bytes 3145736 | tf_op jit(solution)/shard_map/ppermute | solution.py:42
  1.4 15.5 %collective-permute-start = (f32[1024,256]{1,0:T(8,128)}, f32[1024,256]{1,0:T(8,128)S(1)}, u32[]{:S(2)}, u32[]{:S(2)}) collective-permute-start(f32[1024,256]{1,0:T(8,128)} %refs_0_.1), channel_id=1, source_target_pairs={{0,1},{1,2},{2,3},{3,0},{4,5},{5,6},{6,7},{7,4},{8,9},{9,10},{10,1... | collective-permute-start | bytes 3145736 | tf_op jit(solution)/shard_map/ppermute | solution.py:26
  2.8 15.7 %collective-permute-start.17 = (f32[1024,256]{1,0:T(8,128)}, f32[1024,256]{1,0:T(8,128)}, u32[]{:S(2)}, u32[]{:S(2)}) collective-permute-start(f32[1024,256]{1,0:T(8,128)} %refs_0_.1), channel_id=1, source_target_pairs={{0,3},{1,0},{2,1},{3,2},{4,7},{5,4},{6,5},{7,6},{8,11},{9,8},{10,9... | collective-permute-start | bytes 3145736 | tf_op jit(solution)/shard_map/ppermute | solution.py:26
  4.3 44.1 %collective-permute-start.3 = (f32[1024,256]{1,0:T(8,128)S(1)}, f32[1024,256]{1,0:T(8,128)}, u32[]{:S(2)}, u32[]{:S(2)}) collective-permute-start(f32[1024,256]{1,0:T(8,128)S(1)} %collective-permute-done.2.other_ref.refs_1_), channel_id=1, source_target_pairs={{0,3},{1,0},{2,1},{3,2},{4,7},{5,4},{6,5},{7,6},{8,11},{9,8},{10,9... | collective-permute-start | bytes 3145736 | tf_op jit(solution)/shard_map/ppermute | solution.py:26
  6.8 1.2 copy-start
  8.0 43.3 %copy-start.1 = (f32[1024,256]{1,0:T(8,128)S(1)}, f32[1024,256]{1,0:T(8,128)}, u32[]{:S(2)}) copy-start(f32[1024,256]{1,0:T(8,128)} %refs_0_.1) | copy-start | bytes 3145732
  9.6 10.3 %collective-permute-start.9 = (f32[256,256]{1,0:T(8,128)}, f32[256,256]{1,0:T(8,128)}, u32[]{:S(2)}, u32[]{:S(2)}) collective-permute-start(f32[256,256]{1,0:T(8,128)} %get-tuple-element.23.refs_2_), channel_id=1, source_target_pairs={{0,32},{32,64},{64,96},{1,33},{33,65},{65,97},{2,34},{34,66},{66,9... | collective-permute-start | bytes 786440 | tf_op jit(solution)/shard_map/ppermute | solution.py:46
  13.5 10.9 %collective-permute-start.13 = (f32[256,256]{1,0:T(8,128)}, f32[256,256]{1,0:T(8,128)}, u32[]{:S(2)}, u32[]{:S(2)}) collective-permute-start(f32[256,256]{1,0:T(8,128)} %get-tuple-element.25), channel_id=1, source_target_pairs={{0,1},{1,2},{2,3},{3,0},{4,5},{5,6},{6,7},{7,4},{8,9},{9,10},{10,1... | collective-permute-start | bytes 786440 | tf_op jit(solution)/shard_map/ppermute | solution.py:26
  16.9 14.2 %collective-permute-start.14 = (f32[256,256]{1,0:T(8,128)}, f32[256,256]{1,0:T(8,128)}, u32[]{:S(2)}, u32[]{:S(2)}) collective-permute-start(f32[256,256]{1,0:T(8,128)} %get-tuple-element.26), channel_id=1, source_target_pairs={{0,3},{1,0},{2,1},{3,2},{4,7},{5,4},{6,5},{7,6},{8,11},{9,8},{10,9... | collective-permute-start | bytes 786440 | tf_op jit(solution)/shard_map/ppermute | solution.py:26
  18.5 7.2 %collective-permute-start.5 = (f32[256,256]{1,0:T(8,128)}, f32[256,256]{1,0:T(8,128)S(1)}, u32[]{:S(2)}, u32[]{:S(2)}) collective-permute-start(f32[256,256]{1,0:T(8,128)} %get-tuple-element.22), channel_id=1, source_target_pairs={{0,2},{1,3},{2,0},{3,1},{4,6},{5,7},{6,4},{7,5},{8,10},{9,11},{10,... | collective-permute-start | bytes 786440 | tf_op jit(solution)/shard_map/ppermute | solution.py:26
  20.0 13.7 %collective-permute-start.10 = (f32[256,256]{1,0:T(8,128)}, f32[256,256]{1,0:T(8,128)S(1)}, u32[]{:S(2)}, u32[]{:S(2)}) collective-permute-start(f32[256,256]{1,0:T(8,128)} %get-tuple-element.23.refs_2_), channel_id=1, source_target_pairs={{0,96},{1,97},{2,98},{3,99},{4,100},{5,101},{6,102},{7,103},{8,104... | collective-permute-start | bytes 786440 | tf_op jit(solution)/shard_map/ppermute | solution.py:46
  24.4 35.2 %collective-permute-start.12 = (f32[1024,256]{1,0:T(8,128)S(1)}, f32[1024,256]{1,0:T(8,128)S(1)}, u32[]{:S(2)}, u32[]{:S(2)}) collective-permute-start(f32[1024,256]{1,0:T(8,128)S(1)} %collective-permute-done.2.other_ref.refs_1_), channel_id=1, source_target_pairs={{0,1},{1,2},{2,3},{3,0},{4,5},{5,6},{6,7},{7,4},{8,9},{9,10},{10,1... | collective-permute-start | bytes 3145736 | tf_op jit(solution)/shard_map/ppermute | solution.py:26
  25.7 16.0 %collective-permute-start.6 = (f32[256,256]{1,0:T(8,128)S(1)}, f32[256,256]{1,0:T(8,128)S(1)}, u32[]{:S(2)}, u32[]{:S(2)}) collective-permute-start(f32[256,256]{1,0:T(8,128)S(1)} %collective-permute-done.5.refs_2_), channel_id=1, source_target_pairs={{0,32},{32,64},{64,96},{1,33},{33,65},{65,97},{2,34},{34,66},{66,9... | collective-permute-start | bytes 786440 | tf_op jit(solution)/shard_map/ppermute | solution.py:46
  31.1 13.7 %collective-permute-start.11 = (f32[256,256]{1,0:T(8,128)}, f32[256,256]{1,0:T(8,128)S(1)}, u32[]{:S(2)}, u32[]{:S(2)}) collective-permute-start(f32[256,256]{1,0:T(8,128)} %collective-permute-done.9.refs_3_), channel_id=1, source_target_pairs={{32,64},{64,96},{33,65},{65,97},{34,66},{66,98},{35,67},{67,99},{3... | collective-permute-start | bytes 786440 | tf_op jit(solution)/shard_map/ppermute | solution.py:46
  33.7 35.3 %collective-permute-start.1 = (f32[1024,256]{1,0:T(8,128)S(1)}, f32[1024,256]{1,0:T(8,128)S(1)}, u32[]{:S(2)}, u32[]{:S(2)}) collective-permute-start(f32[1024,256]{1,0:T(8,128)S(1)} %collective-permute-done.refs_0_), channel_id=1, source_target_pairs={{0,1},{1,2},{2,3},{3,0},{4,5},{5,6},{6,7},{7,4},{8,9},{9,10},{10,1... | collective-permute-start | bytes 3145736 | tf_op jit(solution)/shard_map/ppermute | solution.py:26
  41.7 13.9 %collective-permute-start.16 = (f32[512,256]{1,0:T(8,128)S(1)}, f32[512,256]{1,0:T(8,128)S(1)}, u32[]{:S(2)}, u32[]{:S(2)}) collective-permute-start(f32[512,256]{1,0:T(8,128)S(1)} %constant_dynamic-update-slice_fusion.refs_2_.refs_7_), channel_id=1, source_target_pairs={{0,96},{32,0},{1,97},{33,1},{2,98},{34,2},{3,99},{35,3},{4,100},{3... | collective-permute-start | bytes 1572872 | tf_op jit(solution)/shard_map/ppermute | solution.py:46
  44.8 14.1 %collective-permute-start.15 = (f32[512,256]{1,0:T(8,128)S(1)}, f32[512,256]{1,0:T(8,128)S(1)}, u32[]{:S(2)}, u32[]{:S(2)}) collective-permute-start(f32[512,256]{1,0:T(8,128)S(1)} %constant_dynamic-update-slice_fusion.refs_2_.refs_7_), channel_id=1, source_target_pairs={{0,32},{32,64},{64,96},{1,33},{33,65},{65,97},{2,34},{34,66},{66,9... | collective-permute-start | bytes 1572872 | tf_op jit(solution)/shard_map/ppermute | solution.py:46
  48.3 24.1 %collective-permute-start.4 = (f32[1024,256]{1,0:T(8,128)}, f32[1024,256]{1,0:T(8,128)S(1)}, u32[]{:S(2)}, u32[]{:S(2)}) collective-permute-start(f32[1024,256]{1,0:T(8,128)} %collective-permute-done.3.refs_6_), channel_id=1, source_target_pairs={{0,3},{1,0},{2,1},{3,2},{4,7},{5,4},{6,5},{7,6},{8,11},{9,8},{10,9... | collective-permute-start | bytes 3145736 | tf_op jit(solution)/shard_map/ppermute | solution.py:26
  55.5 13.5 %collective-permute-start.7 = (f32[256,256]{1,0:T(8,128)S(1)}, f32[256,256]{1,0:T(8,128)S(1)}, u32[]{:S(2)}, u32[]{:S(2)}) collective-permute-start(f32[256,256]{1,0:T(8,128)S(1)} %collective-permute-done.5.refs_2_), channel_id=1, source_target_pairs={{0,96},{1,97},{2,98},{3,99},{4,100},{5,101},{6,102},{7,103},{8,104... | collective-permute-start | bytes 786440 | tf_op jit(solution)/shard_map/ppermute | solution.py:46
  58.9 10.1 %collective-permute-start.8 = (f32[256,256]{1,0:T(8,128)S(1)}, f32[256,256]{1,0:T(8,128)S(1)}, u32[]{:S(2)}, u32[]{:S(2)}) collective-permute-start(f32[256,256]{1,0:T(8,128)S(1)} %collective-permute-done.6.refs_3_), channel_id=1, source_target_pairs={{32,64},{64,96},{33,65},{65,97},{34,66},{66,98},{35,67},{67,99},{3... | collective-permute-start | bytes 786440 | tf_op jit(solution)/shard_map/ppermute | solution.py:46
  59.6 12.8 %collective-permute-start.18 = (f32[512,256]{1,0:T(8,128)S(1)}, f32[512,256]{1,0:T(8,128)S(1)}, u32[]{:S(2)}, u32[]{:S(2)}) collective-permute-start(f32[512,256]{1,0:T(8,128)S(1)} %collective-permute-done.16.refs_4_.refs_9_), channel_id=1, source_target_pairs={{0,96},{96,64},{1,97},{97,65},{2,98},{98,66},{3,99},{99,67},{4,100... | collective-permute-start | bytes 1572872 | tf_op jit(solution)/shard_map/ppermute | solution.py:46
  80.2 18.9 %collective-permute-start.25 = (f32[8,64,512]{2,1,0:T(8,128)S(1)}, f32[8,64,512]{2,1,0:T(8,128)S(1)}, u32[]{:S(2)}, u32[]{:S(2)}) collective-permute-start(f32[8,64,512]{2,1,0:T(8,128)S(1)} %get-tuple-element.37), channel_id=1, source_target_pairs={{0,12},{1,13},{2,14},{3,15},{4,0},{5,1},{6,2},{7,3},{8,4},{9,5},{1... | collective-permute-start | bytes 3145736 | tf_op jit(solution)/shard_map/ppermute | solution.py:26
  87.4 15.5 %collective-permute-start.19 = (f32[8,64,512]{2,1,0:T(8,128)S(1)}, f32[8,64,512]{2,1,0:T(8,128)S(1)}, u32[]{:S(2)}, u32[]{:S(2)}) collective-permute-start(f32[8,64,512]{2,1,0:T(8,128)S(1)} %get-tuple-element.33), channel_id=1, source_target_pairs={{0,4},{1,5},{2,6},{3,7},{4,8},{5,9},{6,10},{7,11},{8,12},{9,13},{1... | collective-permute-start | bytes 3145736 | tf_op jit(solution)/shard_map/ppermute | solution.py:26
  87.4 26.4 %collective-permute-start.27 = (f32[8,64,512]{2,1,0:T(8,128)S(1)}, f32[8,64,512]{2,1,0:T(8,128)S(1)}, u32[]{:S(2)}, u32[]{:S(2)}) collective-permute-start(f32[8,64,512]{2,1,0:T(8,128)S(1)} %get-tuple-element.38), channel_id=1, source_target_pairs={{0,4},{1,5},{2,6},{3,7},{4,8},{5,9},{6,10},{7,11},{8,12},{9,13},{1... | collective-permute-start | bytes 3145736 | tf_op jit(solution)/shard_map/ppermute | solution.py:26
  99.4 15.2 %collective-permute-start.26 = (f32[8,64,512]{2,1,0:T(8,128)S(1)}, f32[8,64,512]{2,1,0:T(8,128)S(1)}, u32[]{:S(2)}, u32[]{:S(2)}) collective-permute-start(f32[8,64,512]{2,1,0:T(8,128)S(1)} %add.271), channel_id=1, source_target_pairs={{0,12},{1,13},{2,14},{3,15},{4,0},{5,1},{6,2},{7,3},{8,4},{9,5},{1... | collective-permute-start | bytes 3145736 | tf_op jit(solution)/shard_map/ppermute | solution.py:26
  102.8 23.0 %collective-permute-start.21 = (f32[8,64,512]{2,1,0:T(8,128)S(1)}, f32[8,64,512]{2,1,0:T(8,128)S(1)}, u32[]{:S(2)}, u32[]{:S(2)}) collective-permute-start(f32[8,64,512]{2,1,0:T(8,128)S(1)} %get-tuple-element.34), channel_id=1, source_target_pairs={{0,12},{1,13},{2,14},{3,15},{4,0},{5,1},{6,2},{7,3},{8,4},{9,5},{1... | collective-permute-start | bytes 3145736 | tf_op jit(solution)/shard_map/ppermute | solution.py:26
  103.1 33.0 %collective-permute-start.20 = (f32[8,64,512]{2,1,0:T(8,128)S(1)}, f32[8,64,512]{2,1,0:T(8,128)S(1)}, u32[]{:S(2)}, u32[]{:S(2)}) collective-permute-start(f32[8,64,512]{2,1,0:T(8,128)S(1)} %add.262), channel_id=1, source_target_pairs={{0,4},{1,5},{2,6},{3,7},{4,8},{5,9},{6,10},{7,11},{8,12},{9,13},{1... | collective-permute-start | bytes 3145736 | tf_op jit(solution)/shard_map/ppermute | solution.py:26
  114.9 22.0 %collective-permute-start.28 = (f32[2,64,512]{2,1,0:T(8,128)S(1)}, f32[2,64,512]{2,1,0:T(8,128)S(1)}, u32[]{:S(2)}, u32[]{:S(2)}) collective-permute-start(f32[2,64,512]{2,1,0:T(8,128)S(1)} %get-tuple-element.42), channel_id=1, source_target_pairs={{0,16},{1,17},{2,18},{3,19},{4,20},{5,21},{6,22},{7,23},{8,24},{9,... | collective-permute-start | bytes 786440 | tf_op jit(solution)/shard_map/ppermute | solution.py:26
  120.2 17.6 %collective-permute-start.29 = (f32[2,64,512]{2,1,0:T(8,128)S(1)}, f32[2,64,512]{2,1,0:T(8,128)S(1)}, u32[]{:S(2)}, u32[]{:S(2)}) collective-permute-start(f32[2,64,512]{2,1,0:T(8,128)S(1)} %get-tuple-element.41), channel_id=1, source_target_pairs={{0,17},{1,18},{2,19},{3,16},{4,21},{5,22},{6,23},{7,20},{8,25},{9,... | collective-permute-start | bytes 786440 | tf_op jit(solution)/shard_map/ppermute | solution.py:26
  121.9 17.8 %collective-permute-start.30 = (f32[2,64,512]{2,1,0:T(8,128)S(1)}, f32[2,64,512]{2,1,0:T(8,128)S(1)}, u32[]{:S(2)}, u32[]{:S(2)}) collective-permute-start(f32[2,64,512]{2,1,0:T(8,128)S(1)} %get-tuple-element.40), channel_id=1, source_target_pairs={{0,18},{1,19},{2,16},{3,17},{4,22},{5,23},{6,20},{7,21},{8,26},{9,... | collective-permute-start | bytes 786440 | tf_op jit(solution)/shard_map/ppermute | solution.py:26
  125.8 14.0 %collective-permute-start.31 = (f32[2,64,512]{2,1,0:T(8,128)S(1)}, f32[2,64,512]{2,1,0:T(8,128)S(1)}, u32[]{:S(2)}, u32[]{:S(2)}) collective-permute-start(f32[2,64,512]{2,1,0:T(8,128)S(1)} %get-tuple-element.39), channel_id=1, source_target_pairs={{0,19},{1,16},{2,17},{3,18},{4,23},{5,20},{6,21},{7,22},{8,27},{9,... | collective-permute-start | bytes 786440 | tf_op jit(solution)/shard_map/ppermute | solution.py:26
  136.5 9.6 %collective-permute-start.22 = (f32[2,64,512]{2,1,0:T(8,128)S(1)}, f32[2,64,512]{2,1,0:T(8,128)S(1)}, u32[]{:S(2)}, u32[]{:S(2)}) collective-permute-start(f32[2,64,512]{2,1,0:T(8,128)S(1)} %get-tuple-element.45), channel_id=1, source_target_pairs={{0,1},{1,2},{2,3},{3,0},{4,5},{5,6},{6,7},{7,4},{8,9},{9,10},{10,1... | collective-permute-start | bytes 786440 | tf_op jit(solution)/shard_map/ppermute | solution.py:26
  136.9 9.2 %collective-permute-start.23 = (f32[2,64,512]{2,1,0:T(8,128)S(1)}, f32[2,64,512]{2,1,0:T(8,128)S(1)}, u32[]{:S(2)}, u32[]{:S(2)}) collective-permute-start(f32[2,64,512]{2,1,0:T(8,128)S(1)} %get-tuple-element.44), channel_id=1, source_target_pairs={{0,2},{1,3},{2,0},{3,1},{4,6},{5,7},{6,4},{7,5},{8,10},{9,11},{10,... | collective-permute-start | bytes 786440 | tf_op jit(solution)/shard_map/ppermute | solution.py:26
  137.8 8.9 %collective-permute-start.24 = (f32[2,64,512]{2,1,0:T(8,128)S(1)}, f32[2,64,512]{2,1,0:T(8,128)S(1)}, u32[]{:S(2)}, u32[]{:S(2)}) collective-permute-start(f32[2,64,512]{2,1,0:T(8,128)S(1)} %get-tuple-element.43), channel_id=1, source_target_pairs={{0,3},{1,0},{2,1},{3,2},{4,7},{5,4},{6,5},{7,6},{8,11},{9,8},{10,9... | collective-permute-start | bytes 786440 | tf_op jit(solution)/shard_map/ppermute | solution.py:26

commit v3 on v2

--- a/solution.py
+++ b/solution.py
@@ -50,28 +50,28 @@
     return [pl.BlockSpec(memory_space=space)] * count
 
 
-def cut_kernel(q, at_ref, mine_ref, other_ref, *outs):
+def cut_kernel(q, group, at_ref, slab_ref, *refs):
     for step in range(N):
         part = lax.rem(at_ref[1] + step, N)
-        for group, ref in enumerate((mine_ref, other_ref)):
-            for block in range(2):
-                start = pl.multiple_of((2 * block + at_ref[0]) * N * q + part * q, q)
-                row = (2 * group + block) * q
-                outs[step][row : row + q, :] = ref[pl.ds(start, q), :]
-
-
-def cut(at, mine, other):
-    rows, inner = mine.shape
+        for block in range(2):
+            start = pl.multiple_of((2 * block + at_ref[0]) * N * q + part * q, q)
+            row = (2 * group + block) * q
+            refs[step - N][row : row + q, :] = slab_ref[pl.ds(start, q), :]
+
+
+def cut(at, slab, held):
+    rows, inner = slab.shape
     q = rows // 16
     return pl.pallas_call(
-        functools.partial(cut_kernel, q),
-        out_shape=[jax.ShapeDtypeStruct((4 * q, inner), mine.dtype)] * N,
-        in_specs=specs(SMEM, 1) + specs(VMEM, 2),
+        functools.partial(cut_kernel, q, 1 if held else 0),
+        out_shape=[jax.ShapeDtypeStruct((4 * q, inner), slab.dtype)] * N,
+        in_specs=specs(SMEM, 1) + specs(VMEM, 1 + len(held)),
         out_specs=specs(VMEM, N),
+        input_output_aliases={2 + k: k for k in range(len(held))},
         compiler_params=pltpu.CompilerParams(vmem_limit_bytes=GRANT),
         cost_estimate=pl.CostEstimate(flops=10**6, bytes_accessed=3 * rows * inner * 4, transcendentals=0),
         name="cut",
-    )(at, mine, other)
+    )(at, slab, *held)
 
 
 def product_kernel(q, work, carried, last, tab_ref, *refs):
@@ -231,7 +231,7 @@
 
     other = swap(panel)
     up, down = [along(panel, 1)], [along(panel, -1)]
-    first, *sends = cut(at, panel, other)
+    first, *sends = cut(at, other, cut(at, panel, []))
     small = [along(sends[s - 1], s) for s in range(1, N)]
     up.append(along(other, 1))
     down.append(along(other, -1))

time: 151 us -> 152 us (level)
  starting transfers between devices: 79.4 us -> 83.8 us
  waiting for transfers between devices: 42 us -> 38.2 us
    ppermute x22, starting transfers between devices: 53.2 us -> 56.4 us  [move(): return lax.ppermute(value, ('c', 'y', 'z'), pairs)]
    ppermute x22, waiting for transfers between devices: 38.2 us -> 35.8 us  [move(): return lax.ppermute(value, ('c', 'y', 'z'), pairs)]
where the time goes in v3:
time: 152 us; the launch traced here: 150 us
  starting transfers between devices  83.8 us (55%)
  waiting for transfers between devices  38.2 us (25%)
  Pallas kernels  22.8 us (15%)
  local copies, waits for them, and re-layouts  3.17 us (2%)
    ppermute x22, starting transfers between devices, move(): return lax.ppermute(value, ('c', 'y', 'z'), pairs)  56.4 us
    ppermute x22, waiting for transfers between devices, move(): return lax.ppermute(value, ('c', 'y', 'z'), pairs)  35.8 us
    ppermute x9, starting transfers between devices, hop(): return lax.ppermute(value, 'x', pairs)  26 us
    pallas_call x3, Pallas kernels, product(): pl.pallas_call(functools.partial(product_kernel, q, form, total is not No...  19 us
  transfers between devices with their start and end apart: 32, of which 11 were waited for; matrix products, arithmetic and copies ran while one was open for 2% of the time, Pallas kernels for 8%

profile of v3, /device:TPU:1, one launch (start us, length us, event | category | flops | bytes accessed | tf_op | source)
XLA Modules:
  0.0 149.7 jit_solution(13115184139177218333)
XLA Ops:
  0.0 1.4 collective-permute-start.2
  1.4 1.4 collective-permute-start
  2.8 1.4 collective-permute-start.17
  4.2 0.0 collective-permute-done.2.slab_ref.refs_1_
  4.3 2.5 %collective-permute-start.3 = (f32[1024,256]{1,0:T(8,128)S(1)}, f32[1024,256]{1,0:T(8,128)}, u32[]{:S(2)}, u32[]{:S(2)}) collective-permute-start(f32[1024,256]{1,0:T(8,128)S(1)} %collective-permute-done.2.slab_ref.refs_1_), channel_id=1, source_target_pairs={{0,3},{1,0},{2,1},{3,2},{4,7},{5,4},{6,5},{7,6},{8,11},{9,8},{10,9... | collective-permute-start | bytes 3145736 | tf_op jit(solution)/shard_map/ppermute | solution.py:26
  6.7 0.1 pad_add_fusion.at_ref
  6.8 1.2 copy-done
  8.0 0.6 cut.2
  8.6 0.6 cut.3
  9.2 3.8 %collective-permute-start.9 = (f32[256,256]{1,0:T(8,128)S(1)}, f32[256,256]{1,0:T(8,128)}, u32[]{:S(2)}, u32[]{:S(2)}) collective-permute-start(f32[256,256]{1,0:T(8,128)S(1)} %get-tuple-element.31.refs_2_), channel_id=1, source_target_pairs={{0,32},{32,64},{64,96},{1,33},{33,65},{65,97},{2,34},{34,66},{66,9... | collective-permute-start | bytes 786440 | tf_op jit(solution)/shard_map/ppermute | solution.py:46
  13.1 3.9 %collective-permute-done.refs_0_ = f32[1024,256]{1,0:T(8,128)} collective-permute-done((f32[1024,256]{1,0:T(8,128)}, f32[1024,256]{1,0:T(8,128)}, u32[]{:S(2)}, u32[]{:S(2)}) %collective-permute-start) | collective-permute-done | bytes 1048608 | tf_op jit(solution)/shard_map/ppermute | solution.py:26
  17.0 1.5 collective-permute-start.14
  18.5 1.2 collective-permute-start.5
  19.7 0.1 broadcast_select_fusion
  19.8 0.2 select_reduce_fusion
  20.0 0.0 collective-permute-done.9.refs_3_
  20.0 4.4 %collective-permute-start.10 = (f32[256,256]{1,0:T(8,128)S(1)}, f32[256,256]{1,0:T(8,128)S(1)}, u32[]{:S(2)}, u32[]{:S(2)}) collective-permute-start(f32[256,256]{1,0:T(8,128)S(1)} %get-tuple-element.31.refs_2_), channel_id=1, source_target_pairs={{0,96},{1,97},{2,98},{3,99},{4,100},{5,101},{6,102},{7,103},{8,104... | collective-permute-start | bytes 786440 | tf_op jit(solution)/shard_map/ppermute | solution.py:46
  24.4 0.0 collective-permute-done.13
  24.4 0.7 collective-permute-start.12
  25.1 0.4 collective-permute-done.5.refs_2_
  25.5 3.1 %collective-permute-start.6 = (f32[256,256]{1,0:T(8,128)S(1)}, f32[256,256]{1,0:T(8,128)S(1)}, u32[]{:S(2)}, u32[]{:S(2)}) collective-permute-start(f32[256,256]{1,0:T(8,128)S(1)} %collective-permute-done.5.refs_2_), channel_id=1, source_target_pairs={{0,32},{32,64},{64,96},{1,33},{33,65},{65,97},{2,34},{34,66},{66,9... | collective-permute-start | bytes 786440 | tf_op jit(solution)/shard_map/ppermute | solution.py:46
  28.6 2.5 %collective-permute-done.14 = f32[256,256]{1,0:T(8,128)} collective-permute-done((f32[256,256]{1,0:T(8,128)S(1)}, f32[256,256]{1,0:T(8,128)}, u32[]{:S(2)}, u32[]{:S(2)}) %collective-permute-start.14) | collective-permute-done | bytes 262176 | tf_op jit(solution)/shard_map/ppermute | solution.py:26
  31.1 0.7 collective-permute-start.11
  31.8 1.0 constant_dynamic-update-slice_fusion.1
  32.8 1.0 constant_dynamic-update-slice_fusion.refs_2_.refs_7_
  33.7 7.9 %collective-permute-start.1 = (f32[1024,256]{1,0:T(8,128)}, f32[1024,256]{1,0:T(8,128)S(1)}, u32[]{:S(2)}, u32[]{:S(2)}) collective-permute-start(f32[1024,256]{1,0:T(8,128)} %collective-permute-done.refs_0_), channel_id=1, source_target_pairs={{0,1},{1,2},{2,3},{3,0},{4,5},{5,6},{6,7},{7,4},{8,9},{9,10},{10,1... | collective-permute-start | bytes 3145736 | tf_op jit(solution)/shard_map/ppermute | solution.py:26
  41.7 0.0 collective-permute-done.6.refs_3_
  41.7 5.3 %collective-permute-start.15 = (f32[512,256]{1,0:T(8,128)S(1)}, f32[512,256]{1,0:T(8,128)S(1)}, u32[]{:S(2)}, u32[]{:S(2)}) collective-permute-start(f32[512,256]{1,0:T(8,128)S(1)} %constant_dynamic-update-slice_fusion.refs_2_.refs_7_), channel_id=1, source_target_pairs={{0,32},{32,64},{64,96},{1,33},{33,65},{65,97},{2,34},{34,66},{66,9... | collective-permute-start | bytes 1572872 | tf_op jit(solution)/shard_map/ppermute | solution.py:46
  47.0 1.9 %collective-permute-start.16 = (f32[512,256]{1,0:T(8,128)S(1)}, f32[512,256]{1,0:T(8,128)S(1)}, u32[]{:S(2)}, u32[]{:S(2)}) collective-permute-start(f32[512,256]{1,0:T(8,128)S(1)} %constant_dynamic-update-slice_fusion.refs_2_.refs_7_), channel_id=1, source_target_pairs={{0,96},{32,0},{1,97},{33,1},{2,98},{34,2},{3,99},{35,3},{4,100},{3... | collective-permute-start | bytes 1572872 | tf_op jit(solution)/shard_map/ppermute | solution.py:46
  48.9 0.0 collective-permute-done.3.refs_6_
  48.9 4.6 %collective-permute-start.4 = (f32[1024,256]{1,0:T(8,128)}, f32[1024,256]{1,0:T(8,128)S(1)}, u32[]{:S(2)}, u32[]{:S(2)}) collective-permute-start(f32[1024,256]{1,0:T(8,128)} %collective-permute-done.3.refs_6_), channel_id=1, source_target_pairs={{0,3},{1,0},{2,1},{3,2},{4,7},{5,4},{6,5},{7,6},{8,11},{9,8},{10,9... | collective-permute-start | bytes 3145736 | tf_op jit(solution)/shard_map/ppermute | solution.py:26
  53.5 3.6 %shard_map.28 = (f32[8,768,256]{2,1,0:T(8,128)S(1)}, bf16[2048,512]{1,0:T(8,128)(2,1)S(1)}) custom-call(s32[64]{0:T(128)S(1)} %broadcast_add_fusion.2.tab_ref, f32[1024,256]{1,0:T(8,128)S(1)} %copy-done.1, f32[1024,256]{1,0:T(8,128)S(1)} %collective-permute-done.2.slab_ref.refs_1_, f32[256,256]{1,0:T(8,128)S(1)} %get-tuple-element.31.refs_2_, ...), custom_call_target="tpu_custom_call" | custom-call | flops 6442450944 | bytes 12582912 | tf_op jit(solution)/shard_map/pallas_call | solution.py:167
  57.1 0.0 collective-permute-done.15.refs_3_.refs_8_
  57.1 1.8 %collective-permute-start.7 = (f32[256,256]{1,0:T(8,128)S(1)}, f32[256,256]{1,0:T(8,128)S(1)}, u32[]{:S(2)}, u32[]{:S(2)}) collective-permute-start(f32[256,256]{1,0:T(8,128)S(1)} %collective-permute-done.5.refs_2_), channel_id=1, source_target_pairs={{0,96},{1,97},{2,98},{3,99},{4,100},{5,101},{6,102},{7,103},{8,104... | collective-permute-start | bytes 786440 | tf_op jit(solution)/shard_map/ppermute | solution.py:46
  59.0 0.0 collective-permute-done.16.refs_4_.refs_9_
  59.0 0.7 collective-permute-start.8
  59.7 4.2 %collective-permute-start.18 = (f32[512,256]{1,0:T(8,128)S(1)}, f32[512,256]{1,0:T(8,128)S(1)}, u32[]{:S(2)}, u32[]{:S(2)}) collective-permute-start(f32[512,256]{1,0:T(8,128)S(1)} %collective-permute-done.16.refs_4_.refs_9_), channel_id=1, source_target_pairs={{0,96},{96,64},{1,97},{97,65},{2,98},{98,66},{3,99},{99,67},{4,100... | collective-permute-start | bytes 1572872 | tf_op jit(solution)/shard_map/ppermute | solution.py:46
  63.9 7.6 %shard_map.29 = (f32[8,768,256]{2,1,0:T(8,128)S(1)}, bf16[2048,512]{1,0:T(8,128)(2,1)S(1)}, bf16[2048,512]{1,0:T(8,128)(2,1)S(1)}) custom-call(s32[64]{0:T(128)S(1)} %broadcast_add_fusion.2.tab_ref, f32[1024,256]{1,0:T(8,128)} %collective-permute-done.refs_0_, f32[1024,256]{1,0:T(8,128)S(1)} %collective-permute-done.12.refs_1_, ...), custom_call_target="tpu_custom_call", output_to_operand_aliasing={{0}: (11, {})} | custom-call | flops 6442450944 | bytes 12582912 | tf_op jit(solution)/shard_map/pallas_call | solution.py:167
  71.5 0.0 collective-permute-done.7.refs_4_
  71.5 2.4 %collective-permute-done.18.refs_9_.refs_11_ = f32[512,256]{1,0:T(8,128)S(1)} collective-permute-done((f32[512,256]{1,0:T(8,128)S(1)}, f32[512,256]{1,0:T(8,128)S(1)}, u32[]{:S(2)}, u32[]{:S(2)}) %collective-permute-start.18) | collective-permute-done | bytes 524320 | tf_op jit(solution)/shard_map/ppermute | solution.py:46
  73.9 7.8 %shard_map.30 = (f32[8,64,512]{2,1,0:T(8,128)S(1)}, f32[8,64,512]{2,1,0:T(8,128)S(1)}, f32[8,64,512]{2,1,0:T(8,128)S(1)}, f32[8,64,512]{2,1,0:T(8,128)S(1)}, f32...) custom-call(s32[64]{0:T(128)S(1)} %broadcast_add_fusion.2.tab_ref, ...), custom_call_target="tpu_custom_call" | custom-call | flops 6442450944 | bytes 12582912 | tf_op jit(solution)/shard_map/pallas_call | solution.py:167
  81.8 6.1 %collective-permute-start.25 = (f32[8,64,512]{2,1,0:T(8,128)S(1)}, f32[8,64,512]{2,1,0:T(8,128)S(1)}, u32[]{:S(2)}, u32[]{:S(2)}) collective-permute-start(f32[8,64,512]{2,1,0:T(8,128)S(1)} %get-tuple-element.45), channel_id=1, source_target_pairs={{0,12},{1,13},{2,14},{3,15},{4,0},{5,1},{6,2},{7,3},{8,4},{9,5},{1... | collective-permute-start | bytes 3145736 | tf_op jit(solution)/shard_map/ppermute | solution.py:26
  87.9 0.5 collective-permute-start.27
  88.4 11.3 %collective-permute-done.25 = f32[8,64,512]{2,1,0:T(8,128)S(1)} collective-permute-done((f32[8,64,512]{2,1,0:T(8,128)S(1)}, f32[8,64,512]{2,1,0:T(8,128)S(1)}, u32[]{:S(2)}, u32[]{:S(2)}) %collective-permute-start.25) | collective-permute-done | bytes 1048608 | tf_op jit(solution)/shard_map/ppermute | solution.py:26
  99.6 0.2 add.271
  99.8 3.5 %collective-permute-start.26 = (f32[8,64,512]{2,1,0:T(8,128)S(1)}, f32[8,64,512]{2,1,0:T(8,128)S(1)}, u32[]{:S(2)}, u32[]{:S(2)}) collective-permute-start(f32[8,64,512]{2,1,0:T(8,128)S(1)} %add.271), channel_id=1, source_target_pairs={{0,12},{1,13},{2,14},{3,15},{4,0},{5,1},{6,2},{7,3},{8,4},{9,5},{1... | collective-permute-start | bytes 3145736 | tf_op jit(solution)/shard_map/ppermute | solution.py:26
  103.3 0.1 collective-permute-start.21
  103.4 0.2 add.262
  103.6 1.7 %collective-permute-start.20 = (f32[8,64,512]{2,1,0:T(8,128)S(1)}, f32[8,64,512]{2,1,0:T(8,128)S(1)}, u32[]{:S(2)}, u32[]{:S(2)}) collective-permute-start(f32[8,64,512]{2,1,0:T(8,128)S(1)} %add.262), channel_id=1, source_target_pairs={{0,4},{1,5},{2,6},{3,7},{4,8},{5,9},{6,10},{7,11},{8,12},{9,13},{1... | collective-permute-start | bytes 3145736 | tf_op jit(solution)/shard_map/ppermute | solution.py:26
  105.3 9.0 %collective-permute-done.27 = f32[8,64,512]{2,1,0:T(8,128)S(1)} collective-permute-done((f32[8,64,512]{2,1,0:T(8,128)S(1)}, f32[8,64,512]{2,1,0:T(8,128)S(1)}, u32[]{:S(2)}, u32[]{:S(2)}) %collective-permute-start.27) | collective-permute-done | bytes 1048608 | tf_op jit(solution)/shard_map/ppermute | solution.py:26
  114.3 0.8 collective-permute-done.26
  115.1 0.3 slice_add_fusion
  115.4 4.2 %collective-permute-start.28 = (f32[2,64,512]{2,1,0:T(8,128)S(1)}, f32[2,64,512]{2,1,0:T(8,128)S(1)}, u32[]{:S(2)}, u32[]{:S(2)}) collective-permute-start(f32[2,64,512]{2,1,0:T(8,128)S(1)} %get-tuple-element.50), channel_id=1, source_target_pairs={{0,16},{1,17},{2,18},{3,19},{4,20},{5,21},{6,22},{7,23},{8,24},{9,... | collective-permute-start | bytes 786440 | tf_op jit(solution)/shard_map/ppermute | solution.py:26
  119.6 2.6 %collective-permute-start.29 = (f32[2,64,512]{2,1,0:T(8,128)S(1)}, f32[2,64,512]{2,1,0:T(8,128)S(1)}, u32[]{:S(2)}, u32[]{:S(2)}) collective-permute-start(f32[2,64,512]{2,1,0:T(8,128)S(1)} %get-tuple-element.49), channel_id=1, source_target_pairs={{0,17},{1,18},{2,19},{3,16},{4,21},{5,22},{6,23},{7,20},{8,25},{9,... | collective-permute-start | bytes 786440 | tf_op jit(solution)/shard_map/ppermute | solution.py:26
  122.2 2.9 %collective-permute-start.30 = (f32[2,64,512]{2,1,0:T(8,128)S(1)}, f32[2,64,512]{2,1,0:T(8,128)S(1)}, u32[]{:S(2)}, u32[]{:S(2)}) collective-permute-start(f32[2,64,512]{2,1,0:T(8,128)S(1)} %get-tuple-element.48), channel_id=1, source_target_pairs={{0,18},{1,19},{2,16},{3,17},{4,22},{5,23},{6,20},{7,21},{8,26},{9,... | collective-permute-start | bytes 786440 | tf_op jit(solution)/shard_map/ppermute | solution.py:26
  125.1 1.2 collective-permute-done.21
  126.3 10.2 %collective-permute-start.31 = (f32[2,64,512]{2,1,0:T(8,128)S(1)}, f32[2,64,512]{2,1,0:T(8,128)S(1)}, u32[]{:S(2)}, u32[]{:S(2)}) collective-permute-start(f32[2,64,512]{2,1,0:T(8,128)S(1)} %get-tuple-element.47), channel_id=1, source_target_pairs={{0,19},{1,16},{2,17},{3,18},{4,23},{5,20},{6,21},{7,22},{8,27},{9,... | collective-permute-start | bytes 786440 | tf_op jit(solution)/shard_map/ppermute | solution.py:26
  136.5 0.3 slice_add_fusion.8
  136.8 1.1 collective-permute-start.22
  137.9 2.5 %collective-permute-start.24 = (f32[2,64,512]{2,1,0:T(8,128)S(1)}, f32[2,64,512]{2,1,0:T(8,128)S(1)}, u32[]{:S(2)}, u32[]{:S(2)}) collective-permute-start(f32[2,64,512]{2,1,0:T(8,128)S(1)} %get-tuple-element.51), channel_id=1, source_target_pairs={{0,3},{1,0},{2,1},{3,2},{4,7},{5,4},{6,5},{7,6},{8,11},{9,8},{10,9... | collective-permute-start | bytes 786440 | tf_op jit(solution)/shard_map/ppermute | solution.py:26
  140.4 0.3 collective-permute-done.31.refs_7_
  140.7 5.4 %collective-permute-done.22.refs_1_ = f32[2,64,512]{2,1,0:T(8,128)S(1)} collective-permute-done((f32[2,64,512]{2,1,0:T(8,128)S(1)}, f32[2,64,512]{2,1,0:T(8,128)S(1)}, u32[]{:S(2)}, u32[]{:S(2)}) %collective-permute-start.22) | collective-permute-done | bytes 262176 | tf_op jit(solution)/shard_map/ppermute | solution.py:26
  146.1 0.9 collective-permute-done.24.refs_3_
  147.1 2.6 %join.1 = f32[1,2,512,512]{3,2,1,0:T(8,128)} custom-call(s32[3]{0:T(128)S(1)} %pad_add_fusion.at_ref, f32[2,64,512]{2,1,0:T(8,128)S(1)} %get-tuple-element.54.refs_0_, f32[2,64,512]{2,1,0:T(8,128)S(1)} %collective-permute-done.22.refs_1_, f32[2,64,512]{2,1,0:T(8,128)S(1)} %collective-permute-done.23.refs_2_, ...), custom_call_target="tpu_custom_call" | custom-call | flops 1000000 | bytes 4194304 | tf_op jit(solution)/shard_map/join/pallas_call | solution.py:196
  (26 shorter events, 0.1 us)
Async XLA Ops:
  0.0 19.8 %copy-start.2 = (s32[16,16]{1,0:T(8,128)S(1)}, s32[16,16]{1,0:T(8,128)}, u32[]{:S(2)}) copy-start(s32[16,16]{1,0:T(8,128)} %param.3) | copy-start | bytes 3076
  0.0 4.2 %collective-permute-start.2 = (f32[1024,256]{1,0:T(8,128)}, f32[1024,256]{1,0:T(8,128)S(1)}, u32[]{:S(2)}, u32[]{:S(2)}) collective-permute-start(f32[1024,256]{1,0:T(8,128)} %refs_0_.1), channel_id=1, source_target_pairs={{0,16},{16,0},{1,17},{17,1},{2,18},{18,2},{3,19},{19,3},{4,20},{20... | collective-permute-start | bytes 3145736 | tf_op jit(solution)/shard_map/ppermute | solution.py:42
  1.4 15.6 %collective-permute-start = (f32[1024,256]{1,0:T(8,128)}, f32[1024,256]{1,0:T(8,128)}, u32[]{:S(2)}, u32[]{:S(2)}) collective-permute-start(f32[1024,256]{1,0:T(8,128)} %refs_0_.1), channel_id=1, source_target_pairs={{0,1},{1,2},{2,3},{3,0},{4,5},{5,6},{6,7},{7,4},{8,9},{9,10},{10,1... | collective-permute-start | bytes 3145736 | tf_op jit(solution)/shard_map/ppermute | solution.py:26
  2.8 15.7 %collective-permute-start.17 = (f32[1024,256]{1,0:T(8,128)}, f32[1024,256]{1,0:T(8,128)}, u32[]{:S(2)}, u32[]{:S(2)}) collective-permute-start(f32[1024,256]{1,0:T(8,128)} %refs_0_.1), channel_id=1, source_target_pairs={{0,3},{1,0},{2,1},{3,2},{4,7},{5,4},{6,5},{7,6},{8,11},{9,8},{10,9... | collective-permute-start | bytes 3145736 | tf_op jit(solution)/shard_map/ppermute | solution.py:26
  4.3 44.7 %collective-permute-start.3 = (f32[1024,256]{1,0:T(8,128)S(1)}, f32[1024,256]{1,0:T(8,128)}, u32[]{:S(2)}, u32[]{:S(2)}) collective-permute-start(f32[1024,256]{1,0:T(8,128)S(1)} %collective-permute-done.2.slab_ref.refs_1_), channel_id=1, source_target_pairs={{0,3},{1,0},{2,1},{3,2},{4,7},{5,4},{6,5},{7,6},{8,11},{9,8},{10,9... | collective-permute-start | bytes 3145736 | tf_op jit(solution)/shard_map/ppermute | solution.py:26
  6.8 1.2 copy-start
  8.0 45.5 %copy-start.1 = (f32[1024,256]{1,0:T(8,128)S(1)}, f32[1024,256]{1,0:T(8,128)}, u32[]{:S(2)}) copy-start(f32[1024,256]{1,0:T(8,128)} %refs_0_.1) | copy-start | bytes 3145732
  9.2 10.8 %collective-permute-start.9 = (f32[256,256]{1,0:T(8,128)S(1)}, f32[256,256]{1,0:T(8,128)}, u32[]{:S(2)}, u32[]{:S(2)}) collective-permute-start(f32[256,256]{1,0:T(8,128)S(1)} %get-tuple-element.31.refs_2_), channel_id=1, source_target_pairs={{0,32},{32,64},{64,96},{1,33},{33,65},{65,97},{2,34},{34,66},{66,9... | collective-permute-start | bytes 786440 | tf_op jit(solution)/shard_map/ppermute | solution.py:46
  13.1 11.3 %collective-permute-start.13 = (f32[256,256]{1,0:T(8,128)S(1)}, f32[256,256]{1,0:T(8,128)}, u32[]{:S(2)}, u32[]{:S(2)}) collective-permute-start(f32[256,256]{1,0:T(8,128)S(1)} %get-tuple-element.33), channel_id=1, source_target_pairs={{0,1},{1,2},{2,3},{3,0},{4,5},{5,6},{6,7},{7,4},{8,9},{9,10},{10,1... | collective-permute-start | bytes 786440 | tf_op jit(solution)/shard_map/ppermute | solution.py:26
  17.0 14.1 %collective-permute-start.14 = (f32[256,256]{1,0:T(8,128)S(1)}, f32[256,256]{1,0:T(8,128)}, u32[]{:S(2)}, u32[]{:S(2)}) collective-permute-start(f32[256,256]{1,0:T(8,128)S(1)} %get-tuple-element.34), channel_id=1, source_target_pairs={{0,3},{1,0},{2,1},{3,2},{4,7},{5,4},{6,5},{7,6},{8,11},{9,8},{10,9... | collective-permute-start | bytes 786440 | tf_op jit(solution)/shard_map/ppermute | solution.py:26
  18.5 7.0 %collective-permute-start.5 = (f32[256,256]{1,0:T(8,128)S(1)}, f32[256,256]{1,0:T(8,128)S(1)}, u32[]{:S(2)}, u32[]{:S(2)}) collective-permute-start(f32[256,256]{1,0:T(8,128)S(1)} %get-tuple-element.30), channel_id=1, source_target_pairs={{0,2},{1,3},{2,0},{3,1},{4,6},{5,7},{6,4},{7,5},{8,10},{9,11},{10,... | collective-permute-start | bytes 786440 | tf_op jit(solution)/shard_map/ppermute | solution.py:26
  20.0 13.7 %collective-permute-start.10 = (f32[256,256]{1,0:T(8,128)S(1)}, f32[256,256]{1,0:T(8,128)S(1)}, u32[]{:S(2)}, u32[]{:S(2)}) collective-permute-start(f32[256,256]{1,0:T(8,128)S(1)} %get-tuple-element.31.refs_2_), channel_id=1, source_target_pairs={{0,96},{1,97},{2,98},{3,99},{4,100},{5,101},{6,102},{7,103},{8,104... | collective-permute-start | bytes 786440 | tf_op jit(solution)/shard_map/ppermute | solution.py:46
  24.4 35.3 %collective-permute-start.12 = (f32[1024,256]{1,0:T(8,128)S(1)}, f32[1024,256]{1,0:T(8,128)S(1)}, u32[]{:S(2)}, u32[]{:S(2)}) collective-permute-start(f32[1024,256]{1,0:T(8,128)S(1)} %collective-permute-done.2.slab_ref.refs_1_), channel_id=1, source_target_pairs={{0,1},{1,2},{2,3},{3,0},{4,5},{5,6},{6,7},{7,4},{8,9},{9,10},{10,1... | collective-permute-start | bytes 3145736 | tf_op jit(solution)/shard_map/ppermute | solution.py:26
  25.5 16.2 %collective-permute-start.6 = (f32[256,256]{1,0:T(8,128)S(1)}, f32[256,256]{1,0:T(8,128)S(1)}, u32[]{:S(2)}, u32[]{:S(2)}) collective-permute-start(f32[256,256]{1,0:T(8,128)S(1)} %collective-permute-done.5.refs_2_), channel_id=1, source_target_pairs={{0,32},{32,64},{64,96},{1,33},{33,65},{65,97},{2,34},{34,66},{66,9... | collective-permute-start | bytes 786440 | tf_op jit(solution)/shard_map/ppermute | solution.py:46
  31.1 15.9 %collective-permute-start.11 = (f32[256,256]{1,0:T(8,128)}, f32[256,256]{1,0:T(8,128)S(1)}, u32[]{:S(2)}, u32[]{:S(2)}) collective-permute-start(f32[256,256]{1,0:T(8,128)} %collective-permute-done.9.refs_3_), channel_id=1, source_target_pairs={{32,64},{64,96},{33,65},{65,97},{34,66},{66,98},{35,67},{67,99},{3... | collective-permute-start | bytes 786440 | tf_op jit(solution)/shard_map/ppermute | solution.py:46
  33.7 37.8 %collective-permute-start.1 = (f32[1024,256]{1,0:T(8,128)}, f32[1024,256]{1,0:T(8,128)S(1)}, u32[]{:S(2)}, u32[]{:S(2)}) collective-permute-start(f32[1024,256]{1,0:T(8,128)} %collective-permute-done.refs_0_), channel_id=1, source_target_pairs={{0,1},{1,2},{2,3},{3,0},{4,5},{5,6},{6,7},{7,4},{8,9},{9,10},{10,1... | collective-permute-start | bytes 3145736 | tf_op jit(solution)/shard_map/ppermute | solution.py:26
  41.7 15.4 %collective-permute-start.15 = (f32[512,256]{1,0:T(8,128)S(1)}, f32[512,256]{1,0:T(8,128)S(1)}, u32[]{:S(2)}, u32[]{:S(2)}) collective-permute-start(f32[512,256]{1,0:T(8,128)S(1)} %constant_dynamic-update-slice_fusion.refs_2_.refs_7_), channel_id=1, source_target_pairs={{0,32},{32,64},{64,96},{1,33},{33,65},{65,97},{2,34},{34,66},{66,9... | collective-permute-start | bytes 1572872 | tf_op jit(solution)/shard_map/ppermute | solution.py:46
  47.0 12.0 %collective-permute-start.16 = (f32[512,256]{1,0:T(8,128)S(1)}, f32[512,256]{1,0:T(8,128)S(1)}, u32[]{:S(2)}, u32[]{:S(2)}) collective-permute-start(f32[512,256]{1,0:T(8,128)S(1)} %constant_dynamic-update-slice_fusion.refs_2_.refs_7_), channel_id=1, source_target_pairs={{0,96},{32,0},{1,97},{33,1},{2,98},{34,2},{3,99},{35,3},{4,100},{3... | collective-permute-start | bytes 1572872 | tf_op jit(solution)/shard_map/ppermute | solution.py:46
  48.9 25.0 %collective-permute-start.4 = (f32[1024,256]{1,0:T(8,128)}, f32[1024,256]{1,0:T(8,128)S(1)}, u32[]{:S(2)}, u32[]{:S(2)}) collective-permute-start(f32[1024,256]{1,0:T(8,128)} %collective-permute-done.3.refs_6_), channel_id=1, source_target_pairs={{0,3},{1,0},{2,1},{3,2},{4,7},{5,4},{6,5},{7,6},{8,11},{9,8},{10,9... | collective-permute-start | bytes 3145736 | tf_op jit(solution)/shard_map/ppermute | solution.py:26
  57.1 14.4 %collective-permute-start.7 = (f32[256,256]{1,0:T(8,128)S(1)}, f32[256,256]{1,0:T(8,128)S(1)}, u32[]{:S(2)}, u32[]{:S(2)}) collective-permute-start(f32[256,256]{1,0:T(8,128)S(1)} %collective-permute-done.5.refs_2_), channel_id=1, source_target_pairs={{0,96},{1,97},{2,98},{3,99},{4,100},{5,101},{6,102},{7,103},{8,104... | collective-permute-start | bytes 786440 | tf_op jit(solution)/shard_map/ppermute | solution.py:46
  59.0 12.5 %collective-permute-start.8 = (f32[256,256]{1,0:T(8,128)S(1)}, f32[256,256]{1,0:T(8,128)S(1)}, u32[]{:S(2)}, u32[]{:S(2)}) collective-permute-start(f32[256,256]{1,0:T(8,128)S(1)} %collective-permute-done.6.refs_3_), channel_id=1, source_target_pairs={{32,64},{64,96},{33,65},{65,97},{34,66},{66,98},{35,67},{67,99},{3... | collective-permute-start | bytes 786440 | tf_op jit(solution)/shard_map/ppermute | solution.py:46
  59.7 14.2 %collective-permute-start.18 = (f32[512,256]{1,0:T(8,128)S(1)}, f32[512,256]{1,0:T(8,128)S(1)}, u32[]{:S(2)}, u32[]{:S(2)}) collective-permute-start(f32[512,256]{1,0:T(8,128)S(1)} %collective-permute-done.16.refs_4_.refs_9_), channel_id=1, source_target_pairs={{0,96},{96,64},{1,97},{97,65},{2,98},{98,66},{3,99},{99,67},{4,100... | collective-permute-start | bytes 1572872 | tf_op jit(solution)/shard_map/ppermute | solution.py:46
  81.8 17.9 %collective-permute-start.25 = (f32[8,64,512]{2,1,0:T(8,128)S(1)}, f32[8,64,512]{2,1,0:T(8,128)S(1)}, u32[]{:S(2)}, u32[]{:S(2)}) collective-permute-start(f32[8,64,512]{2,1,0:T(8,128)S(1)} %get-tuple-element.45), channel_id=1, source_target_pairs={{0,12},{1,13},{2,14},{3,15},{4,0},{5,1},{6,2},{7,3},{8,4},{9,5},{1... | collective-permute-start | bytes 3145736 | tf_op jit(solution)/shard_map/ppermute | solution.py:26
  87.9 15.5 %collective-permute-start.19 = (f32[8,64,512]{2,1,0:T(8,128)S(1)}, f32[8,64,512]{2,1,0:T(8,128)S(1)}, u32[]{:S(2)}, u32[]{:S(2)}) collective-permute-start(f32[8,64,512]{2,1,0:T(8,128)S(1)} %get-tuple-element.41), channel_id=1, source_target_pairs={{0,4},{1,5},{2,6},{3,7},{4,8},{5,9},{6,10},{7,11},{8,12},{9,13},{1... | collective-permute-start | bytes 3145736 | tf_op jit(solution)/shard_map/ppermute | solution.py:26
  87.9 26.4 %collective-permute-start.27 = (f32[8,64,512]{2,1,0:T(8,128)S(1)}, f32[8,64,512]{2,1,0:T(8,128)S(1)}, u32[]{:S(2)}, u32[]{:S(2)}) collective-permute-start(f32[8,64,512]{2,1,0:T(8,128)S(1)} %get-tuple-element.46), channel_id=1, source_target_pairs={{0,4},{1,5},{2,6},{3,7},{4,8},{5,9},{6,10},{7,11},{8,12},{9,13},{1... | collective-permute-start | bytes 3145736 | tf_op jit(solution)/shard_map/ppermute | solution.py:26
  99.8 15.2 %collective-permute-start.26 = (f32[8,64,512]{2,1,0:T(8,128)S(1)}, f32[8,64,512]{2,1,0:T(8,128)S(1)}, u32[]{:S(2)}, u32[]{:S(2)}) collective-permute-start(f32[8,64,512]{2,1,0:T(8,128)S(1)} %add.271), channel_id=1, source_target_pairs={{0,12},{1,13},{2,14},{3,15},{4,0},{5,1},{6,2},{7,3},{8,4},{9,5},{1... | collective-permute-start | bytes 3145736 | tf_op jit(solution)/shard_map/ppermute | solution.py:26
  103.3 23.0 %collective-permute-start.21 = (f32[8,64,512]{2,1,0:T(8,128)S(1)}, f32[8,64,512]{2,1,0:T(8,128)S(1)}, u32[]{:S(2)}, u32[]{:S(2)}) collective-permute-start(f32[8,64,512]{2,1,0:T(8,128)S(1)} %get-tuple-element.42), channel_id=1, source_target_pairs={{0,12},{1,13},{2,14},{3,15},{4,0},{5,1},{6,2},{7,3},{8,4},{9,5},{1... | collective-permute-start | bytes 3145736 | tf_op jit(solution)/shard_map/ppermute | solution.py:26
  103.6 32.9 %collective-permute-start.20 = (f32[8,64,512]{2,1,0:T(8,128)S(1)}, f32[8,64,512]{2,1,0:T(8,128)S(1)}, u32[]{:S(2)}, u32[]{:S(2)}) collective-permute-start(f32[8,64,512]{2,1,0:T(8,128)S(1)} %add.262), channel_id=1, source_target_pairs={{0,4},{1,5},{2,6},{3,7},{4,8},{5,9},{6,10},{7,11},{8,12},{9,13},{1... | collective-permute-start | bytes 3145736 | tf_op jit(solution)/shard_map/ppermute | solution.py:26
  115.4 22.5 %collective-permute-start.28 = (f32[2,64,512]{2,1,0:T(8,128)S(1)}, f32[2,64,512]{2,1,0:T(8,128)S(1)}, u32[]{:S(2)}, u32[]{:S(2)}) collective-permute-start(f32[2,64,512]{2,1,0:T(8,128)S(1)} %get-tuple-element.50), channel_id=1, source_target_pairs={{0,16},{1,17},{2,18},{3,19},{4,20},{5,21},{6,22},{7,23},{8,24},{9,... | collective-permute-start | bytes 786440 | tf_op jit(solution)/shard_map/ppermute | solution.py:26
  119.6 18.3 %collective-permute-start.29 = (f32[2,64,512]{2,1,0:T(8,128)S(1)}, f32[2,64,512]{2,1,0:T(8,128)S(1)}, u32[]{:S(2)}, u32[]{:S(2)}) collective-permute-start(f32[2,64,512]{2,1,0:T(8,128)S(1)} %get-tuple-element.49), channel_id=1, source_target_pairs={{0,17},{1,18},{2,19},{3,16},{4,21},{5,22},{6,23},{7,20},{8,25},{9,... | collective-permute-start | bytes 786440 | tf_op jit(solution)/shard_map/ppermute | solution.py:26
  122.2 18.2 %collective-permute-start.30 = (f32[2,64,512]{2,1,0:T(8,128)S(1)}, f32[2,64,512]{2,1,0:T(8,128)S(1)}, u32[]{:S(2)}, u32[]{:S(2)}) collective-permute-start(f32[2,64,512]{2,1,0:T(8,128)S(1)} %get-tuple-element.48), channel_id=1, source_target_pairs={{0,18},{1,19},{2,16},{3,17},{4,22},{5,23},{6,20},{7,21},{8,26},{9,... | collective-permute-start | bytes 786440 | tf_op jit(solution)/shard_map/ppermute | solution.py:26
  126.3 14.4 %collective-permute-start.31 = (f32[2,64,512]{2,1,0:T(8,128)S(1)}, f32[2,64,512]{2,1,0:T(8,128)S(1)}, u32[]{:S(2)}, u32[]{:S(2)}) collective-permute-start(f32[2,64,512]{2,1,0:T(8,128)S(1)} %get-tuple-element.47), channel_id=1, source_target_pairs={{0,19},{1,16},{2,17},{3,18},{4,23},{5,20},{6,21},{7,22},{8,27},{9,... | collective-permute-start | bytes 786440 | tf_op jit(solution)/shard_map/ppermute | solution.py:26
  136.8 9.3 %collective-permute-start.22 = (f32[2,64,512]{2,1,0:T(8,128)S(1)}, f32[2,64,512]{2,1,0:T(8,128)S(1)}, u32[]{:S(2)}, u32[]{:S(2)}) collective-permute-start(f32[2,64,512]{2,1,0:T(8,128)S(1)} %get-tuple-element.53), channel_id=1, source_target_pairs={{0,1},{1,2},{2,3},{3,0},{4,5},{5,6},{6,7},{7,4},{8,9},{9,10},{10,1... | collective-permute-start | bytes 786440 | tf_op jit(solution)/shard_map/ppermute | solution.py:26
  137.9 8.2 %collective-permute-start.23 = (f32[2,64,512]{2,1,0:T(8,128)S(1)}, f32[2,64,512]{2,1,0:T(8,128)S(1)}, u32[]{:S(2)}, u32[]{:S(2)}) collective-permute-start(f32[2,64,512]{2,1,0:T(8,128)S(1)} %get-tuple-element.52), channel_id=1, source_target_pairs={{0,2},{1,3},{2,0},{3,1},{4,6},{5,7},{6,4},{7,5},{8,10},{9,11},{10,... | collective-permute-start | bytes 786440 | tf_op jit(solution)/shard_map/ppermute | solution.py:26
  137.9 9.1 %collective-permute-start.24 = (f32[2,64,512]{2,1,0:T(8,128)S(1)}, f32[2,64,512]{2,1,0:T(8,128)S(1)}, u32[]{:S(2)}, u32[]{:S(2)}) collective-permute-start(f32[2,64,512]{2,1,0:T(8,128)S(1)} %get-tuple-element.51), channel_id=1, source_target_pairs={{0,3},{1,0},{2,1},{3,2},{4,7},{5,4},{6,5},{7,6},{8,11},{9,8},{10,9... | collective-permute-start | bytes 786440 | tf_op jit(solution)/shard_map/ppermute | solution.py:26
